TPU v7x, 32 devices: a whole 2x2x4 slice. The times are simulated.
32 devices in a mesh: dp: 4 (over y, x), tensor: 8 (over z, core).
Axes of the slice: x: 2, y: 2, z: 4, core: 2. Of those that a mesh axis runs over, the one named last changes fastest.
Arguments:
- layer_input: bfloat16 [8192, 2048], P(('dp', 'tensor')), may hold values from -6 to 6
- segment_ids: int32 [8192], P('dp'), may hold values from 0 to 31, never falling along the last dimension, each value on 1 to 512 neighbouring positions
- first_gain: float32 [2048], replicated, may hold values from 0.5 to 1.5
- first_shift: float32 [2048], replicated, may hold values from -3 to 3
- qkv_weight: bfloat16 [3, 2048, 2048], P(None, 'dp', 'tensor'), may hold values from -0.125 to 0.125
- query_value_bias: float32 [2, 2048], P(None, 'tensor'), may hold values from -3 to 3
- dense_weight: bfloat16 [2048, 2048], P('tensor', 'dp'), may hold values from -0.5 to 0.5
- dense_bias: float32 [2048], replicated, may hold values from -2 to 2
- second_gain: float32 [2048], replicated, may hold values from 0.5 to 1.5
- second_shift: float32 [2048], replicated, may hold values from -3 to 3
- up_weight: bfloat16 [2048, 8192], P('dp', 'tensor'), may hold values from -0.125 to 0.125
- up_bias: float32 [8192], P('tensor'), may hold values from -3 to 3
- down_weight: bfloat16 [8192, 2048], P('tensor', 'dp'), may hold values from -0.0625 to 0.0625
- down_bias: float32 [2048], replicated, may hold values from -2 to 2
- out_grad: bfloat16 [8192, 2048], P(('dp', 'tensor')), may hold values from -6 to 6
Outputs:
- layer_out: bfloat16 [8192, 2048], P(('dp', 'tensor'))
- input_grad: float32 [8192, 2048], P(('dp', 'tensor'))
- first_gain_grad: float32 [2048], replicated
- first_shift_grad: float32 [2048], replicated
- qkv_weight_grad: float32 [3, 2048, 2048], P(None, 'dp', 'tensor')
- query_value_bias_grad: float32 [2, 2048], P(None, 'tensor')
- dense_weight_grad: float32 [2048, 2048], P('tensor', 'dp')
- dense_bias_grad: float32 [2048], replicated
- second_gain_grad: float32 [2048], replicated
- second_shift_grad: float32 [2048], replicated
- up_weight_grad: float32 [2048, 8192], P('dp', 'tensor')
- up_bias_grad: float32 [8192], P('tensor')
- down_weight_grad: float32 [8192, 2048], P('tensor', 'dp')
- down_bias_grad: float32 [2048], replicated
Inputs may be any that keep to these rules, and one draw needn't show every extreme that they name: `segment_ids`: segment numbers never fall along the whole array; a run of equal numbers is one document of at most 512 tokens, and some document has exactly that many.
All inputs are finite; a program needn't handle non-finite values.
Results may differ from a plain program's by a relative error of at most 0.014.
Values may be sent and summed in bfloat16 or wider, within the bound.
A program may use at most 256 MiB of HBM per device.

v0:
```python
import functools

import jax
import jax.numpy as jnp
from jax import lax
from jax.experimental import pallas as pl
from jax.experimental.pallas import tpu as pltpu
from jax.sharding import PartitionSpec as P


HEADS = 32
EPSILON = 1e-05
MESH = pl.DeviceIdType.MESH
HEAD_DIM = 64
PAIR = 2 * HEAD_DIM
Q_BLOCK = 256
MASKED = -1e32
NT = (((1,), (1,)), ((), ()))
NN = (((1,), (0,)), ((), ()))


def key_window(seq_len, block):
    width = min(seq_len, Q_BLOCK + seq_len // 4)
    start = jnp.maximum(block * Q_BLOCK + Q_BLOCK - width, 0)
    return width, pl.multiple_of(start, 128)


def masked_distance(seg_row, seg_col, first_query, first_key, width):
    shape = (width, Q_BLOCK)
    key_pos = lax.broadcasted_iota(jnp.int32, shape, 0) + first_key
    query_pos = lax.broadcasted_iota(jnp.int32, shape, 1) + first_query
    delta = key_pos - query_pos
    allowed = (seg_col == seg_row) & (delta <= 0)
    return jnp.where(allowed, delta.astype(jnp.float32), MASKED)


def half_lanes(rows, half):
    lane = lax.broadcasted_iota(jnp.int32, rows.shape, 1)
    return jnp.where((lane < HEAD_DIM) == (half == 0), rows, jnp.zeros_like(rows))


def forward_kernel(slope_ref, proj_ref, seg_row_ref, seg_col_ref, out_ref, lse_ref, value_t, bias_ref):
    seq_len = proj_ref.shape[0]
    width_all = out_ref.shape[1]
    block = pl.program_id(0)

    @pl.when(block == 0)
    def _():
        value_t[...] = proj_ref[:, 2 * width_all :].T

    first = pl.multiple_of(block * Q_BLOCK, Q_BLOCK)
    width, start = key_window(seq_len, block)
    queries = pl.ds(first, Q_BLOCK)
    keys = pl.ds(start, width)
    bias_ref[...] = masked_distance(
        seg_row_ref[:, queries], seg_col_ref[keys, :], first, start, width
    )
    for pair in range(width_all // PAIR):
        cols = pair * PAIR
        query_pair = proj_ref[queries, cols : cols + PAIR] * 0.125
        key_pair = proj_ref[keys, width_all + cols : width_all + cols + PAIR]
        value_pair = value_t[cols : cols + PAIR, keys]
        mixed = []
        for half in range(2):
            head = 2 * pair + half
            scores = lax.dot_general(
                key_pair, half_lanes(query_pair, half), NT, preferred_element_type=jnp.float32
            )
            scores = scores + slope_ref[head] * bias_ref[...]
            highest = jnp.max(scores, axis=0, keepdims=True)
            exponent = jnp.exp(scores - highest)
            total = jnp.sum(exponent, axis=0, keepdims=True)
            part = lax.dot_general(
                value_pair[half * HEAD_DIM : (half + 1) * HEAD_DIM],
                exponent.astype(jnp.bfloat16),
                NN,
                preferred_element_type=jnp.float32,
            )
            mixed.append(part / total)
            lse_ref[head : head + 1, :] = highest + jnp.log(total)
        out_ref[:, cols : cols + PAIR] = jnp.concatenate(mixed, axis=0).T.astype(jnp.bfloat16)


def attention_forward(projected, segments, slopes):
    seq_len, all_cols = projected.shape
    cols = all_cols // 3
    heads = cols // HEAD_DIM
    width = min(seq_len, Q_BLOCK + seq_len // 4)
    return pl.pallas_call(
        forward_kernel,
        grid=(seq_len // Q_BLOCK,),
        in_specs=[
            pl.BlockSpec(memory_space=pltpu.SMEM),
            pl.BlockSpec((seq_len, all_cols), lambda i: (0, 0)),
            pl.BlockSpec((1, seq_len), lambda i: (0, 0)),
            pl.BlockSpec((seq_len, 1), lambda i: (0, 0)),
        ],
        out_specs=[
            pl.BlockSpec((Q_BLOCK, cols), lambda i: (i, 0)),
            pl.BlockSpec((heads, Q_BLOCK), lambda i: (0, i)),
        ],
        out_shape=[
            jax.ShapeDtypeStruct((seq_len, cols), jnp.bfloat16),
            jax.ShapeDtypeStruct((heads, seq_len), jnp.float32),
        ],
        scratch_shapes=[
            pltpu.VMEM((cols, seq_len), jnp.bfloat16),
            pltpu.VMEM((width, Q_BLOCK), jnp.float32),
        ],
        compiler_params=pltpu.CompilerParams(vmem_limit_bytes=40 * 2**20),
        cost_estimate=pl.CostEstimate(flops=4 * seq_len * width * cols, bytes_accessed=6 * seq_len * cols, transcendentals=0),
        name="attention_forward",
    )(slopes, projected, segments[None, :], segments[:, None])


def backward_kernel(slope_ref, proj_ref, grad_ref, lse_ref, seg_row_ref, seg_col_ref, out_ref,
                    key_t, bias_ref, key_sum, value_sum):
    seq_len = proj_ref.shape[0]
    width_all = grad_ref.shape[1]
    block = pl.program_id(0)

    @pl.when(block == 0)
    def _():
        key_t[...] = proj_ref[:, width_all : 2 * width_all].T
        key_sum[...] = jnp.zeros_like(key_sum)
        value_sum[...] = jnp.zeros_like(value_sum)

    first = pl.multiple_of(block * Q_BLOCK, Q_BLOCK)
    width, start = key_window(seq_len, block)
    queries = pl.ds(first, Q_BLOCK)
    keys = pl.ds(start, width)
    bias_ref[...] = masked_distance(
        seg_row_ref[:, queries], seg_col_ref[keys, :], first, start, width
    )
    for pair in range(width_all // PAIR):
        cols = pair * PAIR
        query_pair = proj_ref[queries, cols : cols + PAIR] * 0.125
        key_pair = proj_ref[keys, width_all + cols : width_all + cols + PAIR]
        value_pair = proj_ref[keys, 2 * width_all + cols : 2 * width_all + cols + PAIR]
        grad_pair = grad_ref[queries, cols : cols + PAIR]
        query_grads = []
        key_part = value_part = None
        for half in range(2):
            head = 2 * pair + half
            query_half = half_lanes(query_pair, half)
            grad_half = half_lanes(grad_pair, half)
            scores = lax.dot_general(key_pair, query_half, NT, preferred_element_type=jnp.float32)
            probs = jnp.exp(scores + slope_ref[head] * bias_ref[...] - lse_ref[head : head + 1, queries])
            prob_grad = lax.dot_general(value_pair, grad_half, NT, preferred_element_type=jnp.float32)
            inner = jnp.sum(probs * prob_grad, axis=0, keepdims=True)
            score_grad = (probs * (prob_grad - inner)).astype(jnp.bfloat16)
            value_half = jnp.dot(probs.astype(jnp.bfloat16), grad_half, preferred_element_type=jnp.float32)
            key_half = jnp.dot(score_grad, query_half, preferred_element_type=jnp.float32)
            query_grads.append(
                jnp.dot(
                    key_t[cols + half * HEAD_DIM : cols + (half + 1) * HEAD_DIM, keys],
                    score_grad,
                    preferred_element_type=jnp.float32,
                )
                * 0.125
            )
            value_part = value_half if half == 0 else value_part + value_half
            key_part = key_half if half == 0 else key_part + key_half
        key_sum[keys, cols : cols + PAIR] += key_part
        value_sum[keys, cols : cols + PAIR] += value_part
        out_ref[queries, cols : cols + PAIR] = (
            jnp.concatenate(query_grads, axis=0).T.astype(jnp.bfloat16)
        )

    @pl.when(block == pl.num_programs(0) - 1)
    def _():
        out_ref[:, width_all : 2 * width_all] = key_sum[...].astype(jnp.bfloat16)
        out_ref[:, 2 * width_all :] = value_sum[...].astype(jnp.bfloat16)


def attention_backward(projected, head_grad, segments, slopes, log_sums):
    seq_len, all_cols = projected.shape
    cols = all_cols // 3
    heads = cols // HEAD_DIM
    width = min(seq_len, Q_BLOCK + seq_len // 4)
    return pl.pallas_call(
        backward_kernel,
        grid=(seq_len // Q_BLOCK,),
        in_specs=[
            pl.BlockSpec(memory_space=pltpu.SMEM),
            pl.BlockSpec((seq_len, all_cols), lambda i: (0, 0)),
            pl.BlockSpec((seq_len, cols), lambda i: (0, 0)),
            pl.BlockSpec((heads, seq_len), lambda i: (0, 0)),
            pl.BlockSpec((1, seq_len), lambda i: (0, 0)),
            pl.BlockSpec((seq_len, 1), lambda i: (0, 0)),
        ],
        out_specs=pl.BlockSpec((seq_len, all_cols), lambda i: (0, 0)),
        out_shape=jax.ShapeDtypeStruct((seq_len, all_cols), jnp.bfloat16),
        scratch_shapes=[
            pltpu.VMEM((cols, seq_len), jnp.bfloat16),
            pltpu.VMEM((width, Q_BLOCK), jnp.float32),
            pltpu.VMEM((seq_len, cols), jnp.float32),
            pltpu.VMEM((seq_len, cols), jnp.float32),
        ],
        compiler_params=pltpu.CompilerParams(vmem_limit_bytes=48 * 2**20),
        cost_estimate=pl.CostEstimate(flops=10 * seq_len * width * cols, bytes_accessed=14 * seq_len * cols, transcendentals=0),
        name="attention_backward",
    )(slopes, projected, head_grad, log_sums, segments[None, :], segments[:, None])


ROW_TILE = 16
SUBS = 4
LAG = 0


def remote(src, dst, send_sem, recv_sem, peer):
    return pltpu.make_async_remote_copy(
        src_ref=src,
        dst_ref=dst,
        send_sem=send_sem,
        recv_sem=recv_sem,
        device_id={"tensor": peer},
        device_id_type=MESH,
    )


class Line:
    def __init__(self, chips, rows):
        self.chips = chips
        self.sub_rows = rows // SUBS
        self.me = lax.axis_index("tensor")
        self.place = self.me // 2
        self.core = self.me % 2
        self.above = self.me + 2
        self.below = self.me - 2
        self.partner = self.me + 1 - 2 * self.core
        self.has_above = self.place < chips - 1
        self.has_below = self.place > 0

    def rows(self, sub):
        return pl.ds(pl.multiple_of(sub * self.sub_rows, self.sub_rows), self.sub_rows)

    def tile(self, sub, tile):
        return pl.ds(pl.multiple_of(sub * self.sub_rows + tile * ROW_TILE, ROW_TILE), ROW_TILE)

    def enter(self):
        barrier = pltpu.get_barrier_semaphore()

        def greet(peer):
            pl.semaphore_signal(barrier, inc=1, device_id={"tensor": peer}, device_id_type=MESH)

        pl.when(self.has_above)(lambda: greet(self.above))
        pl.when(self.has_below)(lambda: greet(self.below))
        greet(self.partner)
        pl.semaphore_wait(
            barrier, 1 + self.has_above.astype(jnp.int32) + self.has_below.astype(jnp.int32)
        )


class Gather:
    def __init__(self, line, source, target, sems):
        self.line, self.source, self.target = line, source, target
        self.own_sem, self.line_send, self.line_recv, self.pair_send, self.pair_recv = sems

    @staticmethod
    def scratch(chips):
        dma = pltpu.SemaphoreType.DMA
        return [
            dma((SUBS,)),
            dma((2, chips, SUBS)),
            dma((2, chips, SUBS)),
            dma((chips, SUBS)),
            dma((chips, SUBS)),
        ]

    def hop(self, way, step, sub, src, block):
        peer = self.line.above if way == 0 else self.line.below
        return remote(
            src,
            self.target.at[block, self.line.rows(sub)],
            self.line_send.at[way, step, sub],
            self.line_recv.at[way, step, sub],
            peer,
        )

    def across(self, chip, sub, src, block):
        return remote(
            src,
            self.target.at[block, self.line.rows(sub)],
            self.pair_send.at[chip, sub],
            self.pair_recv.at[chip, sub],
            self.line.partner,
        )

    def own(self, sub):
        return pltpu.make_async_copy(
            self.source.at[self.line.rows(sub)],
            self.target.at[self.line.me, self.line.rows(sub)],
            self.own_sem.at[sub],
        )

    def start(self, sub):
        line = self.line
        src = self.source.at[line.rows(sub)]
        pl.when(line.has_above)(lambda: self.hop(0, 0, sub, src, line.me).start())
        pl.when(line.has_below)(lambda: self.hop(1, 0, sub, src, line.me).start())
        self.across(line.place, sub, src, line.me).start()
        self.own(sub).start()

    def step(self, sub, step, live):
        line = self.line
        for way, sign in ((0, -1), (1, 1)):
            block = line.me + 2 * sign * (step + 1)
            onward = line.has_above if way == 0 else line.has_below
            inside = block >= 0 if way == 0 else block < 2 * line.chips

            @pl.when(live & inside)
            def _():
                src = self.target.at[block, line.rows(sub)]
                self.hop(way, step, sub, src, block).wait_recv()

                @pl.when(onward)
                def _():
                    self.hop(way, step + 1, sub, src, block).start()

                self.across(block // 2, sub, src, block).start()

    def finish(self):
        line = self.line

        @pl.loop(0, SUBS)
        def _(sub):
            src = self.source.at[line.rows(sub)]
            for chip in range(line.chips):
                copy = self.across(chip, sub, src, 2 * chip + 1 - line.core)
                copy.wait_recv()
                copy.wait_send()
            for step in range(line.chips - 1):
                sent_up = line.has_above & (line.place >= step)
                sent_down = line.has_below & (line.place + step < line.chips)
                pl.when(sent_up)(lambda: self.hop(0, step, sub, src, line.me).wait_send())
                pl.when(sent_down)(lambda: self.hop(1, step, sub, src, line.me).wait_send())
            self.own(sub).wait()


class Reduce:
    def __init__(self, line, partial, bufs, sems):
        self.line, self.partial = line, partial
        self.held, self.paired, self.from_below, self.from_above = bufs
        self.held_sem, self.pair_send, self.pair_recv, self.line_send, self.line_recv = sems

    @staticmethod
    def scratch(chips, rows, width):
        dma = pltpu.SemaphoreType.DMA
        return [pltpu.VMEM((chips, rows, width), jnp.bfloat16)] * 4 + [
            dma((chips, SUBS)),
            dma((chips, SUBS)),
            dma((chips, SUBS)),
            dma((2, chips, SUBS)),
            dma((2, chips, SUBS)),
        ]

    def load(self, chip, sub):
        rows = self.line.rows(sub)
        return pltpu.make_async_copy(
            self.partial.at[2 * chip + self.line.core, rows],
            self.held.at[chip, rows],
            self.held_sem.at[chip, sub],
        )

    def across(self, chip, sub):
        rows = self.line.rows(sub)
        return remote(
            self.partial.at[2 * chip + 1 - self.line.core, rows],
            self.paired.at[chip, rows],
            self.pair_send.at[chip, sub],
            self.pair_recv.at[chip, sub],
            self.line.partner,
        )

    def hop(self, way, chip, sub):
        rows = self.line.rows(sub)
        return remote(
            self.held.at[chip, rows],
            (self.from_below if way == 0 else self.from_above).at[chip, rows],
            self.line_send.at[way, chip, sub],
            self.line_recv.at[way, chip, sub],
            self.line.above if way == 0 else self.line.below,
        )

    def start(self):
        line = self.line
        order = []
        for step in range(line.chips):
            chip = line.chips - 1 - step // 2 if step % 2 == 0 else step // 2
            order.append(chip)

        @pl.loop(0, SUBS)
        def _(sub):
            for chip in order:
                self.across(chip, sub).start()
                self.load(chip, sub).start()

        zeros = jnp.zeros((ROW_TILE, self.held.shape[2]), jnp.bfloat16)

        def clear(buf, chip):
            @pl.loop(0, self.held.shape[1] // ROW_TILE)
            def _(tile):
                buf[chip, pl.ds(pl.multiple_of(tile * ROW_TILE, ROW_TILE), ROW_TILE), :] = zeros

        pl.when(jnp.logical_not(line.has_below))(lambda: clear(self.from_below, 0))
        pl.when(jnp.logical_not(line.has_above))(lambda: clear(self.from_above, line.chips - 1))

    def step(self, way, sub, step, live):
        line = self.line
        chip = line.chips - 1 - step if way == 0 else step
        arrived = self.from_below if way == 0 else self.from_above
        inner = line.has_below if way == 0 else line.has_above

        @pl.when(live & (chip > line.place if way == 0 else chip < line.place))
        def _():
            self.load(chip, sub).wait()
            self.across(chip, sub).wait_recv()

            def add(with_arrived):
                @pl.loop(0, line.sub_rows // ROW_TILE)
                def _(tile):
                    at = line.tile(sub, tile)
                    total = self.held[chip, at, :].astype(jnp.float32)
                    total = total + self.paired[chip, at, :].astype(jnp.float32)
                    if with_arrived:
                        total = total + arrived[chip, at, :].astype(jnp.float32)
                    self.held[chip, at, :] = total.astype(jnp.bfloat16)

            @pl.when(inner)
            def _():
                self.hop(way, chip, sub).wait_recv()
                add(True)

            pl.when(jnp.logical_not(inner))(lambda: add(False))
            self.hop(way, chip, sub).start()

    def arrive(self, sub):
        line = self.line
        place = line.place
        self.load(place, sub).wait()
        self.across(place, sub).wait_recv()
        pl.when(line.has_below)(lambda: self.hop(0, place, sub).wait_recv())
        pl.when(line.has_above)(lambda: self.hop(1, place, sub).wait_recv())

    def total(self, at):
        place = self.line.place
        total = self.held[place, at, :].astype(jnp.float32)
        total = total + self.paired[place, at, :].astype(jnp.float32)
        total = total + self.from_below[place, at, :].astype(jnp.float32)
        return total + self.from_above[place, at, :].astype(jnp.float32)

    def finish(self):
        line = self.line

        @pl.loop(0, SUBS)
        def _(sub):
            for chip in range(line.chips):
                self.across(chip, sub).wait_send()
                pl.when(chip > line.place)(lambda: self.hop(0, chip, sub).wait_send())
                pl.when(chip < line.place)(lambda: self.hop(1, chip, sub).wait_send())


def for_tiles(line, sub, body):
    @pl.loop(0, line.sub_rows // ROW_TILE)
    def _(tile):
        body(line.tile(sub, tile))


def run_gather(line, gather, rows_done):
    line.enter()
    steps = line.chips - 1

    @pl.loop(0, SUBS)
    def _(sub):
        for_tiles(line, sub, rows_done)
        gather.start(sub)

    @pl.loop(0, steps * SUBS)
    def _(at):
        gather.step(at % SUBS, at // SUBS, True)

    gather.finish()


def run_line(line, reduce, gather, rows_done):
    steps = line.chips - 1
    line.enter()
    reduce.start()
    slots = steps * SUBS + LAG + (steps if gather is not None else 0) + 1

    @pl.loop(0, slots)
    def _(slot):
        for way in range(2):
            at = slot - (line.place if way == 0 else steps - line.place)
            sub = jnp.maximum(at, 0) // steps
            reduce.step(way, jnp.minimum(sub, SUBS - 1), jnp.maximum(at, 0) % steps, (at >= 0) & (sub < SUBS))
        at = slot - steps - LAG
        sub = jnp.maximum(at, 0) // steps

        @pl.when((at >= 0) & (at % steps == 0) & (sub < SUBS))
        def _():
            reduce.arrive(sub)
            for_tiles(line, sub, rows_done)
            if gather is not None:
                gather.start(sub)

        if gather is not None:
            at = slot - steps - LAG - 1
            sub = jnp.maximum(at, 0) // steps
            gather.step(
                jnp.minimum(sub, SUBS - 1), jnp.maximum(at, 0) % steps, (at >= 0) & (sub < SUBS)
            )

    reduce.finish()
    if gather is not None:
        gather.finish()


def unit_of(rows):
    centre = jnp.mean(rows, axis=1, keepdims=True)
    centred = rows - centre
    inv_std = lax.rsqrt(jnp.mean(centred * centred, axis=1, keepdims=True) + EPSILON)
    return centred * inv_std, inv_std


def norm_back(grad, unit, inv_std, gain):
    scaled = grad * gain
    return inv_std * (
        scaled
        - jnp.mean(scaled, axis=1, keepdims=True)
        - unit * jnp.mean(scaled * unit, axis=1, keepdims=True)
    )


def fold(rows):
    return jnp.sum(rows.reshape(-1, 8, rows.shape[1]), axis=0)


def norm_gather_kernel(chips, input_ref, gain_ref, shift_ref, whole_ref, normed_ref, *sems):
    line = Line(chips, input_ref.shape[0])
    gather = Gather(line, normed_ref, whole_ref, sems)

    def rows_done(at):
        unit, _ = unit_of(input_ref[at, :].astype(jnp.float32))
        normed_ref[at, :] = (unit * gain_ref[...] + shift_ref[...]).astype(jnp.bfloat16)

    run_gather(line, gather, rows_done)


def branch_norm_gather_kernel(
    chips, partial_ref, input_ref, bias_ref, gain_ref, shift_ref, whole_ref, residual_ref, normed_ref, *rest
):
    line = Line(chips, input_ref.shape[0])
    reduce = Reduce(line, partial_ref, rest[:4], rest[4:9])
    gather = Gather(line, normed_ref, whole_ref, rest[9:])

    def rows_done(at):
        residual = input_ref[at, :].astype(jnp.float32) + (reduce.total(at) + bias_ref[...])
        residual_ref[at, :] = residual
        unit, _ = unit_of(residual)
        normed_ref[at, :] = (unit * gain_ref[...] + shift_ref[...]).astype(jnp.bfloat16)

    run_line(line, reduce, gather, rows_done)


def grad_gather_kernel(
    chips, partial_ref, residual_ref, grad_ref, gain_ref, whole_ref, residual_grad_ref, sums_ref, branch_ref, *rest
):
    line = Line(chips, grad_ref.shape[0])
    reduce = Reduce(line, partial_ref, rest[:4], rest[4:9])
    gather = Gather(line, branch_ref, whole_ref, rest[9:])
    sums_ref[...] = jnp.zeros_like(sums_ref)

    def rows_done(at):
        unit, inv_std = unit_of(residual_ref[at, :])
        grad = reduce.total(at)
        out_grad = grad_ref[at, :].astype(jnp.float32)
        residual_grad = out_grad + norm_back(grad, unit, inv_std, gain_ref[...])
        residual_grad_ref[at, :] = residual_grad
        branch = residual_grad.astype(jnp.bfloat16)
        branch_ref[at, :] = branch
        sums_ref[0] += fold(grad * unit)
        sums_ref[1] += fold(grad)
        sums_ref[2] += fold(branch.astype(jnp.float32))
        sums_ref[3] += fold(out_grad)

    run_line(line, reduce, gather, rows_done)


def grad_kernel(chips, partial_ref, input_ref, residual_grad_ref, gain_ref, out_ref, sums_ref, *rest):
    line = Line(chips, input_ref.shape[0])
    reduce = Reduce(line, partial_ref, rest[:4], rest[4:9])
    sums_ref[...] = jnp.zeros_like(sums_ref)

    def rows_done(at):
        unit, inv_std = unit_of(input_ref[at, :].astype(jnp.float32))
        grad = reduce.total(at)
        out_ref[at, :] = residual_grad_ref[at, :] + norm_back(grad, unit, inv_std, gain_ref[...])
        sums_ref[0] += fold(grad * unit)
        sums_ref[1] += fold(grad)

    run_line(line, reduce, None, rows_done)


def line_call(kernel, collective_id, operands, outs, gathers, reduces, rows, width):
    chips = lax.axis_size("tensor") // 2
    whole = jax.ShapeDtypeStruct((2 * chips, rows, width), jnp.bfloat16)
    in_vmem = pl.BlockSpec(memory_space=pltpu.VMEM)
    in_place = pl.BlockSpec(memory_space=pl.ANY)
    scratch = []
    if gathers:
        scratch.append(pltpu.VMEM((rows, width), jnp.bfloat16))
    if reduces:
        scratch += Reduce.scratch(chips, rows, width)
    if gathers:
        scratch += Gather.scratch(chips)
    return pl.pallas_call(
        functools.partial(kernel, chips),
        in_specs=([in_place] if reduces else []) + [in_vmem] * (len(operands) - int(reduces)),
        out_specs=([in_place] if gathers else []) + [in_vmem] * len(outs),
        out_shape=([whole] if gathers else []) + list(outs),
        scratch_shapes=scratch,
        compiler_params=pltpu.CompilerParams(
            collective_id=collective_id, has_side_effects=True, vmem_limit_bytes=48 * 2**20
        ),
        cost_estimate=pl.CostEstimate(
            flops=8 * rows * width * 100, bytes_accessed=100 * rows * width, transcendentals=0
        ),
    )(*operands)


def total_kernel(ranks, groups, late_ref, early_ref, own_ref, all_ref, dp_ref, mine, first, stage, second, sems):
    send1, recv1, send2, recv2, send3, recv3 = sems
    me = lax.axis_index("tensor")
    group = lax.axis_index("dp")
    part = mine.shape[1] // ranks
    barrier = pltpu.get_barrier_semaphore()
    for step in range(1, ranks):
        pl.semaphore_signal(
            barrier, inc=1, device_id={"tensor": lax.rem(me + step, ranks)}, device_id_type=MESH
        )
    for step in range(1, groups):
        pl.semaphore_signal(
            barrier, inc=1, device_id={"dp": lax.rem(group + step, groups)}, device_id_type=MESH
        )
    mine[...] = jnp.zeros_like(mine)
    for row in range(late_ref.shape[0]):
        mine[row : row + 1, :] = jnp.sum(late_ref[row], axis=0, keepdims=True)
    for row in range(early_ref.shape[0]):
        at = late_ref.shape[0] + row
        mine[at : at + 1, :] = jnp.sum(early_ref[row], axis=0, keepdims=True)
    pl.semaphore_wait(barrier, ranks + groups - 2)

    def columns(rank):
        return pl.ds(pl.multiple_of(rank * part, part), part)

    def scatter(peer, slot, sem):
        return pltpu.make_async_remote_copy(
            src_ref=mine.at[:, columns(peer)],
            dst_ref=first.at[slot],
            send_sem=send1.at[sem],
            recv_sem=recv1.at[slot],
            device_id={"tensor": peer},
            device_id_type=MESH,
        )

    def exchange(peer, slot, sem):
        return pltpu.make_async_remote_copy(
            src_ref=stage,
            dst_ref=second.at[slot],
            send_sem=send2.at[sem],
            recv_sem=recv2.at[slot],
            device_id={"dp": peer},
            device_id_type=MESH,
        )

    def spread(peer, rank, sem):
        return pltpu.make_async_remote_copy(
            src_ref=all_ref.at[:, columns(me)],
            dst_ref=all_ref.at[:, columns(rank)],
            send_sem=send3.at[sem],
            recv_sem=recv3.at[rank],
            device_id={"tensor": peer},
            device_id_type=MESH,
        )

    for step in range(1, ranks):
        scatter(lax.rem(me + step, ranks), me, step).start()
    first[me] = mine[:, columns(me)]
    for step in range(1, ranks):
        other = lax.rem(me + step, ranks)
        scatter(other, other, step).wait_recv()
    rows = mine.shape[0]
    total = first[0]
    for rank in range(1, ranks):
        total = total + first[rank]
    stage[:rows, :] = total
    stage[rows:, :] = own_ref[...]
    for step in range(1, groups):
        exchange(lax.rem(group + step, groups), group, step).start()
    second[group] = stage[...]
    for step in range(1, groups):
        other = lax.rem(group + step, groups)
        exchange(other, other, step).wait_recv()
    total = second[0]
    for index in range(1, groups):
        total = total + second[index]
    all_ref[:, columns(me)] = total[:rows]
    dp_ref[...] = total[rows:]
    for step in range(1, ranks):
        spread(lax.rem(me + step, ranks), me, step).start()
    for step in range(1, ranks):
        other = lax.rem(me + step, ranks)
        spread(other, other, step).wait_recv()
    for step in range(1, ranks):
        other = lax.rem(me + step, ranks)
        scatter(other, me, step).wait_send()
        spread(other, me, step).wait_send()
    for step in range(1, groups):
        exchange(lax.rem(group + step, groups), group, step).wait_send()


def total_call(late, early, own):
    ranks = lax.axis_size("tensor")
    groups = lax.axis_size("dp")
    width = late.shape[2]
    part = width // ranks
    dma = pltpu.SemaphoreType.DMA

    def kernel(late_ref, early_ref, own_ref, all_ref, dp_ref, mine, first, stage, second, *sems):
        total_kernel(
            ranks, groups, late_ref, early_ref, own_ref, all_ref, dp_ref, mine, first, stage, second, sems
        )

    in_vmem = pl.BlockSpec(memory_space=pltpu.VMEM)
    return pl.pallas_call(
        kernel,
        in_specs=[in_vmem] * 3,
        out_specs=[in_vmem] * 2,
        out_shape=[
            jax.ShapeDtypeStruct((8, width), jnp.float32),
            jax.ShapeDtypeStruct((8, part), jnp.float32),
        ],
        scratch_shapes=[
            pltpu.VMEM((8, width), jnp.float32),
            pltpu.VMEM((ranks, 8, part), jnp.float32),
            pltpu.VMEM((16, part), jnp.float32),
            pltpu.VMEM((groups, 16, part), jnp.float32),
            dma((ranks,)),
            dma((ranks,)),
            dma((groups,)),
            dma((groups,)),
            dma((ranks,)),
            dma((ranks,)),
        ],
        compiler_params=pltpu.CompilerParams(collective_id=5, has_side_effects=True),
        name="total_sums",
    )(late, early, own)


def over_dp(grad, dimension):
    return lax.psum_scatter(grad, "dp", scatter_dimension=dimension, tiled=True).astype(jnp.float32)


def layer(
    layer_input,
    segment_ids,
    first_gain,
    first_shift,
    qkv_weight,
    query_value_bias,
    dense_weight,
    dense_bias,
    second_gain,
    second_shift,
    up_weight,
    up_bias,
    down_weight,
    down_bias,
    out_grad,
):
    rows, width = layer_input.shape
    ranks = lax.axis_size("tensor")
    tokens = ranks * rows
    f32_rows = jax.ShapeDtypeStruct((rows, width), jnp.float32)

    qkv_full = lax.all_gather(qkv_weight, "dp", axis=1, tiled=True)
    dense_full = lax.all_gather(dense_weight, "dp", axis=1, tiled=True)
    up_full = lax.all_gather(up_weight, "dp", axis=0, tiled=True)
    down_full = lax.all_gather(down_weight, "dp", axis=1, tiled=True)
    out_whole = lax.all_gather(out_grad, "tensor", axis=0, tiled=True)

    head_width = qkv_full.shape[2]
    up_width = up_bias.shape[0]
    qkv_cat = jnp.transpose(qkv_full, (1, 0, 2)).reshape(width, 3 * head_width)

    (whole1,) = line_call(
        norm_gather_kernel, 1,
        (layer_input, first_gain[None], first_shift[None]), (), True, False, rows, width,
    )
    whole1 = whole1.reshape(tokens, width)
    zero_bias = jnp.zeros_like(query_value_bias[0])
    bias_cat = jnp.concatenate([query_value_bias[0], zero_bias, query_value_bias[1]])
    projected = (jnp.dot(whole1, qkv_cat, preferred_element_type=jnp.float32) + bias_cat).astype(
        jnp.bfloat16
    )
    head_count = head_width // HEAD_DIM
    tensor_pos = lax.axis_index("tensor")
    global_heads = tensor_pos * head_count + jnp.arange(head_count, dtype=jnp.int32)
    slopes = jnp.power(2.0, -8.0 * (global_heads + 1).astype(jnp.float32) / HEADS)
    attended, log_sums = attention_forward(projected, segment_ids, slopes)
    attn_part = jnp.dot(attended, dense_full, preferred_element_type=jnp.float32).astype(jnp.bfloat16)
    whole2, residual = line_call(
        branch_norm_gather_kernel, 2,
        (attn_part.reshape(ranks, rows, width), layer_input, dense_bias[None], second_gain[None], second_shift[None]),
        (f32_rows,), True, True, rows, width,
    )
    whole2 = whole2.reshape(tokens, width)
    pre_act = jnp.dot(whole2, up_full, preferred_element_type=jnp.float32) + up_bias
    activated = jax.nn.gelu(pre_act, approximate=False).astype(jnp.bfloat16)
    mlp_part = jnp.dot(activated, down_full, preferred_element_type=jnp.float32).astype(jnp.bfloat16)
    act_grad = lax.dot_general(
        out_whole, down_full, (((1,), (1,)), ((), ())), preferred_element_type=jnp.float32
    )
    _, gelu_back = jax.vjp(functools.partial(jax.nn.gelu, approximate=False), pre_act)
    pre_grad = gelu_back(act_grad)[0].astype(jnp.bfloat16)
    up_bias_part = jnp.sum(pre_grad.astype(jnp.float32), axis=0)
    down_grad = lax.dot_general(
        activated, out_whole, (((0,), (0,)), ((), ())), preferred_element_type=jnp.float32
    ).astype(jnp.bfloat16)
    up_grad = lax.dot_general(
        whole2, pre_grad, (((0,), (0,)), ((), ())), preferred_element_type=jnp.float32
    ).astype(jnp.bfloat16)
    pre_grad, down_grad, up_grad, mlp_part = lax.optimization_barrier(
        (pre_grad, down_grad, up_grad, mlp_part)
    )
    down_wgrad = over_dp(down_grad, 1)
    up_wgrad = over_dp(up_grad, 0)
    normed2_part = lax.dot_general(
        pre_grad, up_full, (((1,), (1,)), ((), ())), preferred_element_type=jnp.float32
    ).astype(jnp.bfloat16)
    mlp_rows = lax.psum_scatter(mlp_part, "tensor", scatter_dimension=0, tiled=True)
    mlp_branch = mlp_rows.astype(jnp.float32) + down_bias
    layer_out = (residual + mlp_branch).astype(jnp.bfloat16)

    branch_whole, residual_grad, second_sums = line_call(
        grad_gather_kernel, 3,
        (normed2_part.reshape(ranks, rows, width), residual, out_grad, second_gain[None]),
        (f32_rows, jax.ShapeDtypeStruct((4, 8, width), jnp.float32)), True, True, rows, width,
    )
    branch_whole = branch_whole.reshape(tokens, width)
    attended_grad = lax.dot_general(
        branch_whole, dense_full, (((1,), (1,)), ((), ())), preferred_element_type=jnp.float32
    ).astype(jnp.bfloat16)
    dense_grad = lax.dot_general(
        attended, branch_whole, (((0,), (0,)), ((), ())), preferred_element_type=jnp.float32
    ).astype(jnp.bfloat16)
    attended_grad, dense_grad = lax.optimization_barrier((attended_grad, dense_grad))
    qkv_grad_cat = attention_backward(projected, attended_grad, segment_ids, slopes, log_sums)
    dense_wgrad = over_dp(dense_grad, 1)
    qkv_sums = jnp.sum(qkv_grad_cat.astype(jnp.float32), axis=0)
    bias_part = jnp.stack([qkv_sums[:head_width], qkv_sums[2 * head_width :]])
    qkv_grad_flat = lax.dot_general(
        whole1, qkv_grad_cat, (((0,), (0,)), ((), ())), preferred_element_type=jnp.float32
    )
    qkv_grad = jnp.transpose(
        qkv_grad_flat.astype(jnp.bfloat16).reshape(width, 3, head_width), (1, 0, 2)
    )
    qkv_grad, qkv_grad_cat = lax.optimization_barrier((qkv_grad, qkv_grad_cat))
    qkv_wgrad = over_dp(qkv_grad, 1)
    normed1_part = lax.dot_general(
        qkv_grad_cat, qkv_cat, (((1,), (1,)), ((), ())), preferred_element_type=jnp.float32
    ).astype(jnp.bfloat16)
    input_grad, first_sums = line_call(
        grad_kernel, 4,
        (normed1_part.reshape(ranks, rows, width), layer_input, residual_grad, first_gain[None]),
        (f32_rows, jax.ShapeDtypeStruct((2, 8, width), jnp.float32)), False, True, rows, width,
    )
    part = width // ranks
    own = jnp.concatenate([bias_part.reshape(-1), up_bias_part]).reshape(-1, part)
    bias_rows = 2 * head_width // part
    own = jnp.pad(own, ((0, 8 - own.shape[0]), (0, 0)))
    sums, own = total_call(first_sums, second_sums, own)
    up_rows = up_width // part
    return (
        layer_out,
        input_grad,
        sums[0],
        sums[1],
        qkv_wgrad,
        own[:bias_rows].reshape(2, head_width),
        dense_wgrad,
        sums[4],
        sums[2],
        sums[3],
        up_wgrad,
        own[bias_rows : bias_rows + up_rows].reshape(up_width),
        down_wgrad,
        sums[5],
    )


def solution(mesh):
    token_rows = P(("dp", "tensor"), None)
    placed = (
        token_rows,
        P("dp"),
        P(),
        P(),
        P(None, "dp", "tensor"),
        P(None, "tensor"),
        P("tensor", "dp"),
        P(),
        P(),
        P(),
        P("dp", "tensor"),
        P("tensor"),
        P("tensor", "dp"),
        P(),
        token_rows,
    )
    return jax.shard_map(
        layer,
        mesh=mesh,
        in_specs=placed,
        out_specs=(
            token_rows,
            token_rows,
            P(),
            P(),
            P(None, "dp", "tensor"),
            P(None, "tensor"),
            P("tensor", "dp"),
            P(),
            P(),
            P(),
            P("dp", "tensor"),
            P("tensor"),
            P("tensor", "dp"),
            P(),
        ),
        check_vma=False,
    )
```

profile of v0, /device:TPU:8, one launch (start us, length us, event | category | flops | bytes accessed | tf_op | source)
XLA Modules:
  0.0 867.6 jit_solution(14952861093832917507)
XLA Ops:
  7.2 2.3 copy.30
  9.6 0.7 all-gather.8.cloned.1.call-update
  12.3 1.1 copy.31.seg_col_ref
  13.3 1.6 copy-done
  14.9 0.7 copy-done.15
  15.6 0.7 copy-done.19
  16.3 70.8 %shard_map.254 = bf16[8,256,2048]{2,1,0:T(8,128)(2,1)} custom-call(bf16[256,2048]{1,0:T(8,128)(2,1)S(1)} %copy-done, f32[1,2048]{1,0:T(1,128)S(1)} %bitcast.58, f32[1,2048]{1,0:T(1,128)S(1)} %bitcast.62), custom_call_target="tpu_custom_call" | custom-call | flops 419430400 | bytes 52428800 | tf_op jit(solution)/shard_map/pallas_call | solution.py:618
  87.3 10.1 %add_convert_fusion.1.proj_ref = bf16[2048,768]{1,0:T(8,128)(2,1)S(1)} fusion(f32[768]{0:T(1024)S(1)} %pad_maximum_fusion.1, bf16[2048,2048]{1,0:T(8,128)(2,1)} %bitcast.72, bf16[2048,768]{0,1:T(8,128)(2,1)} %bitcast.91), kind=kOutput, calls=%fused_computation.23 | convolution fusion | flops 6445596672 | bytes 14683136 | tf_op jit(solution)/shard_map/dot_general | solution.py:805
  97.4 20.9 %attention_forward.1 = (bf16[2048,256]{1,0:T(8,128)(2,1)S(1)}, f32[4,2048]{1,0:T(4,128)S(1)}) custom-call(f32[4]{0:T(128)S(1)} %multiply_power_fusion.slope_ref, bf16[2048,768]{1,0:T(8,128)(2,1)S(1)} %add_convert_fusion.1.proj_ref, s32[1,2048]{1,0:T(1,128)S(1)} %bitcast.64, s32[2048,1]{1,0:T(8,128)S(1)} %copy.31.seg_col_ref), custom_call_target="tpu_custom_call" | custom-call | flops 1610612736 | bytes 3145728 | tf_op jit(solution)/shard_map/attention_forward/pallas_call | solution.py:89
  118.3 1.7 copy-done.26
  120.0 7.2 convolution_convert_fusion.3
  127.3 184.7 %shard_map.255 = (bf16[8,256,2048]{2,1,0:T(8,128)(2,1)}, f32[256,2048]{1,0:T(8,128)S(1)}) custom-call(bf16[8,256,2048]{2,1,0:T(8,128)(2,1)} %bitcast.68, bf16[256,2048]{1,0:T(8,128)(2,1)S(1)} %copy-done.1, f32[1,2048]{1,0:T(1,128)S(1)} %bitcast.66, f32[1,2048]{1,0:T(1,128)S(1)} %bitcast.60, f32[1,2048]{1,0:T(1,128)S(1)} %bitcast.67), custom_call_target="tpu_custom_call" | custom-call | flops 419430400 | bytes 52428800 | tf_op jit(solution)/shard_map/pallas_call | solution.py:618
  312.0 1.3 copy-done.4
  313.4 14.4 %fusion.10 = f32[2048,1024]{1,0:T(8,128)} fusion(bf16[2048,2048]{1,0:T(8,128)(2,1)} %bitcast.89, bf16[2048,1024]{1,0:T(8,128)(2,1)} %all-gather.10.cloned.1.call-done), kind=kOutput, calls=%fused_computation.38 | convolution fusion | flops 8589934592 | bytes 20971520 | tf_op jit(solution)/shard_map/dot_general | solution.py:820
  327.8 32.9 %convert_reduce_fusion = (f32[1024]{0:T(1024)S(1)}, bf16[2048,1024]{1,0:T(8,128)(2,1)S(1)}, f32[2048,1024]{1,0:T(8,128)}) fusion(f32[2048,1024]{1,0:T(8,128)} %fusion.10, f32[1024]{0:T(1024)S(1)} %copy-done.29, bf16[2048,2048]{1,0:T(8,128)(2,1)} %all-gather.12.cloned.1.call-done, bf16[1024,2048]{1,0:T(8,128)(2,1)} %all-gather.14.cloned.1.call-done), kind=kOutput, calls=%fused_computation.2 | convolution fusion | flops 8747219968 | bytes 33562624 | tf_op jit(solution)/shard_map/dot_general | solution.py:823
  360.7 2.0 copy-done.31
  362.7 13.3 %convolution_convert_fusion.5 = bf16[2048,1024]{1,0:T(8,128)(2,1)} fusion(bf16[2048,2048]{1,0:T(8,128)(2,1)} %bitcast.90, bf16[2048,1024]{1,0:T(8,128)(2,1)S(1)} %get-tuple-element.37), kind=kOutput, calls=%fused_computation.25 | convolution fusion | flops 8592031744 | bytes 16777216 | tf_op jit(solution)/shard_map/dot_general | solution.py:832
  376.0 10.0 %multiply_convert_fusion = bf16[2048,1024]{1,0:T(8,128)(2,1)} fusion(f32[2048,1024]{1,0:T(8,128)} %get-tuple-element.54, f32[2048,1024]{1,0:T(8,128)} %fusion.10, f32[1024]{0:T(1024)S(1)} %copy-done.29), kind=kLoop, calls=%fused_computation.3 | loop fusion | flops 8388608 | bytes 20975616 | tf_op jit(solution)/shard_map/convert_element_type | solution.py:821
  386.0 14.0 %convolution_convert_fusion.4 = bf16[1024,2048]{1,0:T(8,128)(2,1)} fusion(bf16[2048,1024]{1,0:T(8,128)(2,1)} %multiply_convert_fusion, bf16[2048,2048]{1,0:T(8,128)(2,1)} %all-gather.12.cloned.1.call-done), kind=kOutput, calls=%fused_computation.24 | convolution fusion | flops 8592031744 | bytes 16777216 | tf_op jit(solution)/shard_map/dot_general | solution.py:829
  400.0 14.2 %convolution_convert_fusion.2 = bf16[2048,2048]{1,0:T(8,128)(2,1)} fusion(bf16[2048,1024]{1,0:T(8,128)(2,1)} %multiply_convert_fusion, bf16[1024,2048]{1,0:T(8,128)(2,1)} %all-gather.14.cloned.1.call-done), kind=kOutput, calls=%fused_computation.20 | convolution fusion | flops 8594128896 | bytes 16777216 | tf_op jit(solution)/shard_map/dot_general | solution.py:822
  414.2 14.2 %convolution_convert_fusion.1 = bf16[2048,2048]{1,0:T(8,128)(2,1)} fusion(bf16[2048,1024]{1,0:T(8,128)(2,1)} %copy-done.31, bf16[2048,1024]{1,0:T(8,128)(2,1)} %all-gather.10.cloned.1.call-done), kind=kOutput, calls=%fused_computation.19 | convolution fusion | flops 8594128896 | bytes 16777216 | tf_op jit(solution)/shard_map/dot_general | solution.py:840
  428.4 118.5 %shard_map.256 = (bf16[8,256,2048]{2,1,0:T(8,128)(2,1)}, f32[256,2048]{1,0:T(8,128)S(1)}, f32[4,8,2048]{2,1,0:T(8,128)S(1)}) custom-call(bf16[8,256,2048]{2,1,0:T(8,128)(2,1)} %bitcast.74, f32[256,2048]{1,0:T(8,128)S(1)} %copy-done.5, bf16[256,2048]{1,0:T(8,128)(2,1)S(1)} %copy-done.6, f32[1,2048]{1,0:T(1,128)S(1)} %bitcast.61), custom_call_target="tpu_custom_call" | custom-call | flops 419430400 | bytes 52428800 | tf_op jit(solution)/shard_map/pallas_call | solution.py:618
  547.0 1.3 copy-done.8
  548.3 0.7 copy-done.13
  549.0 6.7 convolution_convert_fusion.7
  555.7 7.0 convolution_convert_fusion.8.grad_ref
  562.8 1.2 copy-done.12
  564.1 1.2 copy-done.27
  565.3 27.2 %attention_backward.1 = bf16[2048,768]{1,0:T(8,128)(2,1)S(1)} custom-call(f32[4]{0:T(128)S(1)} %copy-done.25, bf16[2048,768]{1,0:T(8,128)(2,1)} %copy-done.26, bf16[2048,256]{1,0:T(8,128)(2,1)S(1)} %copy-done.27, f32[4,2048]{1,0:T(4,128)S(1)} %get-tuple-element.40.lse_ref, s32[1,2048]{1,0:T(1,128)S(1)} %bitcast.65, s32[2048,1]{1,0:T(8,128)S(1)} %copy-done.12), custom_call_target="tpu_custom_call" | custom-call | flops 4026531840 | bytes 7340032 | tf_op jit(solution)/shard_map/attention_backward/pallas_call | solution.py:181
  592.5 11.5 %convolution_convert_fusion.6 = bf16[2048,768]{0,1:T(8,128)(2,1)} fusion(bf16[2048,2048]{1,0:T(8,128)(2,1)} %bitcast.73, bf16[2048,768]{1,0:T(8,128)(2,1)S(1)} %attention_backward.1), kind=kOutput, calls=%fused_computation.26 | convolution fusion | flops 6444023808 | bytes 14680064 | tf_op jit(solution)/shard_map/dot_general | solution.py:864
  604.0 4.7 copy.33
  608.7 0.7 reduce-scatter.14.cloned.1.call-update
  610.7 2.4 convert_reduce_fusion.1
  613.8 11.4 %convolution_convert_fusion = bf16[2048,2048]{1,0:T(8,128)(2,1)} fusion(bf16[2048,768]{1,0:T(8,128)(2,1)} %copy-done.7, bf16[2048,768]{0,1:T(8,128)(2,1)} %bitcast.92), kind=kOutput, calls=%fused_computation.18 | convolution fusion | flops 6446645248 | bytes 14680064 | tf_op jit(solution)/shard_map/dot_general | solution.py:872
  625.2 79.7 %shard_map.257 = (f32[256,2048]{1,0:T(8,128)S(1)}, f32[2,8,2048]{2,1,0:T(8,128)S(1)}) custom-call(bf16[8,256,2048]{2,1,0:T(8,128)(2,1)} %bitcast.75, bf16[256,2048]{1,0:T(8,128)(2,1)S(1)} %copy-done.1, f32[256,2048]{1,0:T(8,128)S(1)} %copy-done.9, f32[1,2048]{1,0:T(1,128)S(1)} %bitcast.59), custom_call_target="tpu_custom_call" | custom-call | flops 419430400 | bytes 52428800 | tf_op jit(solution)/shard_map/pallas_call | solution.py:618
  704.9 1.3 copy-done.10
  706.9 15.2 %total_sums.1 = (f32[8,2048]{1,0:T(8,128)}, f32[8,256]{1,0:T(8,128)}) custom-call(f32[2,8,2048]{2,1,0:T(8,128)} %copy-done.14, f32[4,8,2048]{2,1,0:T(8,128)} %copy-done.13, f32[8,256]{1,0:T(8,128)} %pad.4.own_ref), custom_call_target="tpu_custom_call" | custom-call | tf_op jit(solution)/shard_map/total_sums/pallas_call | solution.py:737
  722.1 1.3 slice.42
  723.4 0.7 slice_bitcast_fusion
  724.7 1.9 fusion.7
  726.6 1.8 convert_element_type.83
  728.4 2.5 convert_element_type.82
  730.9 2.9 convert_element_type.85
  733.8 32.1 %reduce-scatter.12.cloned.1.call-done = bf16[512,1024]{1,0:T(8,128)(2,1)} async-done(((bf16[2048,1024]{1,0:T(8,128)(2,1)}), bf16[512,1024]{1,0:T(8,128)(2,1)}) %reduce-scatter.12.cloned.1.call-update) | async-done | bytes 1048592 | tf_op jit(solution)/shard_map/reduce_scatter | solution.py:763
  765.8 2.8 convert_element_type.84
  768.6 86.1 %reduce-scatter.6.cloned.1.call-done = bf16[256,2048]{1,0:T(8,128)(2,1)} async-done(((bf16[2048,2048]{1,0:T(8,128)(2,1)}), bf16[256,2048]{1,0:T(8,128)(2,1)}) %reduce-scatter.6.cloned.1.call-update) | async-done | bytes 1048592 | tf_op jit(solution)/shard_map/reduce_scatter | solution.py:843
  854.8 2.5 add_convert_fusion.2
  857.3 3.1 copy.37
  (90 shorter events, 5.5 us)
Async XLA Ops:
  7.2 80.0 %copy-start.30 = (f32[2,256]{1,0:T(2,128)S(1)}, f32[2,256]{1,0:T(2,128)}, u32[]{:S(2)}) copy-start(f32[2,256]{1,0:T(2,128)} %param.20) | copy-start | bytes 6148
  7.2 80.0 %all-gather.6.cloned.1.call-start = ((), (), s32[]{:S(2)}) async-start(), calls=%async_computation.5 | async-start | bytes 3932160 | tf_op jit(solution)/shard_map/all_gather | solution.py:788
  9.6 110.5 %all-gather.8.cloned.1.call-start = ((), (), s32[]{:S(2)}) async-start(), calls=%async_computation.6 | async-start | bytes 1310720 | tf_op jit(solution)/shard_map/all_gather | solution.py:789
  10.3 303.1 %all-gather.10.cloned.1.call-start = ((), (), s32[]{:S(2)}) async-start(), calls=%async_computation.7 | async-start | bytes 5242880 | tf_op jit(solution)/shard_map/all_gather | solution.py:790
  11.0 316.8 %all-gather.14.cloned.1.call-start = ((), (), s32[]{:S(2)}) async-start(), calls=%async_computation.9 | async-start | bytes 5242880 | tf_op jit(solution)/shard_map/all_gather | solution.py:791
  11.6 316.2 %all-gather.12.cloned.1.call-start = ((), (), s32[]{:S(2)}) async-start(), calls=%async_computation.8 | async-start | bytes 9437184 | tf_op jit(solution)/shard_map/all_gather | solution.py:792
  12.2 714.4 %reduce-scatter.10.cloned.1.call-start = ((), (), s32[]{:S(2)}) async-start(), calls=%async_computation.12 | async-start | bytes 1310720 | tf_op jit(solution)/shard_map/reduce_scatter | solution.py:763
  13.3 84.0 %copy-start.11 = (s32[2048,1]{1,0:T(8,128)}, s32[2048,1]{1,0:T(8,128)S(1)}, u32[]{:S(2)}) copy-start(s32[2048,1]{1,0:T(8,128)S(1)} %copy.31.seg_col_ref) | copy-start | bytes 24580
  13.3 1.6 copy-start
  14.9 0.7 copy-start.15
  15.6 0.7 copy-start.19
  87.2 10.2 %copy-start.24 = (f32[4]{0:T(128)}, f32[4]{0:T(128)S(1)}, u32[]{:S(2)}) copy-start(f32[4]{0:T(128)S(1)} %multiply_power_fusion.slope_ref) | copy-start | bytes 52
  87.2 10.1 %copy-start.20 = (s32[2048]{0:T(1024)S(1)}, s32[2048]{0:T(1024)}, u32[]{:S(2)}) copy-start(s32[2048]{0:T(1024)} %param.16) | copy-start | bytes 24580
  118.3 1.7 copy-start.26
  120.0 192.1 %copy-start.2 = (bf16[2048,256]{1,0:T(8,128)(2,1)}, bf16[2048,256]{1,0:T(8,128)(2,1)S(1)}, u32[]{:S(2)}) copy-start(bf16[2048,256]{1,0:T(8,128)(2,1)S(1)} %get-tuple-element.33) | copy-start | bytes 3145732
  120.0 7.3 copy-start.1
  120.0 7.3 copy-start.17
  120.0 7.3 copy-start.22
  120.0 7.3 copy-start.23
  312.0 1.3 copy-start.4
  313.4 14.4 %copy-start.29 = (f32[1024]{0:T(1024)S(1)}, f32[1024]{0:T(1024)}, u32[]{:S(2)}) copy-start(f32[1024]{0:T(1024)} %param.26) | copy-start | bytes 12292
  360.7 2.0 copy-start.31
  414.2 14.2 %copy-start.5 = (f32[256,2048]{1,0:T(8,128)S(1)}, f32[256,2048]{1,0:T(8,128)}, u32[]{:S(2)}) copy-start(f32[256,2048]{1,0:T(8,128)} %copy-done.4) | copy-start | bytes 6291460
  414.2 14.2 %copy-start.6 = (bf16[256,2048]{1,0:T(8,128)(2,1)S(1)}, bf16[256,2048]{1,0:T(8,128)(2,1)}, u32[]{:S(2)}) copy-start(bf16[256,2048]{1,0:T(8,128)(2,1)} %grad_ref.1) | copy-start | bytes 3145732
  414.2 14.2 %copy-start.18 = (f32[2048]{0:T(1024)S(1)}, f32[2048]{0:T(1024)}, u32[]{:S(2)}) copy-start(f32[2048]{0:T(1024)} %param.23) | copy-start | bytes 24580
  428.4 120.6 %copy-start.3 = (bf16[2048,256]{1,0:T(8,128)(2,1)S(1)}, bf16[2048,256]{1,0:T(8,128)(2,1)}, u32[]{:S(2)}) copy-start(bf16[2048,256]{1,0:T(8,128)(2,1)} %copy-done.2) | copy-start | bytes 3145732
  547.0 1.3 copy-start.8
  548.3 0.7 copy-start.13
  555.7 7.1 copy-start.21
  555.7 7.1 copy-start.25
  562.8 165.6 %reduce-scatter.8.cloned.1.call-start = ((), (), s32[]{:S(2)}) async-start(), calls=%async_computation.11 | async-start | bytes 3932160 | tf_op jit(solution)/shard_map/reduce_scatter | solution.py:763
  562.8 1.2 copy-start.12
  564.1 1.2 copy-start.27
  592.5 11.5 %copy-start.7 = (bf16[2048,768]{1,0:T(8,128)(2,1)}, bf16[2048,768]{1,0:T(8,128)(2,1)S(1)}, u32[]{:S(2)}) copy-start(bf16[2048,768]{1,0:T(8,128)(2,1)S(1)} %attention_backward.1) | copy-start | bytes 9437188
  608.6 122.3 %reduce-scatter.14.cloned.1.call-start = ((), (), s32[]{:S(2)}) async-start(), calls=%async_computation.14 | async-start | bytes 5242880 | tf_op jit(solution)/shard_map/reduce_scatter | solution.py:763
  609.4 156.5 %reduce-scatter.12.cloned.1.call-start = ((), (), s32[]{:S(2)}) async-start(), calls=%async_computation.13 | async-start | bytes 5242880 | tf_op jit(solution)/shard_map/reduce_scatter | solution.py:763
  610.1 244.6 %reduce-scatter.6.cloned.1.call-start = ((), (), s32[]{:S(2)}) async-start(), calls=%async_computation.10 | async-start | bytes 9437184 | tf_op jit(solution)/shard_map/reduce_scatter | solution.py:843
  613.8 11.4 %copy-start.9 = (f32[256,2048]{1,0:T(8,128)S(1)}, f32[256,2048]{1,0:T(8,128)}, u32[]{:S(2)}) copy-start(f32[256,2048]{1,0:T(8,128)} %copy-done.8) | copy-start | bytes 6291460
  613.8 11.4 %copy-start.16 = (f32[2048]{0:T(1024)S(1)}, f32[2048]{0:T(1024)}, u32[]{:S(2)}) copy-start(f32[2048]{0:T(1024)} %param.17) | copy-start | bytes 24580
  625.2 229.5 %copy-start.28 = (f32[2048]{0:T(1024)S(1)}, f32[2048]{0:T(1024)}, u32[]{:S(2)}) copy-start(f32[2048]{0:T(1024)} %param.28) | copy-start | bytes 24580
  704.9 1.3 copy-start.10
  706.2 0.7 copy-start.14
Sparse Core Ops, SparseCore 0:
  10.4 44.8 all-gather.5
  57.1 26.3 all-gather.7
  85.4 52.5 all-gather.9
  139.7 52.4 all-gather.13
  193.6 107.0 all-gather.11
  562.9 29.8 reduce-scatter.9
  608.8 45.8 reduce-scatter.7
  657.6 52.5 reduce-scatter.13
  713.2 52.5 reduce-scatter.11
  768.0 86.7 reduce-scatter.5
where the time goes:
time: 880 us; the launch traced here: 868 us
  Pallas kernels  517 us (59%)
  matrix products  157 us (18%)
  waiting for transfers between devices  123 us (14%)
  local copies, waits for them, and re-layouts  30.8 us (4%)
  other arithmetic  24.9 us (3%)
  between operations  14.9 us (2%)
    pallas_call x4, Pallas kernels, line_call(): pl.pallas_call(functools.partial(kernel, chips), in_specs=([in_place] if...  454 us
    reduce_scatter x1, waiting for transfers between devices, layer(): lax.psum_scatter(mlp_part, 'tensor', scatter_dimension=0, tiled=True)  86.1 us
    dot_general x1, matrix products, layer(): lax.dot_general(out_whole, down_full, (((1,), (1,)), ((), ())), preferred...  32.9 us
    reduce_scatter x4, waiting for transfers between devices, over_dp(): lax.psum_scatter(grad, 'dp', scatter_dimension=dimension, tiled=True)  32.1 us
    pallas_call x1, Pallas kernels, attention_backward(): pl.pallas_call(backward_kernel, grid=(seq_len // Q_BLOCK,), in_specs=[pl....  27.2 us
    unnamed x69, local copies, waits for them, and re-layouts  21.2 us
    pallas_call x1, Pallas kernels, attention_forward(): pl.pallas_call(forward_kernel, grid=(seq_len // Q_BLOCK,), in_specs=[pl.B...  20.9 us
  transfers between devices with their start and end apart: 10, of which 2 were waited for; matrix products, arithmetic and copies ran while one was open for 9% of the time, Pallas kernels for 46%

commit v1 on v0

--- a/solution.py
+++ b/solution.py
@@ -1,4 +1,5 @@
 import functools
+import math
 
 import jax
 import jax.numpy as jnp
@@ -759,6 +760,119 @@
     )(late, early, own)
 
 
+MLP_TILE = 256
+
+
+def mlp_forward_kernel(rows_ref, up_ref, bias_ref, down_ref, active_ref, slope_ref, out_ref):
+    width = up_ref.shape[1]
+    for first in range(0, width, MLP_TILE):
+        cols = slice(first, first + MLP_TILE)
+        value = jnp.dot(rows_ref[...], up_ref[:, cols], preferred_element_type=jnp.float32)
+        value = value + bias_ref[:, cols]
+        below = 0.5 + 0.5 * lax.erf(value * math.sqrt(0.5))
+        density = jnp.exp(-0.5 * value * value) * (1.0 / math.sqrt(2.0 * math.pi))
+        slope_ref[:, cols] = below + value * density
+        active_ref[:, cols] = (value * below).astype(jnp.bfloat16)
+    out_ref[...] = jnp.dot(
+        active_ref[...], down_ref[...], preferred_element_type=jnp.float32
+    ).astype(jnp.bfloat16)
+
+
+def resident(shape):
+    return pl.BlockSpec(shape, lambda i: (0,) * len(shape), pipeline_mode=pl.Buffered(1))
+
+
+def mlp_forward(rows, up_full, up_bias, down_full):
+    tokens, width = rows.shape
+    hidden = up_full.shape[1]
+    block = min(256, tokens)
+    return pl.pallas_call(
+        mlp_forward_kernel,
+        grid=(tokens // block,),
+        in_specs=[
+            pl.BlockSpec((block, width), lambda i: (i, 0)),
+            resident((width, hidden)),
+            resident((1, hidden)),
+            resident((hidden, width)),
+        ],
+        out_specs=[
+            pl.BlockSpec((block, hidden), lambda i: (i, 0)),
+            pl.BlockSpec((block, hidden), lambda i: (i, 0)),
+            pl.BlockSpec((block, width), lambda i: (i, 0)),
+        ],
+        out_shape=[
+            jax.ShapeDtypeStruct((tokens, hidden), jnp.bfloat16),
+            jax.ShapeDtypeStruct((tokens, hidden), jnp.float32),
+            jax.ShapeDtypeStruct((tokens, width), jnp.bfloat16),
+        ],
+        compiler_params=pltpu.CompilerParams(vmem_limit_bytes=48 * 2**20),
+        cost_estimate=pl.CostEstimate(
+            flops=4 * tokens * width * hidden, bytes_accessed=8 * tokens * width, transcendentals=0
+        ),
+        name="mlp_forward",
+    )(rows, up_full, up_bias[None], down_full)
+
+
+def mlp_backward_kernel(
+    one_ref, two_ref, slope_ref, down_ref, up_ref, whole_ref, pre_ref, part_ref, sums_ref
+):
+    half = one_ref.shape[1]
+    whole_ref[:half, :] = one_ref[0]
+    whole_ref[half:, :] = two_ref[0]
+    hidden = slope_ref.shape[1]
+
+    @pl.when(pl.program_id(0) == 0)
+    def _():
+        sums_ref[...] = jnp.zeros_like(sums_ref)
+
+    for first in range(0, hidden, MLP_TILE):
+        cols = slice(first, first + MLP_TILE)
+        grad = lax.dot_general(
+            whole_ref[...], down_ref[cols, :], NT, preferred_element_type=jnp.float32
+        )
+        pre = (grad * slope_ref[:, cols]).astype(jnp.bfloat16)
+        pre_ref[:, cols] = pre
+        sums_ref[:, cols] += jnp.sum(pre.astype(jnp.float32).reshape(-1, 8, MLP_TILE), axis=0)
+    part_ref[...] = lax.dot_general(
+        pre_ref[...], up_ref[...], NT, preferred_element_type=jnp.float32
+    ).astype(jnp.bfloat16)
+
+
+def mlp_backward(one, two, slope, down_full, up_full):
+    ranks, half, width = one.shape
+    rows = 2 * half
+    hidden = slope.shape[1]
+    tokens = ranks * rows
+    return pl.pallas_call(
+        mlp_backward_kernel,
+        grid=(ranks,),
+        in_specs=[
+            pl.BlockSpec((1, half, width), lambda i: (i, 0, 0)),
+            pl.BlockSpec((1, half, width), lambda i: (i, 0, 0)),
+            pl.BlockSpec((rows, hidden), lambda i: (i, 0)),
+            resident((hidden, width)),
+            resident((width, hidden)),
+        ],
+        out_specs=[
+            pl.BlockSpec((rows, width), lambda i: (i, 0)),
+            pl.BlockSpec((rows, hidden), lambda i: (i, 0)),
+            pl.BlockSpec((rows, width), lambda i: (i, 0)),
+            pl.BlockSpec((8, hidden), lambda i: (0, 0)),
+        ],
+        out_shape=[
+            jax.ShapeDtypeStruct((tokens, width), jnp.bfloat16),
+            jax.ShapeDtypeStruct((tokens, hidden), jnp.bfloat16),
+            jax.ShapeDtypeStruct((tokens, width), jnp.bfloat16),
+            jax.ShapeDtypeStruct((8, hidden), jnp.float32),
+        ],
+        compiler_params=pltpu.CompilerParams(vmem_limit_bytes=48 * 2**20),
+        cost_estimate=pl.CostEstimate(
+            flops=4 * tokens * width * hidden, bytes_accessed=10 * tokens * width, transcendentals=0
+        ),
+        name="mlp_backward",
+    )(one, two, slope, down_full, up_full)
+
+
 def over_dp(grad, dimension):
     return lax.psum_scatter(grad, "dp", scatter_dimension=dimension, tiled=True).astype(jnp.float32)
 
@@ -789,7 +903,9 @@
     dense_full = lax.all_gather(dense_weight, "dp", axis=1, tiled=True)
     up_full = lax.all_gather(up_weight, "dp", axis=0, tiled=True)
     down_full = lax.all_gather(down_weight, "dp", axis=1, tiled=True)
-    out_whole = lax.all_gather(out_grad, "tensor", axis=0, tiled=True)
+    half = rows // 2
+    out_one = lax.all_gather(out_grad[:half], "tensor", axis=0, tiled=False)
+    out_two = lax.all_gather(out_grad[half:], "tensor", axis=0, tiled=False)
 
     head_width = qkv_full.shape[2]
     up_width = up_bias.shape[0]
@@ -817,29 +933,20 @@
         (f32_rows,), True, True, rows, width,
     )
     whole2 = whole2.reshape(tokens, width)
-    pre_act = jnp.dot(whole2, up_full, preferred_element_type=jnp.float32) + up_bias
-    activated = jax.nn.gelu(pre_act, approximate=False).astype(jnp.bfloat16)
-    mlp_part = jnp.dot(activated, down_full, preferred_element_type=jnp.float32).astype(jnp.bfloat16)
-    act_grad = lax.dot_general(
-        out_whole, down_full, (((1,), (1,)), ((), ())), preferred_element_type=jnp.float32
-    )
-    _, gelu_back = jax.vjp(functools.partial(jax.nn.gelu, approximate=False), pre_act)
-    pre_grad = gelu_back(act_grad)[0].astype(jnp.bfloat16)
-    up_bias_part = jnp.sum(pre_grad.astype(jnp.float32), axis=0)
+    activated, slope, mlp_part = mlp_forward(whole2, up_full, up_bias, down_full)
+    out_whole, pre_grad, normed2_part, up_bias_sums = mlp_backward(
+        out_one, out_two, slope, down_full, up_full
+    )
+    up_bias_part = jnp.sum(up_bias_sums, axis=0)
     down_grad = lax.dot_general(
         activated, out_whole, (((0,), (0,)), ((), ())), preferred_element_type=jnp.float32
     ).astype(jnp.bfloat16)
     up_grad = lax.dot_general(
         whole2, pre_grad, (((0,), (0,)), ((), ())), preferred_element_type=jnp.float32
     ).astype(jnp.bfloat16)
-    pre_grad, down_grad, up_grad, mlp_part = lax.optimization_barrier(
-        (pre_grad, down_grad, up_grad, mlp_part)
-    )
+    normed2_part, down_grad, up_grad = lax.optimization_barrier((normed2_part, down_grad, up_grad))
     down_wgrad = over_dp(down_grad, 1)
     up_wgrad = over_dp(up_grad, 0)
-    normed2_part = lax.dot_general(
-        pre_grad, up_full, (((1,), (1,)), ((), ())), preferred_element_type=jnp.float32
-    ).astype(jnp.bfloat16)
     mlp_rows = lax.psum_scatter(mlp_part, "tensor", scatter_dimension=0, tiled=True)
     mlp_branch = mlp_rows.astype(jnp.float32) + down_bias
     layer_out = (residual + mlp_branch).astype(jnp.bfloat16)

time: 880 us -> 837 us (0.951)
  matrix products: 157 us -> 78.2 us
  Pallas kernels: 517 us -> 568 us
  other arithmetic: 24.9 us -> 15.3 us
    dot_general x4 -> x0, matrix products: 75.7 us -> none  [the longest x1 32.9 us: layer(): lax.dot_general(out_whole, down_full, (((1,), (1,)), ((), ())), preferred...]
    pallas_call x0 -> x2, Pallas kernels: none -> 52.2 us  [the longest x1 26.9 us: mlp_forward(): pl.pallas_call(mlp_forward_kernel, grid=(tokens // block,), in_specs=[pl....]
    convert_element_type x1 -> x0, other arithmetic: 10 us -> none  [layer(): activated = jax.nn.gelu(pre_act, approximate=False).astype(jnp.bfloat16)]
    unnamed x69 -> x57, local copies, waits for them, and re-layouts: 21.2 us -> 15.6 us
  transfers between devices with their start and end apart: 10 -> 11, of which waited for: 2 -> 2; matrix products, arithmetic and copies ran while one was open for 9% -> 8% of each run, Pallas kernels for 46% -> 51%
where the time goes in v1:
time: 837 us; the launch traced here: 825 us
  Pallas kernels  568 us (68%)
  waiting for transfers between devices  123 us (15%)
  matrix products  78.2 us (9%)
  local copies, waits for them, and re-layouts  26.3 us (3%)
  other arithmetic  15.3 us (2%)
  between operations  14.4 us (2%)
    pallas_call x4, Pallas kernels, line_call(): pl.pallas_call(functools.partial(kernel, chips), in_specs=([in_place] if...  452 us
    reduce_scatter x1, waiting for transfers between devices, layer(): lax.psum_scatter(mlp_part, 'tensor', scatter_dimension=0, tiled=True)  86.3 us
    reduce_scatter x4, waiting for transfers between devices, over_dp(): lax.psum_scatter(grad, 'dp', scatter_dimension=dimension, tiled=True)  32 us
    pallas_call x1, Pallas kernels, attention_backward(): pl.pallas_call(backward_kernel, grid=(seq_len // Q_BLOCK,), in_specs=[pl....  27.9 us
    pallas_call x1, Pallas kernels, mlp_forward(): pl.pallas_call(mlp_forward_kernel, grid=(tokens // block,), in_specs=[pl....  26.9 us
    pallas_call x1, Pallas kernels, mlp_backward(): pl.pallas_call(mlp_backward_kernel, grid=(ranks,), in_specs=[pl.BlockSpec...  25.3 us
    pallas_call x1, Pallas kernels, attention_forward(): pl.pallas_call(forward_kernel, grid=(seq_len // Q_BLOCK,), in_specs=[pl.B...  20.9 us
  transfers between devices with their start and end apart: 11, of which 2 were waited for; matrix products, arithmetic and copies ran while one was open for 8% of the time, Pallas kernels for 51%

profile of v1, /device:TPU:8, one launch (start us, length us, event | category | flops | bytes accessed | tf_op | source)
XLA Modules:
  0.0 825.4 jit_solution(13758603747468897657)
XLA Ops:
  7.3 2.4 copy.30
  9.8 0.7 all-gather.11.cloned.1.call-update
  10.5 0.7 all-gather.13.cloned.1.call-update
  11.8 1.0 fusion
  13.5 1.3 copy.31.seg_col_ref
  14.9 70.9 %shard_map.254 = bf16[8,256,2048]{2,1,0:T(8,128)(2,1)} custom-call(bf16[256,2048]{1,0:T(8,128)(2,1)S(1)} %copy-done, f32[1,2048]{1,0:T(1,128)S(1)} %bitcast.53, f32[1,2048]{1,0:T(1,128)S(1)} %bitcast.57), custom_call_target="tpu_custom_call" | custom-call | flops 419430400 | bytes 52428800 | tf_op jit(solution)/shard_map/pallas_call | solution.py:619
  85.9 10.2 %add_convert_fusion.proj_ref = bf16[2048,768]{1,0:T(8,128)(2,1)S(1)} fusion(f32[768]{0:T(1024)S(1)} %pad_maximum_fusion.1, bf16[2048,2048]{1,0:T(8,128)(2,1)} %bitcast.68, bf16[2048,768]{0,1:T(8,128)(2,1)} %bitcast.89), kind=kOutput, calls=%fused_computation.3 | convolution fusion | flops 6445596672 | bytes 14683136 | tf_op jit(solution)/shard_map/dot_general | solution.py:921
  96.1 20.9 %attention_forward.1 = (bf16[2048,256]{1,0:T(8,128)(2,1)S(1)}, f32[4,2048]{1,0:T(4,128)S(1)}) custom-call(f32[4]{0:T(128)S(1)} %multiply_power_fusion.slope_ref, bf16[2048,768]{1,0:T(8,128)(2,1)S(1)} %add_convert_fusion.proj_ref, s32[1,2048]{1,0:T(1,128)S(1)} %bitcast.59, s32[2048,1]{1,0:T(8,128)S(1)} %copy-done.10), custom_call_target="tpu_custom_call" | custom-call | flops 1610612736 | bytes 3145728 | tf_op jit(solution)/shard_map/attention_forward/pallas_call | solution.py:90
  117.0 1.7 copy-done.21
  118.7 6.9 convolution_convert_fusion.1
  125.6 183.0 %shard_map.255 = (bf16[8,256,2048]{2,1,0:T(8,128)(2,1)}, f32[256,2048]{1,0:T(8,128)S(1)}) custom-call(bf16[8,256,2048]{2,1,0:T(8,128)(2,1)} %bitcast.64, bf16[256,2048]{1,0:T(8,128)(2,1)S(1)} %copy-done, f32[1,2048]{1,0:T(1,128)S(1)} %bitcast.61, f32[1,2048]{1,0:T(1,128)S(1)} %bitcast.55, f32[1,2048]{1,0:T(1,128)S(1)} %bitcast.62), custom_call_target="tpu_custom_call" | custom-call | flops 419430400 | bytes 52428800 | tf_op jit(solution)/shard_map/pallas_call | solution.py:619
  308.6 1.3 copy-done.1
  309.9 26.9 %mlp_forward.1 = (bf16[2048,1024]{1,0:T(8,128)(2,1)S(1)}, f32[2048,1024]{1,0:T(8,128)}, bf16[2048,2048]{1,0:T(8,128)(2,1)}) custom-call(bf16[2048,2048]{1,0:T(8,128)(2,1)} %bitcast.85, bf16[2048,1024]{1,0:T(8,128)(2,1)} %all-gather.13.cloned.1.call-done.up_ref, f32[1,1024]{1,0:T(1,128)S(1)} %bitcast.63, bf16[1024,2048]{1,0:T(8,128)(2,1)} %all-gather.15.cloned.1.call-done.down_ref), custom_call_target="tpu_custom_call" | custom-call | flops 17179869184 | bytes 33554432 | tf_op jit(solution)/shard_map/mlp_forward/pallas_call | solution.py:789
  336.8 2.0 copy-done.22
  338.8 25.3 %mlp_backward.1 = (bf16[2048,2048]{1,0:T(8,128)(2,1)}, bf16[2048,1024]{1,0:T(8,128)(2,1)S(1)}, bf16[2048,2048]{1,0:T(8,128)(2,1)}, f32[8,1024]{1,0:T(8,128)S(1)}) custom-call(bf16[8,128,2048]{2,1,0:T(8,128)(2,1)} %bitcast.88, bf16[8,128,2048]{2,1,0:T(8,128)(2,1)} %bitcast.87, f32[2048,1024]{1,0:T(8,128)} %get-tuple-element.43.slope_ref, ...), custom_call_target="tpu_custom_call" | custom-call | flops 17179869184 | bytes 41943040 | tf_op jit(solution)/shard_map/mlp_backward/pallas_call | solution.py:846
  364.0 10.9 %convolution_convert_fusion.3 = bf16[2048,1024]{1,0:T(8,128)(2,1)} fusion(bf16[2048,2048]{1,0:T(8,128)(2,1)S(1)} %bitcast.86, bf16[2048,1024]{1,0:T(8,128)(2,1)S(1)} %get-tuple-element.47), kind=kOutput, calls=%fused_computation.5 | convolution fusion | flops 8592031744 | bytes 16777216 | tf_op jit(solution)/shard_map/dot_general | solution.py:944
  374.9 14.2 %convolution_convert_fusion.2 = bf16[1024,2048]{1,0:T(8,128)(2,1)} fusion(bf16[2048,1024]{1,0:T(8,128)(2,1)} %copy-done.22, bf16[2048,2048]{1,0:T(8,128)(2,1)} %get-tuple-element.46), kind=kOutput, calls=%fused_computation.4 | convolution fusion | flops 8592031744 | bytes 16777216 | tf_op jit(solution)/shard_map/dot_general | solution.py:941
  389.2 1.6 copy-done.2
  390.8 118.5 %shard_map.256 = (bf16[8,256,2048]{2,1,0:T(8,128)(2,1)}, f32[256,2048]{1,0:T(8,128)S(1)}, f32[4,8,2048]{2,1,0:T(8,128)S(1)}) custom-call(bf16[8,256,2048]{2,1,0:T(8,128)(2,1)} %bitcast.70, f32[256,2048]{1,0:T(8,128)S(1)} %copy-done.2, bf16[256,2048]{1,0:T(8,128)(2,1)S(1)} %copy-done.4, f32[1,2048]{1,0:T(1,128)S(1)} %bitcast.56), custom_call_target="tpu_custom_call" | custom-call | flops 419430400 | bytes 52428800 | tf_op jit(solution)/shard_map/pallas_call | solution.py:619
  509.3 1.3 copy-done.6
  510.6 0.7 copy-done.12
  511.3 6.7 convolution_convert_fusion.5
  518.0 6.1 convolution_convert_fusion.6.grad_ref
  524.2 27.9 %attention_backward.1 = bf16[2048,768]{1,0:T(8,128)(2,1)S(1)} custom-call(f32[4]{0:T(128)S(1)} %multiply_power_fusion.slope_ref, bf16[2048,768]{1,0:T(8,128)(2,1)} %copy-done.21, bf16[2048,256]{1,0:T(8,128)(2,1)S(1)} %convolution_convert_fusion.6.grad_ref, f32[4,2048]{1,0:T(4,128)S(1)} %get-tuple-element.51.lse_ref, s32[1,2048]{1,0:T(1,128)S(1)} %bitcast.60, ...), custom_call_target="tpu_custom_call" | custom-call | flops 4026531840 | bytes 7340032 | tf_op jit(solution)/shard_map/attention_backward/pallas_call | solution.py:182
  552.2 11.7 %convolution_convert_fusion.4 = bf16[2048,768]{0,1:T(8,128)(2,1)} fusion(bf16[2048,2048]{1,0:T(8,128)(2,1)} %bitcast.69, bf16[2048,768]{1,0:T(8,128)(2,1)S(1)} %attention_backward.1), kind=kOutput, calls=%fused_computation.6 | convolution fusion | flops 6444023808 | bytes 14680064 | tf_op jit(solution)/shard_map/dot_general | solution.py:971
  563.9 4.7 copy.33
  568.7 0.7 reduce-scatter.14.cloned.1.call-update
  569.4 0.5 reduce-scatter.12.cloned.1.call-update
  570.0 0.7 reduce-scatter.6.cloned.1.call-update
  570.7 2.4 convert_reduce_fusion
  573.2 0.6 pad.4.own_ref
  573.8 11.4 %convolution_convert_fusion = bf16[2048,2048]{1,0:T(8,128)(2,1)} fusion(bf16[2048,768]{1,0:T(8,128)(2,1)} %copy-done.5, bf16[2048,768]{0,1:T(8,128)(2,1)} %bitcast.90), kind=kOutput, calls=%fused_computation | convolution fusion | flops 6446645248 | bytes 14680064 | tf_op jit(solution)/shard_map/dot_general | solution.py:979
  585.2 79.6 %shard_map.257 = (f32[256,2048]{1,0:T(8,128)S(1)}, f32[2,8,2048]{2,1,0:T(8,128)S(1)}) custom-call(bf16[8,256,2048]{2,1,0:T(8,128)(2,1)} %bitcast.71, bf16[256,2048]{1,0:T(8,128)(2,1)S(1)} %copy-done, f32[256,2048]{1,0:T(8,128)S(1)} %copy-done.7, f32[1,2048]{1,0:T(1,128)S(1)} %bitcast.54), custom_call_target="tpu_custom_call" | custom-call | flops 419430400 | bytes 52428800 | tf_op jit(solution)/shard_map/pallas_call | solution.py:619
  664.8 1.3 copy-done.8
  666.1 0.7 copy-done.13
  666.8 15.1 %total_sums.1 = (f32[8,2048]{1,0:T(8,128)}, f32[8,256]{1,0:T(8,128)}) custom-call(f32[2,8,2048]{2,1,0:T(8,128)} %copy-done.13, f32[4,8,2048]{2,1,0:T(8,128)} %copy-done.12, f32[8,256]{1,0:T(8,128)} %pad.4.own_ref), custom_call_target="tpu_custom_call" | custom-call | tf_op jit(solution)/shard_map/total_sums/pallas_call | solution.py:738
  681.8 1.3 slice.50
  683.1 0.7 slice_bitcast_fusion
  683.8 0.6 copy.35
  684.4 1.7 fusion.1
  686.1 1.8 convert_element_type.63
  688.0 2.7 convert_element_type.62
  690.6 2.9 convert_element_type.65
  693.5 32.0 %reduce-scatter.12.cloned.1.call-done = bf16[512,1024]{1,0:T(8,128)(2,1)} async-done(((bf16[2048,1024]{1,0:T(8,128)(2,1)}), bf16[512,1024]{1,0:T(8,128)(2,1)}) %reduce-scatter.12.cloned.1.call-update) | async-done | bytes 1048592 | tf_op jit(solution)/shard_map/reduce_scatter | solution.py:877
  725.5 2.8 convert_element_type.64
  728.3 86.3 %reduce-scatter.6.cloned.1.call-done = bf16[256,2048]{1,0:T(8,128)(2,1)} async-done(((bf16[2048,2048]{1,0:T(8,128)(2,1)}), bf16[256,2048]{1,0:T(8,128)(2,1)}) %reduce-scatter.6.cloned.1.call-update) | async-done | bytes 1048592 | tf_op jit(solution)/shard_map/reduce_scatter | solution.py:950
  814.6 2.7 add_convert_fusion.1
  817.3 1.3 copy.37
  (80 shorter events, 1.7 us)
Async XLA Ops:
  7.2 4.7 copy-start.4
  7.2 6.3 copy-start.17
  7.2 7.7 copy-start
  7.2 7.7 copy-start.16
  7.2 7.7 copy-start.14
  7.2 78.6 %all-gather.9.cloned.1.call-start = ((), (), s32[]{:S(2)}) async-start(), calls=%async_computation.5 | async-start | bytes 3932160 | tf_op jit(solution)/shard_map/all_gather | solution.py:902
  9.7 109.0 %all-gather.11.cloned.1.call-start = ((), (), s32[]{:S(2)}) async-start(), calls=%async_computation.6 | async-start | bytes 1310720 | tf_op jit(solution)/shard_map/all_gather | solution.py:903
  10.5 299.4 %all-gather.13.cloned.1.call-start = ((), (), s32[]{:S(2)}) async-start(), calls=%async_computation.7 | async-start | bytes 5242880 | tf_op jit(solution)/shard_map/all_gather | solution.py:904
  11.2 298.7 %all-gather.15.cloned.1.call-start = ((), (), s32[]{:S(2)}) async-start(), calls=%async_computation.8 | async-start | bytes 5242880 | tf_op jit(solution)/shard_map/all_gather | solution.py:905
  11.8 327.0 %all-gather.19.cloned.1.call-start = ((), (), s32[]{:S(2)}) async-start(), calls=%async_computation.15 | async-start | bytes 4718592 | tf_op jit(solution)/shard_map/all_gather | solution.py:908
  12.9 325.9 %all-gather.17.cloned.1.call-start = ((), (), s32[]{:S(2)}) async-start(), calls=%async_computation.14 | async-start | bytes 4718592 | tf_op jit(solution)/shard_map/all_gather | solution.py:907
  13.5 672.7 %reduce-scatter.10.cloned.1.call-start = ((), (), s32[]{:S(2)}) async-start(), calls=%async_computation.11 | async-start | bytes 1310720 | tf_op jit(solution)/shard_map/reduce_scatter | solution.py:877
  14.9 70.9 %copy-start.24 = (f32[2,256]{1,0:T(2,128)S(1)}, f32[2,256]{1,0:T(2,128)}, u32[]{:S(2)}) copy-start(f32[2,256]{1,0:T(2,128)} %param.20) | copy-start | bytes 6148
  85.9 10.2 %copy-start.10 = (s32[2048,1]{1,0:T(8,128)S(1)}, s32[2048,1]{1,0:T(8,128)}, u32[]{:S(2)}) copy-start(s32[2048,1]{1,0:T(8,128)} %copy.31.seg_col_ref) | copy-start | bytes 24580
  117.0 1.7 copy-start.21
  118.7 6.9 copy-start.15
  118.7 6.9 copy-start.18
  118.7 6.9 copy-start.19
  125.6 184.3 %copy-start.20 = (f32[1024]{0:T(1024)S(1)}, f32[1024]{0:T(1024)}, u32[]{:S(2)}) copy-start(f32[1024]{0:T(1024)} %param.26) | copy-start | bytes 12292
  308.6 1.3 copy-start.1
  336.8 2.0 copy-start.22
  338.8 25.3 %copy-start.25 = (bf16[8,256,2048]{2,1,0:T(8,128)(2,1)S(1)}, bf16[8,256,2048]{2,1,0:T(8,128)(2,1)}, u32[]{:S(2)}) copy-start(bf16[8,256,2048]{2,1,0:T(8,128)(2,1)} %get-tuple-element.41) | copy-start | bytes 25165828
  389.2 1.6 copy-start.2
  509.3 1.3 copy-start.6
  510.6 0.7 copy-start.12
  518.0 6.2 copy-start.11
  524.2 163.8 %reduce-scatter.8.cloned.1.call-start = ((), (), s32[]{:S(2)}) async-start(), calls=%async_computation.10 | async-start | bytes 3932160 | tf_op jit(solution)/shard_map/reduce_scatter | solution.py:877
  552.2 11.7 %copy-start.5 = (bf16[2048,768]{1,0:T(8,128)(2,1)}, bf16[2048,768]{1,0:T(8,128)(2,1)S(1)}, u32[]{:S(2)}) copy-start(bf16[2048,768]{1,0:T(8,128)(2,1)S(1)} %attention_backward.1) | copy-start | bytes 9437188
  568.6 122.0 %reduce-scatter.14.cloned.1.call-start = ((), (), s32[]{:S(2)}) async-start(), calls=%async_computation.13 | async-start | bytes 5242880 | tf_op jit(solution)/shard_map/reduce_scatter | solution.py:877
  569.4 156.2 %reduce-scatter.12.cloned.1.call-start = ((), (), s32[]{:S(2)}) async-start(), calls=%async_computation.12 | async-start | bytes 5242880 | tf_op jit(solution)/shard_map/reduce_scatter | solution.py:877
  569.9 244.6 %reduce-scatter.6.cloned.1.call-start = ((), (), s32[]{:S(2)}) async-start(), calls=%async_computation.9 | async-start | bytes 9437184 | tf_op jit(solution)/shard_map/reduce_scatter | solution.py:950
  573.8 11.4 %copy-start.7 = (f32[256,2048]{1,0:T(8,128)S(1)}, f32[256,2048]{1,0:T(8,128)}, u32[]{:S(2)}) copy-start(f32[256,2048]{1,0:T(8,128)} %copy-done.6) | copy-start | bytes 6291460
  664.8 1.3 copy-start.8
  666.1 0.7 copy-start.13
  688.0 126.6 %copy-start.3 = (f32[256,2048]{1,0:T(8,128)S(1)}, f32[256,2048]{1,0:T(8,128)}, u32[]{:S(2)}) copy-start(f32[256,2048]{1,0:T(8,128)} %copy-done.1) | copy-start | bytes 6291460
  688.0 126.6 %copy-start.23 = (f32[2048]{0:T(1024)S(1)}, f32[2048]{0:T(1024)}, u32[]{:S(2)}) copy-start(f32[2048]{0:T(1024)} %param.28) | copy-start | bytes 24580
  814.6 2.7 copy-start.9
Sparse Core Ops, SparseCore 0:
  10.4 44.9 all-gather.8
  57.3 26.3 all-gather.10
  85.5 52.6 all-gather.12
  139.8 52.4 all-gather.14
  194.3 61.1 all-gather.18
  257.5 53.3 all-gather.16
  524.3 29.7 reduce-scatter.9
  568.7 45.7 reduce-scatter.7
  617.5 52.5 reduce-scatter.13
  672.9 52.5 reduce-scatter.11
  727.8 86.7 reduce-scatter.5

commit v2 on v1

--- a/solution.py
+++ b/solution.py
@@ -340,8 +340,8 @@
 
 
 class Reduce:
-    def __init__(self, line, partial, bufs, sems):
-        self.line, self.partial = line, partial
+    def __init__(self, line, partial, bufs, sems, product=None):
+        self.line, self.partial, self.product = line, partial, product
         self.held, self.paired, self.from_below, self.from_above = bufs
         self.held_sem, self.pair_send, self.pair_recv, self.line_send, self.line_recv = sems
 
@@ -366,8 +366,9 @@
 
     def across(self, chip, sub):
         rows = self.line.rows(sub)
+        block = chip if self.product is not None else 2 * chip + 1 - self.line.core
         return remote(
-            self.partial.at[2 * chip + 1 - self.line.core, rows],
+            self.partial.at[block, rows],
             self.paired.at[chip, rows],
             self.pair_send.at[chip, sub],
             self.pair_recv.at[chip, sub],
@@ -391,11 +392,13 @@
             chip = line.chips - 1 - step // 2 if step % 2 == 0 else step // 2
             order.append(chip)
 
-        @pl.loop(0, SUBS)
-        def _(sub):
-            for chip in order:
-                self.across(chip, sub).start()
-                self.load(chip, sub).start()
+        if self.product is None:
+
+            @pl.loop(0, SUBS)
+            def _(sub):
+                for chip in order:
+                    self.across(chip, sub).start()
+                    self.load(chip, sub).start()
 
         zeros = jnp.zeros((ROW_TILE, self.held.shape[2]), jnp.bfloat16)
 
@@ -406,6 +409,22 @@
 
         pl.when(jnp.logical_not(line.has_below))(lambda: clear(self.from_below, 0))
         pl.when(jnp.logical_not(line.has_above))(lambda: clear(self.from_above, line.chips - 1))
+
+    def multiply(self, slot):
+        line = self.line
+
+        @pl.when(slot < line.chips // 2)
+        def _():
+            chips = (line.chips - 1 - slot, slot)
+            for chip in chips:
+                self.product(2 * chip + 1 - line.core, self.partial, chip)
+
+                @pl.loop(0, SUBS)
+                def _(sub):
+                    self.across(chip, sub).start()
+
+            for chip in chips:
+                self.product(2 * chip + line.core, self.held, chip)
 
     def step(self, way, sub, step, live):
         line = self.line
@@ -415,7 +434,8 @@
 
         @pl.when(live & (chip > line.place if way == 0 else chip < line.place))
         def _():
-            self.load(chip, sub).wait()
+            if self.product is None:
+                self.load(chip, sub).wait()
             self.across(chip, sub).wait_recv()
 
             def add(with_arrived):
@@ -439,7 +459,8 @@
     def arrive(self, sub):
         line = self.line
         place = line.place
-        self.load(place, sub).wait()
+        if self.product is None:
+            self.load(place, sub).wait()
         self.across(place, sub).wait_recv()
         pl.when(line.has_below)(lambda: self.hop(0, place, sub).wait_recv())
         pl.when(line.has_above)(lambda: self.hop(1, place, sub).wait_recv())
@@ -484,14 +505,19 @@
     gather.finish()
 
 
-def run_line(line, reduce, gather, rows_done):
+def run_line(line, reduce, gather, rows_done, beside=None):
     steps = line.chips - 1
-    line.enter()
+    if beside is None:
+        line.enter()
     reduce.start()
     slots = steps * SUBS + LAG + (steps if gather is not None else 0) + 1
 
     @pl.loop(0, slots)
     def _(slot):
+        if reduce.product is not None:
+            reduce.multiply(slot)
+        if beside is not None:
+            beside(slot)
         for way in range(2):
             at = slot - (line.place if way == 0 else steps - line.place)
             sub = jnp.maximum(at, 0) // steps
@@ -550,10 +576,20 @@
 
 
 def branch_norm_gather_kernel(
-    chips, partial_ref, input_ref, bias_ref, gain_ref, shift_ref, whole_ref, residual_ref, normed_ref, *rest
+    chips, attended_ref, dense_ref, input_ref, bias_ref, gain_ref, shift_ref, whole_ref, residual_ref, normed_ref, mirror, *rest
 ):
     line = Line(chips, input_ref.shape[0])
-    reduce = Reduce(line, partial_ref, rest[:4], rest[4:9])
+    rows = input_ref.shape[0]
+    parts, _, part = dense_ref.shape
+
+    def product(block, target, slot):
+        source = attended_ref[pl.ds(pl.multiple_of(block * rows, rows), rows), :]
+        for index in range(parts):
+            target[slot, :, index * part : (index + 1) * part] = jnp.dot(
+                source, dense_ref[index], preferred_element_type=jnp.float32
+            ).astype(jnp.bfloat16)
+
+    reduce = Reduce(line, mirror, rest[:4], rest[4:9], product)
     gather = Gather(line, normed_ref, whole_ref, rest[9:])
 
     def rows_done(at):
@@ -589,41 +625,220 @@
     run_line(line, reduce, gather, rows_done)
 
 
-def grad_kernel(chips, partial_ref, input_ref, residual_grad_ref, gain_ref, out_ref, sums_ref, *rest):
+def grad_kernel(
+    chips, grad_cat_ref, weight_ref, input_ref, residual_grad_ref, gain_ref, early_ref, own_ref,
+    out_ref, early_out_ref, own_out_ref, late_ref, mirror, *rest
+):
     line = Line(chips, input_ref.shape[0])
-    reduce = Reduce(line, partial_ref, rest[:4], rest[4:9])
-    sums_ref[...] = jnp.zeros_like(sums_ref)
+    rows = input_ref.shape[0]
+    parts, three, part, head_width = weight_ref.shape
+
+    def product(block, target, slot):
+        at = pl.ds(pl.multiple_of(block * rows, rows), rows)
+        for index in range(parts):
+            total = None
+            for kind in range(three):
+                term = lax.dot_general(
+                    grad_cat_ref[at, kind * head_width : (kind + 1) * head_width],
+                    weight_ref[index, kind],
+                    NT,
+                    preferred_element_type=jnp.float32,
+                )
+                total = term if kind == 0 else total + term
+            target[slot, :, index * part : (index + 1) * part] = total.astype(jnp.bfloat16)
+
+    reduce = Reduce(line, mirror, rest[:4], rest[4:9], product)
+    sums = Sums(2 * chips, early_ref, own_ref, early_out_ref, own_out_ref, late_ref, rest[9:])
+    sums.late_sum[...] = jnp.zeros_like(sums.late_sum)
 
     def rows_done(at):
         unit, inv_std = unit_of(input_ref[at, :].astype(jnp.float32))
         grad = reduce.total(at)
         out_ref[at, :] = residual_grad_ref[at, :] + norm_back(grad, unit, inv_std, gain_ref[...])
-        sums_ref[0] += fold(grad * unit)
-        sums_ref[1] += fold(grad)
-
-    run_line(line, reduce, None, rows_done)
-
-
-def line_call(kernel, collective_id, operands, outs, gathers, reduces, rows, width):
-    chips = lax.axis_size("tensor") // 2
-    whole = jax.ShapeDtypeStruct((2 * chips, rows, width), jnp.bfloat16)
+        sums.late_sum[0] += fold(grad * unit)
+        sums.late_sum[1] += fold(grad)
+
+    sums.greet()
+    run_line(line, reduce, None, rows_done, sums.beside)
+    sums.close()
+
+
+class Sums:
+    def __init__(self, ranks, early_ref, own_ref, early_out, own_out, late_out, scratch):
+        self.ranks = ranks
+        self.groups = lax.axis_size("dp")
+        self.me = lax.axis_index("tensor")
+        self.group = lax.axis_index("dp")
+        self.early, self.own = early_ref, own_ref
+        self.early_out, self.own_out, self.late_out = early_out, own_out, late_out
+        (
+            self.late_sum, self.mine, self.first, self.stage, self.second,
+            self.late_mine, self.late_group, self.late_stage, self.late_all,
+        ) = scratch[:9]
+        self.sems = scratch[9:]
+        self.part = self.mine.shape[1] // ranks
+
+    @staticmethod
+    def scratch(ranks, groups, width):
+        part = width // ranks
+        f32 = jnp.float32
+        dma = pltpu.SemaphoreType.DMA
+        return [
+            pltpu.VMEM((2, 8, width), f32),
+            pltpu.VMEM((8, width), f32),
+            pltpu.VMEM((ranks, 8, part), f32),
+            pltpu.VMEM((16, part), f32),
+            pltpu.VMEM((groups, 16, part), f32),
+            pltpu.VMEM((8, width), f32),
+            pltpu.VMEM((groups, 8, width), f32),
+            pltpu.VMEM((8, width), f32),
+            pltpu.VMEM((ranks, 8, width), f32),
+        ] + [dma((ranks,)), dma((ranks,)), dma((groups,)), dma((groups,)), dma((ranks,)), dma((ranks,)),
+             dma((groups,)), dma((groups,)), dma((ranks,)), dma((ranks,))]
+
+    def rank(self, step):
+        return lax.rem(self.me + step, self.ranks)
+
+    def peer(self, step):
+        return lax.rem(self.group + step, self.groups)
+
+    def columns(self, rank):
+        return pl.ds(pl.multiple_of(rank * self.part, self.part), self.part)
+
+    def greet(self):
+        barrier = pltpu.get_barrier_semaphore()
+        for step in range(1, self.ranks):
+            pl.semaphore_signal(
+                barrier, inc=1, device_id={"tensor": self.rank(step)}, device_id_type=MESH
+            )
+        for step in range(1, self.groups):
+            pl.semaphore_signal(
+                barrier, inc=1, device_id={"dp": self.peer(step)}, device_id_type=MESH
+            )
+        pl.semaphore_wait(barrier, self.ranks + self.groups - 2)
+
+    def copy(self, stage, src, dst, sem, slot, axis, peer):
+        return pltpu.make_async_remote_copy(
+            src_ref=src,
+            dst_ref=dst,
+            send_sem=self.sems[2 * stage].at[sem],
+            recv_sem=self.sems[2 * stage + 1].at[slot],
+            device_id={axis: peer},
+            device_id_type=MESH,
+        )
+
+    def scatter(self, peer, slot, sem):
+        return self.copy(0, self.mine.at[:, self.columns(peer)], self.first.at[slot], sem, slot, "tensor", peer)
+
+    def exchange(self, peer, slot, sem):
+        return self.copy(1, self.stage, self.second.at[slot], sem, slot, "dp", peer)
+
+    def spread(self, peer, rank, sem):
+        return self.copy(
+            2, self.early_out.at[:, self.columns(self.me)], self.early_out.at[:, self.columns(rank)],
+            sem, rank, "tensor", peer,
+        )
+
+    def late_exchange(self, peer, slot, sem):
+        return self.copy(3, self.late_mine, self.late_group.at[slot], sem, slot, "dp", peer)
+
+    def late_spread(self, peer, slot, sem):
+        return self.copy(4, self.late_stage, self.late_all.at[slot], sem, slot, "tensor", peer)
+
+    def beside(self, slot):
+        @pl.when(slot == 1)
+        def _():
+            self.mine[...] = jnp.zeros_like(self.mine)
+            for row in range(self.early.shape[0]):
+                self.mine[row : row + 1, :] = jnp.sum(self.early[row], axis=0, keepdims=True)
+            for step in range(1, self.ranks):
+                self.scatter(self.rank(step), self.me, step).start()
+            self.first[self.me] = self.mine[:, self.columns(self.me)]
+
+        @pl.when(slot == 4)
+        def _():
+            for step in range(1, self.ranks):
+                self.scatter(self.rank(step), self.rank(step), step).wait_recv()
+            total = self.first[0]
+            for rank in range(1, self.ranks):
+                total = total + self.first[rank]
+            self.stage[:8, :] = total
+            self.stage[8:, :] = self.own[...]
+            for step in range(1, self.groups):
+                self.exchange(self.peer(step), self.group, step).start()
+            self.second[self.group] = self.stage[...]
+
+        @pl.when(slot == 7)
+        def _():
+            for step in range(1, self.groups):
+                self.exchange(self.peer(step), self.peer(step), step).wait_recv()
+            total = self.second[0]
+            for index in range(1, self.groups):
+                total = total + self.second[index]
+            self.early_out[:, self.columns(self.me)] = total[:8]
+            self.own_out[...] = total[8:]
+            for step in range(1, self.ranks):
+                self.spread(self.rank(step), self.me, step).start()
+
+    def close(self):
+        self.late_mine[...] = jnp.zeros_like(self.late_mine)
+        for row in range(2):
+            self.late_mine[row : row + 1, :] = jnp.sum(self.late_sum[row], axis=0, keepdims=True)
+        for step in range(1, self.groups):
+            self.late_exchange(self.peer(step), self.group, step).start()
+        self.late_group[self.group] = self.late_mine[...]
+        for step in range(1, self.groups):
+            self.late_exchange(self.peer(step), self.peer(step), step).wait_recv()
+        total = self.late_group[0]
+        for index in range(1, self.groups):
+            total = total + self.late_group[index]
+        self.late_stage[...] = total
+        for step in range(1, self.ranks):
+            self.late_spread(self.rank(step), self.me, step).start()
+        self.late_all[self.me] = total
+        for step in range(1, self.ranks):
+            self.spread(self.rank(step), self.rank(step), step).wait_recv()
+        for step in range(1, self.ranks):
+            self.late_spread(self.rank(step), self.rank(step), step).wait_recv()
+        total = self.late_all[0]
+        for rank in range(1, self.ranks):
+            total = total + self.late_all[rank]
+        self.late_out[...] = total
+        for step in range(1, self.ranks):
+            self.scatter(self.rank(step), self.me, step).wait_send()
+            self.spread(self.rank(step), self.me, step).wait_send()
+            self.late_spread(self.rank(step), self.me, step).wait_send()
+        for step in range(1, self.groups):
+            self.exchange(self.peer(step), self.group, step).wait_send()
+            self.late_exchange(self.peer(step), self.group, step).wait_send()
+
+
+def line_call(kernel, collective_id, operands, outs, rows, width, gathers=True, reduces=True, product=False, sums=False):
+    ranks = lax.axis_size("tensor")
+    chips = ranks // 2
+    whole = jax.ShapeDtypeStruct((ranks, rows, width), jnp.bfloat16)
     in_vmem = pl.BlockSpec(memory_space=pltpu.VMEM)
     in_place = pl.BlockSpec(memory_space=pl.ANY)
+    streamed = int(reduces and not product)
     scratch = []
     if gathers:
         scratch.append(pltpu.VMEM((rows, width), jnp.bfloat16))
+    if product:
+        scratch.append(pltpu.VMEM((chips, rows, width), jnp.bfloat16))
     if reduces:
         scratch += Reduce.scratch(chips, rows, width)
     if gathers:
         scratch += Gather.scratch(chips)
+    if sums:
+        scratch += Sums.scratch(ranks, lax.axis_size("dp"), width)
     return pl.pallas_call(
         functools.partial(kernel, chips),
-        in_specs=([in_place] if reduces else []) + [in_vmem] * (len(operands) - int(reduces)),
+        in_specs=[in_place] * streamed + [in_vmem] * (len(operands) - streamed),
         out_specs=([in_place] if gathers else []) + [in_vmem] * len(outs),
         out_shape=([whole] if gathers else []) + list(outs),
         scratch_shapes=scratch,
         compiler_params=pltpu.CompilerParams(
-            collective_id=collective_id, has_side_effects=True, vmem_limit_bytes=48 * 2**20
+            collective_id=collective_id, has_side_effects=True, vmem_limit_bytes=52 * 2**20
         ),
         cost_estimate=pl.CostEstimate(
             flops=8 * rows * width * 100, bytes_accessed=100 * rows * width, transcendentals=0
@@ -631,139 +846,189 @@
     )(*operands)
 
 
-def total_kernel(ranks, groups, late_ref, early_ref, own_ref, all_ref, dp_ref, mine, first, stage, second, sems):
-    send1, recv1, send2, recv2, send3, recv3 = sems
-    me = lax.axis_index("tensor")
-    group = lax.axis_index("dp")
-    part = mine.shape[1] // ranks
-    barrier = pltpu.get_barrier_semaphore()
-    for step in range(1, ranks):
-        pl.semaphore_signal(
-            barrier, inc=1, device_id={"tensor": lax.rem(me + step, ranks)}, device_id_type=MESH
+def qkv_grad_kernel(rows_ref, grad_ref, out_ref, sums_ref):
+    head_width = out_ref.shape[2]
+
+    @pl.when(pl.program_id(0) == 0)
+    def _():
+        for kind in range(3):
+            cols = slice(kind * head_width, (kind + 1) * head_width)
+            sums_ref[kind] = jnp.sum(
+                grad_ref[:, cols].astype(jnp.float32).reshape(-1, 8, head_width), axis=0
+            )
+
+    product = lax.dot_general(
+        rows_ref[...], grad_ref[...], (((0,), (0,)), ((), ())), preferred_element_type=jnp.float32
+    )
+    for kind in range(3):
+        out_ref[kind] = product[:, kind * head_width : (kind + 1) * head_width].astype(jnp.bfloat16)
+
+
+def qkv_weight_grad(whole, grad_cat):
+    tokens, width = whole.shape
+    head_width = grad_cat.shape[1] // 3
+    block = 256
+    return pl.pallas_call(
+        qkv_grad_kernel,
+        grid=(width // block,),
+        in_specs=[
+            pl.BlockSpec((tokens, block), lambda i: (0, i)),
+            pl.BlockSpec(grad_cat.shape, lambda i: (0, 0)),
+        ],
+        out_specs=[
+            pl.BlockSpec((3, block, head_width), lambda i: (0, i, 0)),
+            pl.BlockSpec((3, 8, head_width), lambda i: (0, 0, 0)),
+        ],
+        out_shape=[
+            jax.ShapeDtypeStruct((3, width, head_width), jnp.bfloat16),
+            jax.ShapeDtypeStruct((3, 8, head_width), jnp.float32),
+        ],
+        compiler_params=pltpu.CompilerParams(vmem_limit_bytes=40 * 2**20),
+        cost_estimate=pl.CostEstimate(
+            flops=6 * tokens * width * head_width, bytes_accessed=4 * tokens * width, transcendentals=0
+        ),
+        name="qkv_weight_grad",
+    )(whole, grad_cat)
+
+
+def finish_kernel(down_ref, up_ref, dense_ref, qkv_ref, one_ref, two_ref, residual_ref, bias_ref, grad_ref,
+                  down_out, up_out, dense_out, qkv_out, rows_out, grad_out):
+    down_out[...] = down_ref[...].astype(jnp.float32)
+    up_out[...] = up_ref[...].astype(jnp.float32)
+    dense_out[...] = dense_ref[...].astype(jnp.float32)
+    qkv_out[...] = qkv_ref[...].astype(jnp.float32)
+    half = pl.program_id(0) < pl.num_programs(0) // 2
+    branch = jnp.where(half, one_ref[...], two_ref[...]).astype(jnp.float32) + bias_ref[...]
+    rows_out[...] = (residual_ref[...] + branch).astype(jnp.bfloat16)
+    grad_out[...] = grad_ref[...]
+
+
+def finish(down, up, dense, qkv, one, two, residual, bias, input_grad):
+    steps = 4
+
+    def split(shape):
+        if len(shape) == 3:
+            return pl.BlockSpec((shape[0], shape[1] // steps, shape[2]), lambda i: (0, i, 0))
+        return pl.BlockSpec((shape[0] // steps, shape[1]), lambda i: (i, 0))
+
+    operands = (down, up, dense, qkv, one, two, residual, bias[None], input_grad)
+    specs = [split(item.shape) for item in operands]
+    row_part = (residual.shape[0] // steps, residual.shape[1])
+    specs[4] = pl.BlockSpec(row_part, lambda i: (jnp.minimum(i, steps // 2 - 1), 0))
+    specs[5] = pl.BlockSpec(row_part, lambda i: (jnp.maximum(i - steps // 2, 0), 0))
+    specs[7] = pl.BlockSpec((1, bias.shape[0]), lambda i: (0, 0))
+    outs = [jax.ShapeDtypeStruct(item.shape, jnp.float32) for item in (down, up, dense, qkv)]
+    outs.append(jax.ShapeDtypeStruct(residual.shape, jnp.bfloat16))
+    outs.append(jax.ShapeDtypeStruct(input_grad.shape, jnp.float32))
+    return pl.pallas_call(
+        finish_kernel,
+        grid=(steps,),
+        in_specs=specs,
+        out_specs=[split(item.shape) for item in outs],
+        out_shape=outs,
+        compiler_params=pltpu.CompilerParams(vmem_limit_bytes=32 * 2**20),
+        name="finish",
+    )(*operands)
+
+
+def dense_backward_kernel(branch_ref, attended_ref, dense_ref, grad_ref, weight_ref, total):
+    parts, _, part = dense_ref.shape
+    block = pl.program_id(0)
+
+    @pl.when(block == 0)
+    def _():
+        total[...] = jnp.zeros_like(total)
+
+    back = None
+    for index in range(parts):
+        cols = slice(index * part, (index + 1) * part)
+        term = lax.dot_general(
+            branch_ref[:, cols], dense_ref[index], NT, preferred_element_type=jnp.float32
         )
-    for step in range(1, groups):
-        pl.semaphore_signal(
-            barrier, inc=1, device_id={"dp": lax.rem(group + step, groups)}, device_id_type=MESH
-        )
-    mine[...] = jnp.zeros_like(mine)
-    for row in range(late_ref.shape[0]):
-        mine[row : row + 1, :] = jnp.sum(late_ref[row], axis=0, keepdims=True)
-    for row in range(early_ref.shape[0]):
-        at = late_ref.shape[0] + row
-        mine[at : at + 1, :] = jnp.sum(early_ref[row], axis=0, keepdims=True)
-    pl.semaphore_wait(barrier, ranks + groups - 2)
-
-    def columns(rank):
-        return pl.ds(pl.multiple_of(rank * part, part), part)
-
-    def scatter(peer, slot, sem):
-        return pltpu.make_async_remote_copy(
-            src_ref=mine.at[:, columns(peer)],
-            dst_ref=first.at[slot],
-            send_sem=send1.at[sem],
-            recv_sem=recv1.at[slot],
-            device_id={"tensor": peer},
-            device_id_type=MESH,
-        )
-
-    def exchange(peer, slot, sem):
-        return pltpu.make_async_remote_copy(
-            src_ref=stage,
-            dst_ref=second.at[slot],
-            send_sem=send2.at[sem],
-            recv_sem=recv2.at[slot],
-            device_id={"dp": peer},
-            device_id_type=MESH,
-        )
-
-    def spread(peer, rank, sem):
-        return pltpu.make_async_remote_copy(
-            src_ref=all_ref.at[:, columns(me)],
-            dst_ref=all_ref.at[:, columns(rank)],
-            send_sem=send3.at[sem],
-            recv_sem=recv3.at[rank],
-            device_id={"tensor": peer},
-            device_id_type=MESH,
-        )
-
-    for step in range(1, ranks):
-        scatter(lax.rem(me + step, ranks), me, step).start()
-    first[me] = mine[:, columns(me)]
-    for step in range(1, ranks):
-        other = lax.rem(me + step, ranks)
-        scatter(other, other, step).wait_recv()
-    rows = mine.shape[0]
-    total = first[0]
-    for rank in range(1, ranks):
-        total = total + first[rank]
-    stage[:rows, :] = total
-    stage[rows:, :] = own_ref[...]
-    for step in range(1, groups):
-        exchange(lax.rem(group + step, groups), group, step).start()
-    second[group] = stage[...]
-    for step in range(1, groups):
-        other = lax.rem(group + step, groups)
-        exchange(other, other, step).wait_recv()
-    total = second[0]
-    for index in range(1, groups):
-        total = total + second[index]
-    all_ref[:, columns(me)] = total[:rows]
-    dp_ref[...] = total[rows:]
-    for step in range(1, ranks):
-        spread(lax.rem(me + step, ranks), me, step).start()
-    for step in range(1, ranks):
-        other = lax.rem(me + step, ranks)
-        spread(other, other, step).wait_recv()
-    for step in range(1, ranks):
-        other = lax.rem(me + step, ranks)
-        scatter(other, me, step).wait_send()
-        spread(other, me, step).wait_send()
-    for step in range(1, groups):
-        exchange(lax.rem(group + step, groups), group, step).wait_send()
-
-
-def total_call(late, early, own):
-    ranks = lax.axis_size("tensor")
-    groups = lax.axis_size("dp")
-    width = late.shape[2]
-    part = width // ranks
-    dma = pltpu.SemaphoreType.DMA
-
-    def kernel(late_ref, early_ref, own_ref, all_ref, dp_ref, mine, first, stage, second, *sems):
-        total_kernel(
-            ranks, groups, late_ref, early_ref, own_ref, all_ref, dp_ref, mine, first, stage, second, sems
-        )
-
-    in_vmem = pl.BlockSpec(memory_space=pltpu.VMEM)
+        back = term if index == 0 else back + term
+    grad_ref[...] = back.astype(jnp.bfloat16)
+    total[...] += lax.dot_general(
+        attended_ref[...], branch_ref[...], (((0,), (0,)), ((), ())), preferred_element_type=jnp.float32
+    )
+
+    @pl.when(block == pl.num_programs(0) - 1)
+    def _():
+        weight_ref[...] = total[...].astype(jnp.bfloat16)
+
+
+def dense_backward(branch, attended, dense_all):
+    tokens, width = branch.shape
+    head_width = attended.shape[1]
+    block = min(512, tokens)
     return pl.pallas_call(
-        kernel,
-        in_specs=[in_vmem] * 3,
-        out_specs=[in_vmem] * 2,
+        dense_backward_kernel,
+        grid=(tokens // block,),
+        in_specs=[
+            pl.BlockSpec((block, width), lambda i: (i, 0)),
+            pl.BlockSpec((block, head_width), lambda i: (i, 0)),
+            pl.BlockSpec(dense_all.shape, lambda i: (0, 0, 0)),
+        ],
+        out_specs=[
+            pl.BlockSpec((block, head_width), lambda i: (i, 0)),
+            pl.BlockSpec((head_width, width), lambda i: (0, 0)),
+        ],
         out_shape=[
-            jax.ShapeDtypeStruct((8, width), jnp.float32),
-            jax.ShapeDtypeStruct((8, part), jnp.float32),
-        ],
-        scratch_shapes=[
-            pltpu.VMEM((8, width), jnp.float32),
-            pltpu.VMEM((ranks, 8, part), jnp.float32),
-            pltpu.VMEM((16, part), jnp.float32),
-            pltpu.VMEM((groups, 16, part), jnp.float32),
-            dma((ranks,)),
-            dma((ranks,)),
-            dma((groups,)),
-            dma((groups,)),
-            dma((ranks,)),
-            dma((ranks,)),
-        ],
-        compiler_params=pltpu.CompilerParams(collective_id=5, has_side_effects=True),
-        name="total_sums",
-    )(late, early, own)
+            jax.ShapeDtypeStruct((tokens, head_width), jnp.bfloat16),
+            jax.ShapeDtypeStruct((head_width, width), jnp.bfloat16),
+        ],
+        scratch_shapes=[pltpu.VMEM((head_width, width), jnp.float32)],
+        compiler_params=pltpu.CompilerParams(vmem_limit_bytes=40 * 2**20),
+        cost_estimate=pl.CostEstimate(
+            flops=4 * tokens * width * head_width, bytes_accessed=2 * tokens * width, transcendentals=0
+        ),
+        name="dense_backward",
+    )(branch, attended, dense_all)
+
+
+def project_kernel(rows_ref, weight_ref, bias_ref, out_ref):
+    parts, three, part, head_width = weight_ref.shape
+    for kind in range(three):
+        total = None
+        for index in range(parts):
+            term = jnp.dot(
+                rows_ref[:, index * part : (index + 1) * part],
+                weight_ref[index, kind],
+                preferred_element_type=jnp.float32,
+            )
+            total = term if index == 0 else total + term
+        cols = slice(kind * head_width, (kind + 1) * head_width)
+        out_ref[:, cols] = (total + bias_ref[:, cols]).astype(jnp.bfloat16)
+
+
+def project(whole, qkv_all, query_value_bias):
+    tokens, width = whole.shape
+    head_width = qkv_all.shape[3]
+    bias = jnp.concatenate(
+        [query_value_bias[0], jnp.zeros_like(query_value_bias[0]), query_value_bias[1]]
+    )[None]
+    block = min(512, tokens)
+    return pl.pallas_call(
+        project_kernel,
+        grid=(tokens // block,),
+        in_specs=[
+            pl.BlockSpec((block, width), lambda i: (i, 0)),
+            pl.BlockSpec(qkv_all.shape, lambda i: (0, 0, 0, 0)),
+            pl.BlockSpec((1, 3 * head_width), lambda i: (0, 0)),
+        ],
+        out_specs=pl.BlockSpec((block, 3 * head_width), lambda i: (i, 0)),
+        out_shape=jax.ShapeDtypeStruct((tokens, 3 * head_width), jnp.bfloat16),
+        compiler_params=pltpu.CompilerParams(vmem_limit_bytes=40 * 2**20),
+        cost_estimate=pl.CostEstimate(
+            flops=6 * tokens * width * head_width, bytes_accessed=2 * tokens * width, transcendentals=0
+        ),
+        name="project",
+    )(whole, qkv_all, bias)
 
 
 MLP_TILE = 256
 
 
-def mlp_forward_kernel(rows_ref, up_ref, bias_ref, down_ref, active_ref, slope_ref, out_ref):
+def mlp_forward_kernel(rows_ref, up_ref, bias_ref, down_ref, active_ref, slope_ref, one_ref, two_ref):
     width = up_ref.shape[1]
     for first in range(0, width, MLP_TILE):
         cols = slice(first, first + MLP_TILE)
@@ -773,19 +1038,21 @@
         density = jnp.exp(-0.5 * value * value) * (1.0 / math.sqrt(2.0 * math.pi))
         slope_ref[:, cols] = below + value * density
         active_ref[:, cols] = (value * below).astype(jnp.bfloat16)
-    out_ref[...] = jnp.dot(
+    branch = jnp.dot(
         active_ref[...], down_ref[...], preferred_element_type=jnp.float32
     ).astype(jnp.bfloat16)
+    half = one_ref.shape[0]
+    one_ref[...] = branch[:half]
+    two_ref[...] = branch[half:]
 
 
 def resident(shape):
     return pl.BlockSpec(shape, lambda i: (0,) * len(shape), pipeline_mode=pl.Buffered(1))
 
 
-def mlp_forward(rows, up_full, up_bias, down_full):
+def mlp_forward(rows, block, up_full, up_bias, down_full):
     tokens, width = rows.shape
     hidden = up_full.shape[1]
-    block = min(256, tokens)
     return pl.pallas_call(
         mlp_forward_kernel,
         grid=(tokens // block,),
@@ -798,12 +1065,14 @@
         out_specs=[
             pl.BlockSpec((block, hidden), lambda i: (i, 0)),
             pl.BlockSpec((block, hidden), lambda i: (i, 0)),
-            pl.BlockSpec((block, width), lambda i: (i, 0)),
+            pl.BlockSpec((block // 2, width), lambda i: (i, 0)),
+            pl.BlockSpec((block // 2, width), lambda i: (i, 0)),
         ],
         out_shape=[
             jax.ShapeDtypeStruct((tokens, hidden), jnp.bfloat16),
             jax.ShapeDtypeStruct((tokens, hidden), jnp.float32),
-            jax.ShapeDtypeStruct((tokens, width), jnp.bfloat16),
+            jax.ShapeDtypeStruct((tokens // 2, width), jnp.bfloat16),
+            jax.ShapeDtypeStruct((tokens // 2, width), jnp.bfloat16),
         ],
         compiler_params=pltpu.CompilerParams(vmem_limit_bytes=48 * 2**20),
         cost_estimate=pl.CostEstimate(
@@ -874,7 +1143,7 @@
 
 
 def over_dp(grad, dimension):
-    return lax.psum_scatter(grad, "dp", scatter_dimension=dimension, tiled=True).astype(jnp.float32)
+    return lax.psum_scatter(grad, "dp", scatter_dimension=dimension, tiled=True)
 
 
 def layer(
@@ -899,41 +1168,34 @@
     tokens = ranks * rows
     f32_rows = jax.ShapeDtypeStruct((rows, width), jnp.float32)
 
-    qkv_full = lax.all_gather(qkv_weight, "dp", axis=1, tiled=True)
-    dense_full = lax.all_gather(dense_weight, "dp", axis=1, tiled=True)
+    qkv_all = lax.all_gather(qkv_weight, "dp", axis=0, tiled=False)
+    dense_all = lax.all_gather(dense_weight, "dp", axis=0, tiled=False)
     up_full = lax.all_gather(up_weight, "dp", axis=0, tiled=True)
     down_full = lax.all_gather(down_weight, "dp", axis=1, tiled=True)
     half = rows // 2
     out_one = lax.all_gather(out_grad[:half], "tensor", axis=0, tiled=False)
     out_two = lax.all_gather(out_grad[half:], "tensor", axis=0, tiled=False)
 
-    head_width = qkv_full.shape[2]
+    head_width = qkv_all.shape[3]
     up_width = up_bias.shape[0]
-    qkv_cat = jnp.transpose(qkv_full, (1, 0, 2)).reshape(width, 3 * head_width)
-
     (whole1,) = line_call(
         norm_gather_kernel, 1,
-        (layer_input, first_gain[None], first_shift[None]), (), True, False, rows, width,
+        (layer_input, first_gain[None], first_shift[None]), (), rows, width, reduces=False,
     )
     whole1 = whole1.reshape(tokens, width)
-    zero_bias = jnp.zeros_like(query_value_bias[0])
-    bias_cat = jnp.concatenate([query_value_bias[0], zero_bias, query_value_bias[1]])
-    projected = (jnp.dot(whole1, qkv_cat, preferred_element_type=jnp.float32) + bias_cat).astype(
-        jnp.bfloat16
-    )
+    projected = project(whole1, qkv_all, query_value_bias)
     head_count = head_width // HEAD_DIM
     tensor_pos = lax.axis_index("tensor")
     global_heads = tensor_pos * head_count + jnp.arange(head_count, dtype=jnp.int32)
     slopes = jnp.power(2.0, -8.0 * (global_heads + 1).astype(jnp.float32) / HEADS)
     attended, log_sums = attention_forward(projected, segment_ids, slopes)
-    attn_part = jnp.dot(attended, dense_full, preferred_element_type=jnp.float32).astype(jnp.bfloat16)
     whole2, residual = line_call(
         branch_norm_gather_kernel, 2,
-        (attn_part.reshape(ranks, rows, width), layer_input, dense_bias[None], second_gain[None], second_shift[None]),
-        (f32_rows,), True, True, rows, width,
+        (attended, dense_all, layer_input, dense_bias[None], second_gain[None], second_shift[None]),
+        (f32_rows,), rows, width, product=True,
     )
     whole2 = whole2.reshape(tokens, width)
-    activated, slope, mlp_part = mlp_forward(whole2, up_full, up_bias, down_full)
+    activated, slope, mlp_one, mlp_two = mlp_forward(whole2, rows, up_full, up_bias, down_full)
     out_whole, pre_grad, normed2_part, up_bias_sums = mlp_backward(
         out_one, out_two, slope, down_full, up_full
     )
@@ -947,64 +1209,53 @@
     normed2_part, down_grad, up_grad = lax.optimization_barrier((normed2_part, down_grad, up_grad))
     down_wgrad = over_dp(down_grad, 1)
     up_wgrad = over_dp(up_grad, 0)
-    mlp_rows = lax.psum_scatter(mlp_part, "tensor", scatter_dimension=0, tiled=True)
-    mlp_branch = mlp_rows.astype(jnp.float32) + down_bias
-    layer_out = (residual + mlp_branch).astype(jnp.bfloat16)
+    mlp_rows_one = lax.psum_scatter(mlp_one, "tensor", scatter_dimension=0, tiled=True)
+    mlp_rows_two = lax.psum_scatter(mlp_two, "tensor", scatter_dimension=0, tiled=True)
 
     branch_whole, residual_grad, second_sums = line_call(
         grad_gather_kernel, 3,
         (normed2_part.reshape(ranks, rows, width), residual, out_grad, second_gain[None]),
-        (f32_rows, jax.ShapeDtypeStruct((4, 8, width), jnp.float32)), True, True, rows, width,
+        (f32_rows, jax.ShapeDtypeStruct((4, 8, width), jnp.float32)), rows, width,
     )
     branch_whole = branch_whole.reshape(tokens, width)
-    attended_grad = lax.dot_general(
-        branch_whole, dense_full, (((1,), (1,)), ((), ())), preferred_element_type=jnp.float32
-    ).astype(jnp.bfloat16)
-    dense_grad = lax.dot_general(
-        attended, branch_whole, (((0,), (0,)), ((), ())), preferred_element_type=jnp.float32
-    ).astype(jnp.bfloat16)
-    attended_grad, dense_grad = lax.optimization_barrier((attended_grad, dense_grad))
+    attended_grad, dense_grad = dense_backward(branch_whole, attended, dense_all)
     qkv_grad_cat = attention_backward(projected, attended_grad, segment_ids, slopes, log_sums)
     dense_wgrad = over_dp(dense_grad, 1)
-    qkv_sums = jnp.sum(qkv_grad_cat.astype(jnp.float32), axis=0)
-    bias_part = jnp.stack([qkv_sums[:head_width], qkv_sums[2 * head_width :]])
-    qkv_grad_flat = lax.dot_general(
-        whole1, qkv_grad_cat, (((0,), (0,)), ((), ())), preferred_element_type=jnp.float32
-    )
-    qkv_grad = jnp.transpose(
-        qkv_grad_flat.astype(jnp.bfloat16).reshape(width, 3, head_width), (1, 0, 2)
-    )
+    qkv_grad, qkv_sums = qkv_weight_grad(whole1, qkv_grad_cat)
     qkv_grad, qkv_grad_cat = lax.optimization_barrier((qkv_grad, qkv_grad_cat))
     qkv_wgrad = over_dp(qkv_grad, 1)
-    normed1_part = lax.dot_general(
-        qkv_grad_cat, qkv_cat, (((1,), (1,)), ((), ())), preferred_element_type=jnp.float32
-    ).astype(jnp.bfloat16)
-    input_grad, first_sums = line_call(
+    qkv_sums = jnp.sum(qkv_sums, axis=1)
+    part = width // ranks
+    bias_rows = 2 * head_width // part
+    up_rows = up_width // part
+    own = jnp.concatenate([qkv_sums[0], qkv_sums[2], up_bias_part]).reshape(-1, part)
+    own = jnp.pad(own, ((0, 8 - own.shape[0]), (0, 0)))
+    f32_sums = jax.ShapeDtypeStruct((8, width), jnp.float32)
+    input_grad, early, own, late = line_call(
         grad_kernel, 4,
-        (normed1_part.reshape(ranks, rows, width), layer_input, residual_grad, first_gain[None]),
-        (f32_rows, jax.ShapeDtypeStruct((2, 8, width), jnp.float32)), False, True, rows, width,
-    )
-    part = width // ranks
-    own = jnp.concatenate([bias_part.reshape(-1), up_bias_part]).reshape(-1, part)
-    bias_rows = 2 * head_width // part
-    own = jnp.pad(own, ((0, 8 - own.shape[0]), (0, 0)))
-    sums, own = total_call(first_sums, second_sums, own)
-    up_rows = up_width // part
+        (qkv_grad_cat, qkv_all, layer_input, residual_grad, first_gain[None], second_sums, own),
+        (f32_rows, f32_sums, jax.ShapeDtypeStruct((8, part), jnp.float32), f32_sums),
+        rows, width, gathers=False, product=True, sums=True,
+    )
+    down_wgrad, up_wgrad, dense_wgrad, qkv_wgrad, layer_out, input_grad = finish(
+        down_wgrad, up_wgrad, dense_wgrad, qkv_wgrad,
+        mlp_rows_one, mlp_rows_two, residual, down_bias, input_grad,
+    )
     return (
         layer_out,
         input_grad,
-        sums[0],
-        sums[1],
+        late[0],
+        late[1],
         qkv_wgrad,
         own[:bias_rows].reshape(2, head_width),
         dense_wgrad,
-        sums[4],
-        sums[2],
-        sums[3],
+        early[2],
+        early[0],
+        early[1],
         up_wgrad,
         own[bias_rows : bias_rows + up_rows].reshape(up_width),
         down_wgrad,
-        sums[5],
+        early[3],
     )
 
 

time: 837 us -> 863 us (1.031); the launches traced: 825 us -> 860 us
  Pallas kernels: 568 us -> 638 us
  matrix products: 78.2 us -> 24.7 us
  waiting for transfers between devices: 123 us -> 158 us
  other arithmetic: 15.3 us -> 0.06 us
    pallas_call x5 -> x8, Pallas kernels: 467 us -> 538 us  [the longest x4 506 us: line_call(): pl.pallas_call(functools.partial(kernel, chips), in_specs=[in_place] * st...]
    dot_general x6 -> x0, matrix products: 53 us -> none  [the longest x1 11.7 us: layer(): lax.dot_general(whole1, qkv_grad_cat, (((0,), (0,)), ((), ())), preferred...]
    reduce_scatter x5 -> x6, waiting for transfers between devices: 118 us -> 152 us  [the longest x4 113 us: over_dp(): return lax.psum_scatter(grad, 'dp', scatter_dimension=dimension, tiled=True)]
    convert_element_type x5 -> x0, other arithmetic: 12.8 us -> none  [the longest x4 10.1 us: over_dp(): lax.psum_scatter(grad, 'dp', scatter_dimension=dimension, tiled=True)]
    unnamed x57 -> x60, local copies, waits for them, and re-layouts: 15.6 us -> 20 us
  transfers between devices with their start and end apart: 11 -> 12, of which waited for: 2 -> 3; matrix products, arithmetic and copies ran while one was open for 8% -> 1% of each run, Pallas kernels for 51% -> 56%
where the time goes in v2:
time: 863 us; the launch traced here: 860 us
  Pallas kernels  638 us (74%)
  waiting for transfers between devices  158 us (18%)
  matrix products  24.7 us (3%)
  local copies, waits for them, and re-layouts  23.9 us (3%)
  between operations  14.6 us (2%)
    pallas_call x4, Pallas kernels, line_call(): pl.pallas_call(functools.partial(kernel, chips), in_specs=[in_place] * st...  506 us
    reduce_scatter x4, waiting for transfers between devices, over_dp(): return lax.psum_scatter(grad, 'dp', scatter_dimension=dimension, tiled=True)  113 us
    reduce_scatter x1, waiting for transfers between devices, layer(): lax.psum_scatter(mlp_two, 'tensor', scatter_dimension=0, tiled=True)  39.2 us
    pallas_call x1, Pallas kernels, attention_backward(): pl.pallas_call(backward_kernel, grid=(seq_len // Q_BLOCK,), in_specs=[pl....  27.1 us
    pallas_call x1, Pallas kernels, mlp_forward(): pl.pallas_call(mlp_forward_kernel, grid=(tokens // block,), in_specs=[pl....  26.8 us
    pallas_call x1, Pallas kernels, mlp_backward(): pl.pallas_call(mlp_backward_kernel, grid=(ranks,), in_specs=[pl.BlockSpec...  25.3 us
    pallas_call x1, Pallas kernels, attention_forward(): pl.pallas_call(forward_kernel, grid=(seq_len // Q_BLOCK,), in_specs=[pl.B...  20.9 us
    unnamed x60, local copies, waits for them, and re-layouts  20 us
  transfers between devices with their start and end apart: 12, of which 3 were waited for; matrix products, arithmetic and copies ran while one was open for 1% of the time, Pallas kernels for 56%

profile of v2, /device:TPU:8, one launch (start us, length us, event | category | flops | bytes accessed | tf_op | source)
XLA Modules:
  0.0 860.1 jit_solution(4618135803012476273)
XLA Ops:
  7.3 0.7 all-gather.19.cloned.1.call-update
  8.0 0.7 all-gather.21.cloned.1.call-update
  8.8 0.7 all-gather.11.cloned.1.call-update
  9.5 0.5 all-gather.13.cloned.1.call-update
  10.1 2.3 fusion
  12.4 0.0 all-gather.15.cloned.1.call-start
  12.4 0.5 all-gather.15.cloned.1.call-update
  13.1 0.4 copy.31.seg_col_ref
  13.5 70.9 %shard_map.254 = bf16[8,256,2048]{2,1,0:T(8,128)(2,1)} custom-call(bf16[256,2048]{1,0:T(8,128)(2,1)S(1)} %copy-done, f32[1,2048]{1,0:T(1,128)S(1)} %bitcast.40, f32[1,2048]{1,0:T(1,128)S(1)} %bitcast.42), custom_call_target="tpu_custom_call" | custom-call | flops 419430400 | bytes 52428800 | tf_op jit(solution)/shard_map/pallas_call | solution.py:834
  84.4 1.9 copy-done.4
  86.3 8.8 %project.1.proj_ref = bf16[2048,768]{1,0:T(8,128)(2,1)S(1)} custom-call(bf16[2048,2048]{1,0:T(8,128)(2,1)} %bitcast.51, bf16[4,3,512,256]{3,2,1,0:T(8,128)(2,1)S(1)} %bitcast.35, f32[1,768]{1,0:T(1,128)S(1)} %broadcast_in_dim.40.bias_ref), custom_call_target="tpu_custom_call" | custom-call | flops 6442450944 | bytes 8388608 | tf_op jit(solution)/shard_map/project/pallas_call | solution.py:1010
  95.2 20.9 %attention_forward.1 = (bf16[2048,256]{1,0:T(8,128)(2,1)S(1)}, f32[4,2048]{1,0:T(4,128)S(1)}) custom-call(f32[4]{0:T(128)S(1)} %multiply_power_fusion.slope_ref, bf16[2048,768]{1,0:T(8,128)(2,1)S(1)} %project.1.proj_ref, s32[1,2048]{1,0:T(1,128)S(1)} %bitcast.46, s32[2048,1]{1,0:T(8,128)S(1)} %copy.31.seg_col_ref), custom_call_target="tpu_custom_call" | custom-call | flops 1610612736 | bytes 3145728 | tf_op jit(solution)/shard_map/attention_forward/pallas_call | solution.py:90
  116.1 1.7 copy-done.23
  117.8 175.9 %shard_map.255 = (bf16[8,256,2048]{2,1,0:T(8,128)(2,1)}, f32[256,2048]{1,0:T(8,128)}) custom-call(bf16[2048,256]{1,0:T(8,128)(2,1)S(1)} %get-tuple-element.48.attended_ref, bf16[4,256,512]{2,1,0:T(8,128)(2,1)} %bitcast.36, bf16[256,2048]{1,0:T(8,128)(2,1)} %input_ref.5, f32[1,2048]{1,0:T(1,128)S(1)} %bitcast.43, f32[1,2048]{1,0:T(1,128)S(1)} %bitcast.38, ...), custom_call_target="tpu_custom_call" | custom-call | flops 419430400 | bytes 52428800 | tf_op jit(solution)/shard_map/pallas_call | solution.py:834
  293.7 26.8 %mlp_forward.1 = (bf16[2048,1024]{1,0:T(8,128)(2,1)S(1)}, f32[2048,1024]{1,0:T(8,128)}, bf16[1024,2048]{1,0:T(8,128)(2,1)}, bf16[1024,2048]{1,0:T(8,128)(2,1)}) custom-call(bf16[2048,2048]{1,0:T(8,128)(2,1)} %bitcast.65, bf16[2048,1024]{1,0:T(8,128)(2,1)} %all-gather.11.cloned.1.call-done.up_ref, f32[1,1024]{1,0:T(1,128)S(1)} %bitcast.50, ...), custom_call_target="tpu_custom_call" | custom-call | flops 17179869184 | bytes 33554432 | tf_op jit(solution)/shard_map/mlp_forward/pallas_call | solution.py:1056
  320.6 2.0 copy-done.26
  322.6 25.3 %mlp_backward.1 = (bf16[2048,2048]{1,0:T(8,128)(2,1)}, bf16[2048,1024]{1,0:T(8,128)(2,1)S(1)}, bf16[2048,2048]{1,0:T(8,128)(2,1)}, f32[8,1024]{1,0:T(8,128)S(1)}) custom-call(bf16[8,128,2048]{2,1,0:T(8,128)(2,1)} %bitcast.68, bf16[8,128,2048]{2,1,0:T(8,128)(2,1)} %bitcast.67, f32[2048,1024]{1,0:T(8,128)} %get-tuple-element.50.slope_ref, ...), custom_call_target="tpu_custom_call" | custom-call | flops 17179869184 | bytes 41943040 | tf_op jit(solution)/shard_map/mlp_backward/pallas_call | solution.py:1115
  347.8 10.6 %convolution_convert_fusion.1 = bf16[2048,1024]{1,0:T(8,128)(2,1)} fusion(bf16[2048,2048]{1,0:T(8,128)(2,1)S(1)} %bitcast.66, bf16[2048,1024]{1,0:T(8,128)(2,1)S(1)} %get-tuple-element.54), kind=kOutput, calls=%fused_computation.1 | convolution fusion | flops 8592031744 | bytes 16777216 | tf_op jit(solution)/shard_map/dot_general | solution.py:1206
  358.4 14.1 %convolution_convert_fusion = bf16[1024,2048]{1,0:T(8,128)(2,1)} fusion(bf16[2048,1024]{1,0:T(8,128)(2,1)} %copy-done.26, bf16[2048,2048]{1,0:T(8,128)(2,1)} %get-tuple-element.53), kind=kOutput, calls=%fused_computation | convolution fusion | flops 8592031744 | bytes 16777216 | tf_op jit(solution)/shard_map/dot_general | solution.py:1203
  372.6 123.0 %shard_map.256 = (bf16[8,256,2048]{2,1,0:T(8,128)(2,1)}, f32[256,2048]{1,0:T(8,128)}, f32[4,8,2048]{2,1,0:T(8,128)S(1)}) custom-call(bf16[8,256,2048]{2,1,0:T(8,128)(2,1)} %bitcast.53, f32[256,2048]{1,0:T(8,128)} %get-tuple-element.58.residual_ref, bf16[256,2048]{1,0:T(8,128)(2,1)S(1)} %copy-done.3, f32[1,2048]{1,0:T(1,128)S(1)} %bitcast.39), custom_call_target="tpu_custom_call" | custom-call | flops 419430400 | bytes 52428800 | tf_op jit(solution)/shard_map/pallas_call | solution.py:834
  495.6 3.4 copy-done.21
  499.0 6.5 dense_backward.1
  505.4 1.0 copy-done.24
  506.4 0.0 reduce-scatter.13.cloned.1.call-start
  506.5 1.2 copy-done.25
  507.7 27.1 %attention_backward.1.grad_ref.grad_cat_ref = bf16[2048,768]{1,0:T(8,128)(2,1)S(1)} custom-call(f32[4]{0:T(128)S(1)} %multiply_power_fusion.slope_ref, bf16[2048,768]{1,0:T(8,128)(2,1)} %copy-done.23, bf16[2048,256]{1,0:T(8,128)(2,1)S(1)} %copy-done.25, f32[4,2048]{1,0:T(4,128)S(1)} %get-tuple-element.62.lse_ref, s32[1,2048]{1,0:T(1,128)S(1)} %bitcast.47, ...), custom_call_target="tpu_custom_call" | custom-call | flops 4026531840 | bytes 7340032 | tf_op jit(solution)/shard_map/attention_backward/pallas_call | solution.py:182
  534.8 13.0 %qkv_weight_grad.1 = (bf16[3,2048,256]{2,1,0:T(8,128)(2,1)}, f32[3,8,256]{2,1,0:T(8,128)S(1)}) custom-call(bf16[2048,2048]{1,0:T(8,128)(2,1)} %bitcast.52, bf16[2048,768]{1,0:T(8,128)(2,1)S(1)} %attention_backward.1.grad_ref.grad_cat_ref), custom_call_target="tpu_custom_call" | custom-call | flops 6442450944 | bytes 16777216 | tf_op jit(solution)/shard_map/qkv_weight_grad/pallas_call | solution.py:871
  547.9 0.0 reduce-scatter.15.cloned.1.call-start
  547.9 0.7 reduce-scatter.15.cloned.1.call-update
  548.7 0.5 reduce-scatter.17.cloned.1.call-update
  549.3 0.7 reduce-scatter.7.cloned.1.call-update
  550.0 0.3 reduce-scatter.9.cloned.1.call-start
  550.3 0.3 reduce-scatter.9.cloned.1.call-update
  550.7 136.5 %shard_map.257 = (f32[256,2048]{1,0:T(8,128)}, f32[8,2048]{1,0:T(8,128)S(1)}, f32[8,256]{1,0:T(8,128)S(1)}, f32[8,2048]{1,0:T(8,128)S(1)}) custom-call(bf16[2048,768]{1,0:T(8,128)(2,1)} %copy-done.5, bf16[4,3,512,256]{3,2,1,0:T(8,128)(2,1)} %bitcast.34, bf16[256,2048]{1,0:T(8,128)(2,1)S(1)} %copy-done.1, f32[256,2048]{1,0:T(8,128)} %get-tuple-element.68.residual_grad_ref, ...), custom_call_target="tpu_custom_call" | custom-call | flops 419430400 | bytes 52428800 | tf_op jit(solution)/shard_map/pallas_call | solution.py:834
  687.2 0.6 slice.50
  687.8 0.6 copy.33
  688.4 0.6 fusion.1
  689.1 39.2 %reduce-scatter.17.cloned.1.call-done.two_ref = bf16[128,2048]{1,0:T(8,128)(2,1)} async-done(((bf16[1024,2048]{1,0:T(8,128)(2,1)}), bf16[128,2048]{1,0:T(8,128)(2,1)}) %reduce-scatter.17.cloned.1.call-update) | async-done | bytes 524304 | tf_op jit(solution)/shard_map/reduce_scatter | solution.py:1213
  728.3 57.6 %reduce-scatter.7.cloned.1.call-done.down_ref = bf16[1024,512]{1,0:T(8,128)(2,1)} async-done(((bf16[1024,2048]{1,0:T(8,128)(2,1)}), bf16[1024,512]{1,0:T(8,128)(2,1)}) %reduce-scatter.7.cloned.1.call-update) | async-done | bytes 1048592 | tf_op jit(solution)/shard_map/reduce_scatter | solution.py:1146
  785.9 55.5 %reduce-scatter.9.cloned.1.call-done.up_ref = bf16[512,1024]{1,0:T(8,128)(2,1)} async-done(((bf16[2048,1024]{1,0:T(8,128)(2,1)}), bf16[512,1024]{1,0:T(8,128)(2,1)}) %reduce-scatter.9.cloned.1.call-update) | async-done | bytes 1048592 | tf_op jit(solution)/shard_map/reduce_scatter | solution.py:1146
  841.3 1.6 copy-done.6
  842.9 1.2 copy-done.8
  844.2 1.2 copy-done.9
  845.4 1.1 copy-done.10
  846.5 1.0 copy-done.11
  847.6 1.0 copy-done.12
  848.6 0.9 copy-done.13
  849.6 3.7 finish.1
  (77 shorter events, 0.6 us)
Async XLA Ops:
  7.2 5.8 copy-start.27
  7.2 5.9 copy-start.19
  7.2 6.3 copy-start
  7.2 6.2 copy-start.16
  7.2 6.2 copy-start.15
  7.2 77.1 %all-gather.19.cloned.1.call-start = ((), (), s32[]{:S(2)}) async-start(), calls=%async_computation.16 | async-start | bytes 3932160 | tf_op jit(solution)/shard_map/all_gather | solution.py:1171
  8.0 109.8 %all-gather.21.cloned.1.call-start = ((), (), s32[]{:S(2)}) async-start(), calls=%async_computation.17 | async-start | bytes 1310720 | tf_op jit(solution)/shard_map/all_gather | solution.py:1172
  8.7 285.0 %all-gather.11.cloned.1.call-start = ((), (), s32[]{:S(2)}) async-start(), calls=%async_computation.6 | async-start | bytes 5242880 | tf_op jit(solution)/shard_map/all_gather | solution.py:1173
  9.5 284.2 %all-gather.13.cloned.1.call-start = ((), (), s32[]{:S(2)}) async-start(), calls=%async_computation.7 | async-start | bytes 5242880 | tf_op jit(solution)/shard_map/all_gather | solution.py:1174
  10.0 312.5 %all-gather.17.cloned.1.call-start = ((), (), s32[]{:S(2)}) async-start(), calls=%async_computation.15 | async-start | bytes 4718592 | tf_op jit(solution)/shard_map/all_gather | solution.py:1177
  12.4 310.2 %all-gather.15.cloned.1.call-start = ((), (), s32[]{:S(2)}) async-start(), calls=%async_computation.14 | async-start | bytes 4718592 | tf_op jit(solution)/shard_map/all_gather | solution.py:1176
  13.0 676.1 %reduce-scatter.11.cloned.1.call-start = ((), (), s32[]{:S(2)}) async-start(), calls=%async_computation.10 | async-start | bytes 1310720 | tf_op jit(solution)/shard_map/reduce_scatter | solution.py:1146
  84.4 1.9 copy-start.4
  95.1 22.6 %copy-start.14 = (f32[2048]{0:T(1024)S(1)}, f32[2048]{0:T(1024)}, u32[]{:S(2)}) copy-start(f32[2048]{0:T(1024)} %param.23) | copy-start | bytes 24580
  95.1 22.6 %copy-start.17 = (f32[2048]{0:T(1024)S(1)}, f32[2048]{0:T(1024)}, u32[]{:S(2)}) copy-start(f32[2048]{0:T(1024)} %param.22) | copy-start | bytes 24580
  95.1 22.6 %copy-start.18 = (f32[2048]{0:T(1024)S(1)}, f32[2048]{0:T(1024)}, u32[]{:S(2)}) copy-start(f32[2048]{0:T(1024)} %param.24) | copy-start | bytes 24580
  95.1 198.6 %copy-start.22 = (f32[1024]{0:T(1024)S(1)}, f32[1024]{0:T(1024)}, u32[]{:S(2)}) copy-start(f32[1024]{0:T(1024)} %param.26) | copy-start | bytes 12292
  116.1 1.7 copy-start.23
  320.6 2.0 copy-start.26
  322.6 25.3 %copy-start.28 = (bf16[8,256,2048]{2,1,0:T(8,128)(2,1)S(1)}, bf16[8,256,2048]{2,1,0:T(8,128)(2,1)}, u32[]{:S(2)}) copy-start(bf16[8,256,2048]{2,1,0:T(8,128)(2,1)} %get-tuple-element.49) | copy-start | bytes 25165828
  358.4 14.1 %copy-start.3 = (bf16[256,2048]{1,0:T(8,128)(2,1)S(1)}, bf16[256,2048]{1,0:T(8,128)(2,1)}, u32[]{:S(2)}) copy-start(bf16[256,2048]{1,0:T(8,128)(2,1)} %grad_ref.1) | copy-start | bytes 3145732
  372.6 123.0 %copy-start.7 = (bf16[1024,512]{1,0:T(8,128)(2,1)S(1)}, bf16[1024,512]{1,0:T(8,128)(2,1)}, u32[]{:S(2)}) copy-start(bf16[1024,512]{1,0:T(8,128)(2,1)} %all-gather.21.cloned.1.call-done) | copy-start | bytes 3145732
  495.6 3.4 copy-start.21
  505.4 1.0 copy-start.24
  506.4 182.6 %reduce-scatter.13.cloned.1.call-start = ((), (), s32[]{:S(2)}) async-start(), calls=%async_computation.11 | async-start | bytes 3932160 | tf_op jit(solution)/shard_map/reduce_scatter | solution.py:1146
  506.5 1.2 copy-start.25
  534.8 13.1 %copy-start.5 = (bf16[2048,768]{1,0:T(8,128)(2,1)}, bf16[2048,768]{1,0:T(8,128)(2,1)S(1)}, u32[]{:S(2)}) copy-start(bf16[2048,768]{1,0:T(8,128)(2,1)S(1)} %attention_backward.1.grad_ref.grad_cat_ref) | copy-start | bytes 9437188
  547.9 141.2 %reduce-scatter.15.cloned.1.call-start = ((), (), s32[]{:S(2)}) async-start(), calls=%async_computation.12 | async-start | bytes 4718592 | tf_op jit(solution)/shard_map/reduce_scatter | solution.py:1212
  548.6 179.7 %reduce-scatter.17.cloned.1.call-start = ((), (), s32[]{:S(2)}) async-start(), calls=%async_computation.13 | async-start | bytes 4718592 | tf_op jit(solution)/shard_map/reduce_scatter | solution.py:1213
  549.2 1.4 copy-start.1
  549.2 236.6 %reduce-scatter.7.cloned.1.call-start = ((), (), s32[]{:S(2)}) async-start(), calls=%async_computation.8 | async-start | bytes 5242880 | tf_op jit(solution)/shard_map/reduce_scatter | solution.py:1146
  550.0 291.4 %reduce-scatter.9.cloned.1.call-start = ((), (), s32[]{:S(2)}) async-start(), calls=%async_computation.9 | async-start | bytes 5242880 | tf_op jit(solution)/shard_map/reduce_scatter | solution.py:1146
  550.6 290.7 %copy-start.2 = (f32[256,2048]{1,0:T(8,128)S(1)}, f32[256,2048]{1,0:T(8,128)}, u32[]{:S(2)}) copy-start(f32[256,2048]{1,0:T(8,128)} %get-tuple-element.58.residual_ref) | copy-start | bytes 6291460
  550.7 290.7 %copy-start.20 = (f32[2048]{0:T(1024)S(1)}, f32[2048]{0:T(1024)}, u32[]{:S(2)}) copy-start(f32[2048]{0:T(1024)} %param.28) | copy-start | bytes 24580
  841.3 1.6 copy-start.6
  842.9 1.2 copy-start.8
  844.2 1.2 copy-start.9
  845.4 1.1 copy-start.10
  846.5 1.0 copy-start.11
  847.6 1.0 copy-start.12
  848.6 0.9 copy-start.13
Sparse Core Ops, SparseCore 0:
  9.9 45.0 all-gather.18
  56.9 26.4 all-gather.20
  85.2 52.6 all-gather.10
  139.6 52.4 all-gather.12
  194.1 58.0 all-gather.16
  254.2 51.3 all-gather.14
  506.6 30.1 reduce-scatter.10
  548.0 46.8 reduce-scatter.12
  597.2 84.5 reduce-scatter.14
  683.9 44.3 reduce-scatter.16
  731.3 54.5 reduce-scatter.6
  788.7 52.5 reduce-scatter.8

commit v3 on v2

--- a/solution.py
+++ b/solution.py
@@ -16,6 +16,7 @@
 PAIR = 2 * HEAD_DIM
 Q_BLOCK = 256
 MASKED = -1e32
+VMEM_BYTES = 67043328
 NT = (((1,), (1,)), ((), ()))
 NN = (((1,), (0,)), ((), ()))
 
@@ -108,7 +109,7 @@
             pltpu.VMEM((cols, seq_len), jnp.bfloat16),
             pltpu.VMEM((width, Q_BLOCK), jnp.float32),
         ],
-        compiler_params=pltpu.CompilerParams(vmem_limit_bytes=40 * 2**20),
+        compiler_params=pltpu.CompilerParams(vmem_limit_bytes=VMEM_BYTES),
         cost_estimate=pl.CostEstimate(flops=4 * seq_len * width * cols, bytes_accessed=6 * seq_len * cols, transcendentals=0),
         name="attention_forward",
     )(slopes, projected, segments[None, :], segments[:, None])
@@ -198,7 +199,7 @@
             pltpu.VMEM((seq_len, cols), jnp.float32),
             pltpu.VMEM((seq_len, cols), jnp.float32),
         ],
-        compiler_params=pltpu.CompilerParams(vmem_limit_bytes=48 * 2**20),
+        compiler_params=pltpu.CompilerParams(vmem_limit_bytes=VMEM_BYTES),
         cost_estimate=pl.CostEstimate(flops=10 * seq_len * width * cols, bytes_accessed=14 * seq_len * cols, transcendentals=0),
         name="attention_backward",
     )(slopes, projected, head_grad, log_sums, segments[None, :], segments[:, None])
@@ -484,9 +485,11 @@
 
 
 def for_tiles(line, sub, body):
-    @pl.loop(0, line.sub_rows // ROW_TILE)
+    size = min(2 * ROW_TILE, line.sub_rows)
+
+    @pl.loop(0, line.sub_rows // size)
     def _(tile):
-        body(line.tile(sub, tile))
+        body(pl.ds(pl.multiple_of(sub * line.sub_rows + tile * size, size), size))
 
 
 def run_gather(line, gather, rows_done):
@@ -505,9 +508,9 @@
     gather.finish()
 
 
-def run_line(line, reduce, gather, rows_done, beside=None):
+def run_line(line, reduce, gather, rows_done, beside=None, entered=False):
     steps = line.chips - 1
-    if beside is None:
+    if not entered:
         line.enter()
     reduce.start()
     slots = steps * SUBS + LAG + (steps if gather is not None else 0) + 1
@@ -601,12 +604,69 @@
     run_line(line, reduce, gather, rows_done)
 
 
+class Beside:
+    def __init__(self, whole, pre, out, scratch):
+        self.whole, self.pre, self.out = whole, pre, out
+        self.loaded, self.stored, self.load_sem, self.store_sem = scratch
+        self.block = self.loaded.shape[2]
+        self.count = out.shape[0] // self.block
+
+    @staticmethod
+    def scratch(tokens, width, hidden):
+        block = min(256, width)
+        dma = pltpu.SemaphoreType.DMA
+        return [
+            pltpu.VMEM((2, tokens, block), jnp.bfloat16),
+            pltpu.VMEM((2, block, hidden), jnp.bfloat16),
+            dma((2,)),
+            dma((2,)),
+        ]
+
+    def at(self, index):
+        return pl.ds(pl.multiple_of(index * self.block, self.block), self.block)
+
+    def load(self, index):
+        return pltpu.make_async_copy(
+            self.whole.at[:, self.at(index)], self.loaded.at[index % 2], self.load_sem.at[index % 2]
+        )
+
+    def store(self, index):
+        return pltpu.make_async_copy(
+            self.stored.at[index % 2], self.out.at[self.at(index)], self.store_sem.at[index % 2]
+        )
+
+    def start(self):
+        self.load(0).start()
+
+    def slot(self, slot):
+        index = slot - 1
+
+        @pl.when((index >= 0) & (index < self.count))
+        def _():
+            self.load(index).wait()
+            pl.when(index + 1 < self.count)(lambda: self.load(index + 1).start())
+            pl.when(index >= 2)(lambda: self.store(index - 2).wait())
+            self.stored[index % 2] = lax.dot_general(
+                self.loaded[index % 2],
+                self.pre[...],
+                (((0,), (0,)), ((), ())),
+                preferred_element_type=jnp.float32,
+            ).astype(jnp.bfloat16)
+            self.store(index).start()
+
+    def finish(self):
+        for index in range(max(self.count - 2, 0), self.count):
+            self.store(index).wait()
+
+
 def grad_gather_kernel(
-    chips, partial_ref, residual_ref, grad_ref, gain_ref, whole_ref, residual_grad_ref, sums_ref, branch_ref, *rest
+    chips, partial_ref, whole_in_ref, residual_ref, grad_ref, gain_ref, pre_ref,
+    whole_ref, up_ref, residual_grad_ref, sums_ref, branch_ref, *rest
 ):
     line = Line(chips, grad_ref.shape[0])
     reduce = Reduce(line, partial_ref, rest[:4], rest[4:9])
-    gather = Gather(line, branch_ref, whole_ref, rest[9:])
+    gather = Gather(line, branch_ref, whole_ref, rest[9:14])
+    beside = Beside(whole_in_ref, pre_ref, up_ref, rest[14:])
     sums_ref[...] = jnp.zeros_like(sums_ref)
 
     def rows_done(at):
@@ -622,12 +682,63 @@
         sums_ref[2] += fold(branch.astype(jnp.float32))
         sums_ref[3] += fold(out_grad)
 
-    run_line(line, reduce, gather, rows_done)
+    beside.start()
+    run_line(line, reduce, gather, rows_done, beside.slot)
+    beside.finish()
+
+
+class Exchange:
+    def __init__(self, partial, parts, scratch):
+        self.partial, self.parts = partial, parts
+        self.stage, self.in_sem, self.out_sem, self.send_sem, self.recv_sem = scratch
+        self.groups = lax.axis_size("dp")
+        self.group = lax.axis_index("dp")
+
+    @staticmethod
+    def scratch(groups, block):
+        dma = pltpu.SemaphoreType.DMA
+        return [pltpu.VMEM(block, jnp.bfloat16), dma, dma, dma((groups,)), dma((groups,))]
+
+    def peer(self, step):
+        return lax.rem(self.group + step, self.groups)
+
+    def copy(self, peer, slot, step):
+        return pltpu.make_async_remote_copy(
+            src_ref=self.partial.at[peer],
+            dst_ref=self.parts.at[slot],
+            send_sem=self.send_sem.at[step],
+            recv_sem=self.recv_sem.at[slot],
+            device_id={"dp": peer},
+            device_id_type=MESH,
+        )
+
+    def own_in(self):
+        return pltpu.make_async_copy(self.partial.at[self.group], self.stage, self.in_sem)
+
+    def own_out(self):
+        return pltpu.make_async_copy(self.stage, self.parts.at[self.group], self.out_sem)
+
+    def start(self):
+        for step in range(1, self.groups):
+            self.copy(self.peer(step), self.group, step).start()
+        self.own_in().start()
+
+    def slot(self, slot):
+        @pl.when(slot == 2)
+        def _():
+            self.own_in().wait()
+            self.own_out().start()
+
+    def finish(self):
+        for step in range(1, self.groups):
+            self.copy(self.peer(step), self.peer(step), step).wait_recv()
+            self.copy(self.peer(step), self.group, step).wait_send()
+        self.own_out().wait()
 
 
 def grad_kernel(
-    chips, grad_cat_ref, weight_ref, input_ref, residual_grad_ref, gain_ref, early_ref, own_ref,
-    out_ref, early_out_ref, own_out_ref, late_ref, mirror, *rest
+    chips, up_ref, grad_cat_ref, weight_ref, input_ref, residual_grad_ref, gain_ref, early_ref, own_ref,
+    up_parts_ref, out_ref, early_out_ref, own_out_ref, late_ref, mirror, *rest
 ):
     line = Line(chips, input_ref.shape[0])
     rows = input_ref.shape[0]
@@ -648,7 +759,8 @@
             target[slot, :, index * part : (index + 1) * part] = total.astype(jnp.bfloat16)
 
     reduce = Reduce(line, mirror, rest[:4], rest[4:9], product)
-    sums = Sums(2 * chips, early_ref, own_ref, early_out_ref, own_out_ref, late_ref, rest[9:])
+    sums = Sums(2 * chips, early_ref, own_ref, early_out_ref, own_out_ref, late_ref, rest[9:28])
+    exchange = Exchange(up_ref, up_parts_ref, rest[28:])
     sums.late_sum[...] = jnp.zeros_like(sums.late_sum)
 
     def rows_done(at):
@@ -658,9 +770,15 @@
         sums.late_sum[0] += fold(grad * unit)
         sums.late_sum[1] += fold(grad)
 
+    def beside(slot):
+        sums.beside(slot)
+        exchange.slot(slot)
+
     sums.greet()
-    run_line(line, reduce, None, rows_done, sums.beside)
+    exchange.start()
+    run_line(line, reduce, None, rows_done, beside, True)
     sums.close()
+    exchange.finish()
 
 
 class Sums:
@@ -689,10 +807,10 @@
             pltpu.VMEM((ranks, 8, part), f32),
             pltpu.VMEM((16, part), f32),
             pltpu.VMEM((groups, 16, part), f32),
-            pltpu.VMEM((8, width), f32),
-            pltpu.VMEM((groups, 8, width), f32),
-            pltpu.VMEM((8, width), f32),
-            pltpu.VMEM((ranks, 8, width), f32),
+            pltpu.VMEM((2, width), f32),
+            pltpu.VMEM((groups, 2, width), f32),
+            pltpu.VMEM((2, width), f32),
+            pltpu.VMEM((ranks, 2, width), f32),
         ] + [dma((ranks,)), dma((ranks,)), dma((groups,)), dma((groups,)), dma((ranks,)), dma((ranks,)),
              dma((groups,)), dma((groups,)), dma((ranks,)), dma((ranks,))]
 
@@ -781,7 +899,6 @@
                 self.spread(self.rank(step), self.me, step).start()
 
     def close(self):
-        self.late_mine[...] = jnp.zeros_like(self.late_mine)
         for row in range(2):
             self.late_mine[row : row + 1, :] = jnp.sum(self.late_sum[row], axis=0, keepdims=True)
         for step in range(1, self.groups):
@@ -813,13 +930,13 @@
             self.late_exchange(self.peer(step), self.group, step).wait_send()
 
 
-def line_call(kernel, collective_id, operands, outs, rows, width, gathers=True, reduces=True, product=False, sums=False):
+def line_call(kernel, collective_id, operands, outs, rows, width, gathers=True, reduces=True, product=False, sums=False, placed=(), more=()):
     ranks = lax.axis_size("tensor")
     chips = ranks // 2
     whole = jax.ShapeDtypeStruct((ranks, rows, width), jnp.bfloat16)
     in_vmem = pl.BlockSpec(memory_space=pltpu.VMEM)
     in_place = pl.BlockSpec(memory_space=pl.ANY)
-    streamed = int(reduces and not product)
+    ins_placed, outs_placed = placed or (0, 0)
     scratch = []
     if gathers:
         scratch.append(pltpu.VMEM((rows, width), jnp.bfloat16))
@@ -831,14 +948,15 @@
         scratch += Gather.scratch(chips)
     if sums:
         scratch += Sums.scratch(ranks, lax.axis_size("dp"), width)
+    scratch += list(more)
     return pl.pallas_call(
         functools.partial(kernel, chips),
-        in_specs=[in_place] * streamed + [in_vmem] * (len(operands) - streamed),
-        out_specs=([in_place] if gathers else []) + [in_vmem] * len(outs),
+        in_specs=[in_place] * ins_placed + [in_vmem] * (len(operands) - ins_placed),
+        out_specs=[in_place] * (outs_placed + int(gathers)) + [in_vmem] * (len(outs) - outs_placed),
         out_shape=([whole] if gathers else []) + list(outs),
         scratch_shapes=scratch,
         compiler_params=pltpu.CompilerParams(
-            collective_id=collective_id, has_side_effects=True, vmem_limit_bytes=52 * 2**20
+            collective_id=collective_id, has_side_effects=True, vmem_limit_bytes=VMEM_BYTES
         ),
         cost_estimate=pl.CostEstimate(
             flops=8 * rows * width * 100, bytes_accessed=100 * rows * width, transcendentals=0
@@ -883,7 +1001,7 @@
             jax.ShapeDtypeStruct((3, width, head_width), jnp.bfloat16),
             jax.ShapeDtypeStruct((3, 8, head_width), jnp.float32),
         ],
-        compiler_params=pltpu.CompilerParams(vmem_limit_bytes=40 * 2**20),
+        compiler_params=pltpu.CompilerParams(vmem_limit_bytes=VMEM_BYTES),
         cost_estimate=pl.CostEstimate(
             flops=6 * tokens * width * head_width, bytes_accessed=4 * tokens * width, transcendentals=0
         ),
@@ -894,7 +1012,10 @@
 def finish_kernel(down_ref, up_ref, dense_ref, qkv_ref, one_ref, two_ref, residual_ref, bias_ref, grad_ref,
                   down_out, up_out, dense_out, qkv_out, rows_out, grad_out):
     down_out[...] = down_ref[...].astype(jnp.float32)
-    up_out[...] = up_ref[...].astype(jnp.float32)
+    total = up_ref[0].astype(jnp.float32)
+    for group in range(1, up_ref.shape[0]):
+        total = total + up_ref[group].astype(jnp.float32)
+    up_out[...] = total
     dense_out[...] = dense_ref[...].astype(jnp.float32)
     qkv_out[...] = qkv_ref[...].astype(jnp.float32)
     half = pl.program_id(0) < pl.num_programs(0) // 2
@@ -917,7 +1038,7 @@
     specs[4] = pl.BlockSpec(row_part, lambda i: (jnp.minimum(i, steps // 2 - 1), 0))
     specs[5] = pl.BlockSpec(row_part, lambda i: (jnp.maximum(i - steps // 2, 0), 0))
     specs[7] = pl.BlockSpec((1, bias.shape[0]), lambda i: (0, 0))
-    outs = [jax.ShapeDtypeStruct(item.shape, jnp.float32) for item in (down, up, dense, qkv)]
+    outs = [jax.ShapeDtypeStruct(item.shape, jnp.float32) for item in (down, up[0], dense, qkv)]
     outs.append(jax.ShapeDtypeStruct(residual.shape, jnp.bfloat16))
     outs.append(jax.ShapeDtypeStruct(input_grad.shape, jnp.float32))
     return pl.pallas_call(
@@ -926,7 +1047,7 @@
         in_specs=specs,
         out_specs=[split(item.shape) for item in outs],
         out_shape=outs,
-        compiler_params=pltpu.CompilerParams(vmem_limit_bytes=32 * 2**20),
+        compiler_params=pltpu.CompilerParams(vmem_limit_bytes=VMEM_BYTES),
         name="finish",
     )(*operands)
 
@@ -977,7 +1098,7 @@
             jax.ShapeDtypeStruct((head_width, width), jnp.bfloat16),
         ],
         scratch_shapes=[pltpu.VMEM((head_width, width), jnp.float32)],
-        compiler_params=pltpu.CompilerParams(vmem_limit_bytes=40 * 2**20),
+        compiler_params=pltpu.CompilerParams(vmem_limit_bytes=VMEM_BYTES),
         cost_estimate=pl.CostEstimate(
             flops=4 * tokens * width * head_width, bytes_accessed=2 * tokens * width, transcendentals=0
         ),
@@ -1017,7 +1138,7 @@
         ],
         out_specs=pl.BlockSpec((block, 3 * head_width), lambda i: (i, 0)),
         out_shape=jax.ShapeDtypeStruct((tokens, 3 * head_width), jnp.bfloat16),
-        compiler_params=pltpu.CompilerParams(vmem_limit_bytes=40 * 2**20),
+        compiler_params=pltpu.CompilerParams(vmem_limit_bytes=VMEM_BYTES),
         cost_estimate=pl.CostEstimate(
             flops=6 * tokens * width * head_width, bytes_accessed=2 * tokens * width, transcendentals=0
         ),
@@ -1074,7 +1195,7 @@
             jax.ShapeDtypeStruct((tokens // 2, width), jnp.bfloat16),
             jax.ShapeDtypeStruct((tokens // 2, width), jnp.bfloat16),
         ],
-        compiler_params=pltpu.CompilerParams(vmem_limit_bytes=48 * 2**20),
+        compiler_params=pltpu.CompilerParams(vmem_limit_bytes=VMEM_BYTES),
         cost_estimate=pl.CostEstimate(
             flops=4 * tokens * width * hidden, bytes_accessed=8 * tokens * width, transcendentals=0
         ),
@@ -1134,7 +1255,7 @@
             jax.ShapeDtypeStruct((tokens, width), jnp.bfloat16),
             jax.ShapeDtypeStruct((8, hidden), jnp.float32),
         ],
-        compiler_params=pltpu.CompilerParams(vmem_limit_bytes=48 * 2**20),
+        compiler_params=pltpu.CompilerParams(vmem_limit_bytes=VMEM_BYTES),
         cost_estimate=pl.CostEstimate(
             flops=4 * tokens * width * hidden, bytes_accessed=10 * tokens * width, transcendentals=0
         ),
@@ -1203,19 +1324,20 @@
     down_grad = lax.dot_general(
         activated, out_whole, (((0,), (0,)), ((), ())), preferred_element_type=jnp.float32
     ).astype(jnp.bfloat16)
-    up_grad = lax.dot_general(
-        whole2, pre_grad, (((0,), (0,)), ((), ())), preferred_element_type=jnp.float32
-    ).astype(jnp.bfloat16)
-    normed2_part, down_grad, up_grad = lax.optimization_barrier((normed2_part, down_grad, up_grad))
+    normed2_part, down_grad = lax.optimization_barrier((normed2_part, down_grad))
     down_wgrad = over_dp(down_grad, 1)
-    up_wgrad = over_dp(up_grad, 0)
     mlp_rows_one = lax.psum_scatter(mlp_one, "tensor", scatter_dimension=0, tiled=True)
     mlp_rows_two = lax.psum_scatter(mlp_two, "tensor", scatter_dimension=0, tiled=True)
 
-    branch_whole, residual_grad, second_sums = line_call(
+    branch_whole, up_grad, residual_grad, second_sums = line_call(
         grad_gather_kernel, 3,
-        (normed2_part.reshape(ranks, rows, width), residual, out_grad, second_gain[None]),
-        (f32_rows, jax.ShapeDtypeStruct((4, 8, width), jnp.float32)), rows, width,
+        (normed2_part.reshape(ranks, rows, width), whole2, residual, out_grad, second_gain[None], pre_grad),
+        (
+            jax.ShapeDtypeStruct((width, up_width), jnp.bfloat16),
+            f32_rows,
+            jax.ShapeDtypeStruct((4, 8, width), jnp.float32),
+        ),
+        rows, width, placed=(2, 1), more=Beside.scratch(tokens, width, up_width),
     )
     branch_whole = branch_whole.reshape(tokens, width)
     attended_grad, dense_grad = dense_backward(branch_whole, attended, dense_all)
@@ -1231,14 +1353,23 @@
     own = jnp.concatenate([qkv_sums[0], qkv_sums[2], up_bias_part]).reshape(-1, part)
     own = jnp.pad(own, ((0, 8 - own.shape[0]), (0, 0)))
     f32_sums = jax.ShapeDtypeStruct((8, width), jnp.float32)
-    input_grad, early, own, late = line_call(
+    groups = lax.axis_size("dp")
+    up_block = (width // groups, up_width)
+    up_parts, input_grad, early, own, late = line_call(
         grad_kernel, 4,
-        (qkv_grad_cat, qkv_all, layer_input, residual_grad, first_gain[None], second_sums, own),
-        (f32_rows, f32_sums, jax.ShapeDtypeStruct((8, part), jnp.float32), f32_sums),
-        rows, width, gathers=False, product=True, sums=True,
+        (up_grad.reshape((groups,) + up_block), qkv_grad_cat, qkv_all, layer_input, residual_grad, first_gain[None], second_sums, own),
+        (
+            jax.ShapeDtypeStruct((groups,) + up_block, jnp.bfloat16),
+            f32_rows,
+            f32_sums,
+            jax.ShapeDtypeStruct((8, part), jnp.float32),
+            jax.ShapeDtypeStruct((2, width), jnp.float32),
+        ),
+        rows, width, gathers=False, product=True, sums=True, placed=(1, 1),
+        more=Exchange.scratch(groups, up_block),
     )
     down_wgrad, up_wgrad, dense_wgrad, qkv_wgrad, layer_out, input_grad = finish(
-        down_wgrad, up_wgrad, dense_wgrad, qkv_wgrad,
+        down_wgrad, up_parts, dense_wgrad, qkv_wgrad,
         mlp_rows_one, mlp_rows_two, residual, down_bias, input_grad,
     )
     return (

time: 863 us -> 819 us (0.949)
  waiting for transfers between devices: 158 us -> 120 us
  Pallas kernels: 638 us -> 658 us
  local copies, waits for them, and re-layouts: 23.9 us -> 9.07 us
  matrix products: 24.7 us -> 14.1 us
    reduce_scatter x4 -> x3, waiting for transfers between devices: 113 us -> 57.6 us  [over_dp(): return lax.psum_scatter(grad, 'dp', scatter_dimension=dimension, tiled=True)]
    unnamed x60 -> x10, local copies, waits for them, and re-layouts: 20 us -> 1.32 us
    dot_general x1 -> x0, matrix products: 10.6 us -> none  [layer(): lax.dot_general(whole2, pre_grad, (((0,), (0,)), ((), ())), preferred_ele...]
    reduce_scatter x1, waiting for transfers between devices: 39.2 us -> 49.6 us  [layer(): lax.psum_scatter(mlp_two, 'tensor', scatter_dimension=0, tiled=True)]
  transfers between devices with their start and end apart: 12 -> 11, of which waited for: 3 -> 3; matrix products, arithmetic and copies ran while one was open for 1% -> 1% of each run, Pallas kernels for 56% -> 61%
where the time goes in v3:
time: 819 us; the launch traced here: 816 us
  Pallas kernels  658 us (80%)
  waiting for transfers between devices  120 us (15%)
  matrix products  14.1 us (2%)
  between operations  14.1 us (2%)
  local copies, waits for them, and re-layouts  9.07 us (1%)
    pallas_call x4, Pallas kernels, line_call(): pl.pallas_call(functools.partial(kernel, chips), in_specs=[in_place] * in...  512 us
    reduce_scatter x3, waiting for transfers between devices, over_dp(): return lax.psum_scatter(grad, 'dp', scatter_dimension=dimension, tiled=True)  57.6 us
    reduce_scatter x1, waiting for transfers between devices, layer(): lax.psum_scatter(mlp_two, 'tensor', scatter_dimension=0, tiled=True)  49.6 us
    pallas_call x1, Pallas kernels, attention_backward(): pl.pallas_call(backward_kernel, grid=(seq_len // Q_BLOCK,), in_specs=[pl....  29.4 us
    pallas_call x1, Pallas kernels, mlp_forward(): pl.pallas_call(mlp_forward_kernel, grid=(tokens // block,), in_specs=[pl....  26.9 us
    pallas_call x1, Pallas kernels, mlp_backward(): pl.pallas_call(mlp_backward_kernel, grid=(ranks,), in_specs=[pl.BlockSpec...  25.2 us
    pallas_call x1, Pallas kernels, attention_forward(): pl.pallas_call(forward_kernel, grid=(seq_len // Q_BLOCK,), in_specs=[pl.B...  23.3 us
  transfers between devices with their start and end apart: 11, of which 3 were waited for; matrix products, arithmetic and copies ran while one was open for 1% of the time, Pallas kernels for 61%

profile of v3, /device:TPU:8, one launch (start us, length us, event | category | flops | bytes accessed | tf_op | source)
XLA Modules:
  0.0 816.4 jit_solution(15559932084674953108)
XLA Ops:
  7.2 0.0 all-gather.19.cloned.1.call-start
  7.2 0.7 all-gather.19.cloned.1.call-update
  7.9 0.0 all-gather.21.cloned.1.call-start
  8.0 0.7 all-gather.21.cloned.1.call-update
  8.7 0.0 all-gather.11.cloned.1.call-start
  8.7 0.7 all-gather.11.cloned.1.call-update
  9.4 0.0 all-gather.13.cloned.1.call-start
  9.5 0.5 all-gather.13.cloned.1.call-update
  10.0 0.0 all-gather.17.cloned.1.call-start
  10.0 2.3 fusion
  12.3 0.0 all-gather.15.cloned.1.call-start
  12.4 0.5 all-gather.15.cloned.1.call-update
  12.9 0.0 reduce-scatter.8.cloned.1.call-start
  13.0 0.6 broadcast_in_dim.40.bias_ref
  13.6 1.3 copy.31.seg_col_ref
  15.0 71.7 %shard_map.254 = bf16[8,256,2048]{2,1,0:T(8,128)(2,1)} custom-call(bf16[256,2048]{1,0:T(8,128)(2,1)} %input_ref.5, f32[1,2048]{1,0:T(1,128)} %bitcast.45, f32[1,2048]{1,0:T(1,128)} %bitcast.47), custom_call_target="tpu_custom_call" | custom-call | flops 419430400 | bytes 52428800 | tf_op jit(solution)/shard_map/pallas_call | solution.py:952
  86.6 0.5 multiply_power_fusion.slope_ref
  87.2 11.0 %project.1.proj_ref = bf16[2048,768]{1,0:T(8,128)(2,1)} custom-call(bf16[2048,2048]{1,0:T(8,128)(2,1)} %bitcast.33, bf16[4,3,512,256]{3,2,1,0:T(8,128)(2,1)} %bitcast.39, f32[1,768]{1,0:T(1,128)} %broadcast_in_dim.40.bias_ref), custom_call_target="tpu_custom_call" | custom-call | flops 6442450944 | bytes 8388608 | tf_op jit(solution)/shard_map/project/pallas_call | solution.py:1131
  98.1 23.3 %attention_forward.1 = (bf16[2048,256]{1,0:T(8,128)(2,1)}, f32[4,2048]{1,0:T(4,128)}) custom-call(f32[4]{0:T(128)} %multiply_power_fusion.slope_ref, bf16[2048,768]{1,0:T(8,128)(2,1)} %project.1.proj_ref, s32[1,2048]{1,0:T(1,128)} %bitcast.50, s32[2048,1]{1,0:T(8,128)} %copy.31.seg_col_ref), custom_call_target="tpu_custom_call" | custom-call | flops 1610612736 | bytes 3145728 | tf_op jit(solution)/shard_map/attention_forward/pallas_call | solution.py:91
  121.4 187.2 %shard_map.255 = (bf16[8,256,2048]{2,1,0:T(8,128)(2,1)}, f32[256,2048]{1,0:T(8,128)}) custom-call(bf16[2048,256]{1,0:T(8,128)(2,1)} %get-tuple-element.49.attended_ref, bf16[4,256,512]{2,1,0:T(8,128)(2,1)} %bitcast.41, bf16[256,2048]{1,0:T(8,128)(2,1)} %input_ref.5, f32[1,2048]{1,0:T(1,128)} %bitcast.48, f32[1,2048]{1,0:T(1,128)} %bitcast.43, f32[1,2048]{1,0:T(1,128)} %bitcast.49), custom_call_target="tpu_custom_call" | custom-call | flops 419430400 | bytes 52428800 | tf_op jit(solution)/shard_map/pallas_call | solution.py:952
  308.6 0.0 all-gather.11.cloned.1.call-done.up_ref
  308.6 0.0 all-gather.13.cloned.1.call-done.down_ref
  308.6 26.9 %mlp_forward.1 = (bf16[2048,1024]{1,0:T(8,128)(2,1)}, f32[2048,1024]{1,0:T(8,128)}, bf16[1024,2048]{1,0:T(8,128)(2,1)}, bf16[1024,2048]{1,0:T(8,128)(2,1)}) custom-call(bf16[2048,2048]{1,0:T(8,128)(2,1)} %bitcast.35, bf16[2048,1024]{1,0:T(8,128)(2,1)} %all-gather.11.cloned.1.call-done.up_ref, f32[1,1024]{1,0:T(1,128)} %bitcast.68, ...), custom_call_target="tpu_custom_call" | custom-call | flops 17179869184 | bytes 33554432 | tf_op jit(solution)/shard_map/mlp_forward/pallas_call | solution.py:1177
  335.6 25.2 %mlp_backward.1 = (bf16[2048,2048]{1,0:T(8,128)(2,1)}, bf16[2048,1024]{1,0:T(8,128)(2,1)}, bf16[2048,2048]{1,0:T(8,128)(2,1)}, f32[8,1024]{1,0:T(8,128)}) custom-call(bf16[8,128,2048]{2,1,0:T(8,128)(2,1)} %bitcast.67, bf16[8,128,2048]{2,1,0:T(8,128)(2,1)} %bitcast.66, f32[2048,1024]{1,0:T(8,128)} %get-tuple-element.51.slope_ref, ...), custom_call_target="tpu_custom_call" | custom-call | flops 17179869184 | bytes 41943040 | tf_op jit(solution)/shard_map/mlp_backward/pallas_call | solution.py:1236
  360.8 14.1 %convolution_convert_fusion = bf16[1024,2048]{1,0:T(8,128)(2,1)} fusion(bf16[2048,1024]{1,0:T(8,128)(2,1)} %get-tuple-element.53, bf16[2048,2048]{1,0:T(8,128)(2,1)} %get-tuple-element.54), kind=kOutput, calls=%fused_computation | convolution fusion | flops 8592031744 | bytes 16777216 | tf_op jit(solution)/shard_map/dot_general | solution.py:1324
  374.9 121.4 %shard_map.256 = (bf16[8,256,2048]{2,1,0:T(8,128)(2,1)}, bf16[2048,1024]{1,0:T(8,128)(2,1)}, f32[256,2048]{1,0:T(8,128)}, f32[4,8,2048]{2,1,0:T(8,128)}) custom-call(bf16[8,256,2048]{2,1,0:T(8,128)(2,1)} %bitcast.37, bf16[2048,2048]{1,0:T(8,128)(2,1)} %bitcast.36, f32[256,2048]{1,0:T(8,128)} %get-tuple-element.57.residual_ref, bf16[256,2048]{1,0:T(8,128)(2,1)} %grad_ref.1, ...), custom_call_target="tpu_custom_call" | custom-call | flops 419430400 | bytes 52428800 | tf_op jit(solution)/shard_map/pallas_call | solution.py:952
  496.2 8.9 %dense_backward.1 = (bf16[2048,256]{1,0:T(8,128)(2,1)}, bf16[256,2048]{1,0:T(8,128)(2,1)}) custom-call(bf16[2048,2048]{1,0:T(8,128)(2,1)} %bitcast.65, bf16[2048,256]{1,0:T(8,128)(2,1)} %get-tuple-element.49.attended_ref, bf16[4,256,512]{2,1,0:T(8,128)(2,1)} %bitcast.42), custom_call_target="tpu_custom_call" | custom-call | flops 4294967296 | bytes 8388608 | tf_op jit(solution)/shard_map/dense_backward/pallas_call | solution.py:1084
  505.2 0.0 reduce-scatter.8.cloned.1.call-update
  505.2 0.0 reduce-scatter.10.cloned.1.call-start
  505.2 29.4 %attention_backward.1.grad_ref.grad_cat_ref = bf16[2048,768]{1,0:T(8,128)(2,1)} custom-call(f32[4]{0:T(128)} %multiply_power_fusion.slope_ref, bf16[2048,768]{1,0:T(8,128)(2,1)} %project.1.proj_ref, bf16[2048,256]{1,0:T(8,128)(2,1)} %get-tuple-element.61.grad_ref, f32[4,2048]{1,0:T(4,128)} %get-tuple-element.62.lse_ref, s32[1,2048]{1,0:T(1,128)} %bitcast.51, ...), custom_call_target="tpu_custom_call" | custom-call | flops 4026531840 | bytes 7340032 | tf_op jit(solution)/shard_map/attention_backward/pallas_call | solution.py:183
  534.6 13.2 %qkv_weight_grad.1 = (bf16[3,2048,256]{2,1,0:T(8,128)(2,1)}, f32[3,8,256]{2,1,0:T(8,128)}) custom-call(bf16[2048,2048]{1,0:T(8,128)(2,1)} %bitcast.34, bf16[2048,768]{1,0:T(8,128)(2,1)} %attention_backward.1.grad_ref.grad_cat_ref), custom_call_target="tpu_custom_call" | custom-call | flops 6442450944 | bytes 16777216 | tf_op jit(solution)/shard_map/qkv_weight_grad/pallas_call | solution.py:989
  547.8 0.0 reduce-scatter.12.cloned.1.call-start
  547.9 0.7 reduce-scatter.12.cloned.1.call-update
  548.6 0.0 reduce-scatter.14.cloned.1.call-start
  548.6 0.5 reduce-scatter.14.cloned.1.call-update
  549.2 0.0 reduce-scatter.6.cloned.1.call-start
  549.2 0.7 reduce-scatter.6.cloned.1.call-update
  550.0 0.6 pad.4.own_ref
  550.6 132.2 %shard_map.257 = (bf16[4,512,1024]{2,1,0:T(8,128)(2,1)}, f32[256,2048]{1,0:T(8,128)}, f32[8,2048]{1,0:T(8,128)}, f32[8,256]{1,0:T(8,128)}, f32[2,2048]{1,0:T(2,128)}) custom-call(bf16[4,512,1024]{2,1,0:T(8,128)(2,1)} %bitcast.38, bf16[2048,768]{1,0:T(8,128)(2,1)} %attention_backward.1.grad_ref.grad_cat_ref, bf16[4,3,512,256]{3,2,1,0:T(8,128)(2,1)} %bitcast.40, ...), custom_call_target="tpu_custom_call" | custom-call | flops 419430400 | bytes 52428800 | tf_op jit(solution)/shard_map/pallas_call | solution.py:952
  682.8 1.3 slice.50
  684.1 0.7 slice_bitcast_fusion
  684.8 0.6 copy.33
  685.4 1.7 fusion.1
  687.0 0.0 reduce-scatter.10.cloned.1.call-done.qkv_ref
  687.1 7.8 reduce-scatter.12.cloned.1.call-done.one_ref
  694.9 49.6 %reduce-scatter.14.cloned.1.call-done.two_ref = bf16[128,2048]{1,0:T(8,128)(2,1)} async-done(((bf16[1024,2048]{1,0:T(8,128)(2,1)}), bf16[128,2048]{1,0:T(8,128)(2,1)}) %reduce-scatter.14.cloned.1.call-update) | async-done | bytes 524304 | tf_op jit(solution)/shard_map/reduce_scatter | solution.py:1330
  744.4 57.6 %reduce-scatter.6.cloned.1.call-done.down_ref = bf16[1024,512]{1,0:T(8,128)(2,1)} async-done(((bf16[1024,2048]{1,0:T(8,128)(2,1)}), bf16[1024,512]{1,0:T(8,128)(2,1)}) %reduce-scatter.6.cloned.1.call-update) | async-done | bytes 1048592 | tf_op jit(solution)/shard_map/reduce_scatter | solution.py:1267
  802.0 7.8 finish.1
  (23 shorter events, 0.1 us)
Async XLA Ops:
  7.2 5.8 copy-start.3
  7.2 6.4 copy-start.2
  7.2 80.0 %all-gather.19.cloned.1.call-start = ((), (), s32[]{:S(2)}) async-start(), calls=%async_computation.14 | async-start | bytes 3932160 | tf_op jit(solution)/shard_map/all_gather | solution.py:1292
  7.9 113.5 %all-gather.21.cloned.1.call-start = ((), (), s32[]{:S(2)}) async-start(), calls=%async_computation.15 | async-start | bytes 1310720 | tf_op jit(solution)/shard_map/all_gather | solution.py:1293
  8.7 299.9 %all-gather.11.cloned.1.call-start = ((), (), s32[]{:S(2)}) async-start(), calls=%async_computation.5 | async-start | bytes 5242880 | tf_op jit(solution)/shard_map/all_gather | solution.py:1294
  9.4 299.2 %all-gather.13.cloned.1.call-start = ((), (), s32[]{:S(2)}) async-start(), calls=%async_computation.6 | async-start | bytes 5242880 | tf_op jit(solution)/shard_map/all_gather | solution.py:1295
  10.0 325.5 %all-gather.17.cloned.1.call-start = ((), (), s32[]{:S(2)}) async-start(), calls=%async_computation.13 | async-start | bytes 4718592 | tf_op jit(solution)/shard_map/all_gather | solution.py:1298
  12.3 323.2 %all-gather.15.cloned.1.call-start = ((), (), s32[]{:S(2)}) async-start(), calls=%async_computation.12 | async-start | bytes 4718592 | tf_op jit(solution)/shard_map/all_gather | solution.py:1297
  12.9 674.1 %reduce-scatter.8.cloned.1.call-start = ((), (), s32[]{:S(2)}) async-start(), calls=%async_computation.8 | async-start | bytes 1310720 | tf_op jit(solution)/shard_map/reduce_scatter | solution.py:1267
  505.2 181.9 %reduce-scatter.10.cloned.1.call-start = ((), (), s32[]{:S(2)}) async-start(), calls=%async_computation.9 | async-start | bytes 3932160 | tf_op jit(solution)/shard_map/reduce_scatter | solution.py:1267
  547.8 147.0 %reduce-scatter.12.cloned.1.call-start = ((), (), s32[]{:S(2)}) async-start(), calls=%async_computation.10 | async-start | bytes 4718592 | tf_op jit(solution)/shard_map/reduce_scatter | solution.py:1329
  548.6 195.9 %reduce-scatter.14.cloned.1.call-start = ((), (), s32[]{:S(2)}) async-start(), calls=%async_computation.11 | async-start | bytes 4718592 | tf_op jit(solution)/shard_map/reduce_scatter | solution.py:1330
  548.6 1.3 copy-start.1
  548.6 1.3 copy-start
  549.2 252.9 %reduce-scatter.6.cloned.1.call-start = ((), (), s32[]{:S(2)}) async-start(), calls=%async_computation.7 | async-start | bytes 5242880 | tf_op jit(solution)/shard_map/reduce_scatter | solution.py:1267
Sparse Core Ops, SparseCore 0:
  9.8 44.9 all-gather.18
  56.7 26.4 all-gather.20
  85.1 52.5 all-gather.10
  139.4 52.3 all-gather.12
  193.9 60.6 all-gather.16
  256.6 52.6 all-gather.14
  505.3 31.1 reduce-scatter.7
  548.0 84.0 reduce-scatter.9
  634.3 60.5 reduce-scatter.11
  697.0 47.3 reduce-scatter.13
  747.4 54.5 reduce-scatter.5

commit v4 on v3

--- a/solution.py
+++ b/solution.py
@@ -240,8 +240,12 @@
     def tile(self, sub, tile):
         return pl.ds(pl.multiple_of(sub * self.sub_rows + tile * ROW_TILE, ROW_TILE), ROW_TILE)
 
-    def enter(self):
+    def enter(self, with_groups=False):
         barrier = pltpu.get_barrier_semaphore()
+        groups = lax.axis_size("dp") if with_groups else 1
+        for step in range(1, groups):
+            peer = lax.rem(lax.axis_index("dp") + step, groups)
+            pl.semaphore_signal(barrier, inc=1, device_id={"dp": peer}, device_id_type=MESH)
 
         def greet(peer):
             pl.semaphore_signal(barrier, inc=1, device_id={"tensor": peer}, device_id_type=MESH)
@@ -250,7 +254,7 @@
         pl.when(self.has_below)(lambda: greet(self.below))
         greet(self.partner)
         pl.semaphore_wait(
-            barrier, 1 + self.has_above.astype(jnp.int32) + self.has_below.astype(jnp.int32)
+            barrier, groups + self.has_above.astype(jnp.int32) + self.has_below.astype(jnp.int32)
         )
 
 
@@ -605,35 +609,57 @@
 
 
 class Beside:
-    def __init__(self, whole, pre, out, scratch):
-        self.whole, self.pre, self.out = whole, pre, out
-        self.loaded, self.stored, self.load_sem, self.store_sem = scratch
-        self.block = self.loaded.shape[2]
-        self.count = out.shape[0] // self.block
+    def __init__(self, whole, pre, parts, scratch):
+        self.whole, self.pre, self.parts = whole, pre, parts
+        self.loaded, self.stored, self.load_sem, self.send_sem, self.recv_sem = scratch
+        self.count, self.block = self.stored.shape[:2]
+        self.groups = parts.shape[0]
+        self.group = lax.axis_index("dp")
+        self.each = self.count // self.groups
 
     @staticmethod
-    def scratch(tokens, width, hidden):
-        block = min(256, width)
+    def scratch(tokens, width, hidden, groups):
+        block = min(256, width // groups)
+        count = width // block
         dma = pltpu.SemaphoreType.DMA
         return [
             pltpu.VMEM((2, tokens, block), jnp.bfloat16),
-            pltpu.VMEM((2, block, hidden), jnp.bfloat16),
+            pltpu.VMEM((count, block, hidden), jnp.bfloat16),
             dma((2,)),
-            dma((2,)),
+            dma((count,)),
+            dma((count,)),
         ]
 
-    def at(self, index):
-        return pl.ds(pl.multiple_of(index * self.block, self.block), self.block)
+    def place(self, index):
+        return lax.rem(index + self.group * self.each, self.count)
 
     def load(self, index):
+        columns = pl.ds(pl.multiple_of(self.place(index) * self.block, self.block), self.block)
         return pltpu.make_async_copy(
-            self.whole.at[:, self.at(index)], self.loaded.at[index % 2], self.load_sem.at[index % 2]
-        )
-
-    def store(self, index):
+            self.whole.at[:, columns], self.loaded.at[index % 2], self.load_sem.at[index % 2]
+        )
+
+    def target(self, source, within):
+        return self.parts.at[source, pl.ds(pl.multiple_of(within * self.block, self.block), self.block)]
+
+    def keep(self, index):
         return pltpu.make_async_copy(
-            self.stored.at[index % 2], self.out.at[self.at(index)], self.store_sem.at[index % 2]
-        )
+            self.stored.at[index], self.target(self.group, index), self.send_sem.at[index]
+        )
+
+    def send(self, index, source, peer):
+        within = index % self.each
+        return pltpu.make_async_remote_copy(
+            src_ref=self.stored.at[index],
+            dst_ref=self.target(source, within),
+            send_sem=self.send_sem.at[index],
+            recv_sem=self.recv_sem.at[source * self.each + within],
+            device_id={"dp": peer},
+            device_id_type=MESH,
+        )
+
+    def peer(self, index):
+        return lax.rem(index // self.each + self.group, self.groups)
 
     def start(self):
         self.load(0).start()
@@ -645,28 +671,35 @@
         def _():
             self.load(index).wait()
             pl.when(index + 1 < self.count)(lambda: self.load(index + 1).start())
-            pl.when(index >= 2)(lambda: self.store(index - 2).wait())
-            self.stored[index % 2] = lax.dot_general(
+            self.stored[index] = lax.dot_general(
                 self.loaded[index % 2],
                 self.pre[...],
                 (((0,), (0,)), ((), ())),
                 preferred_element_type=jnp.float32,
             ).astype(jnp.bfloat16)
-            self.store(index).start()
+
+            pl.when(index < self.each)(lambda: self.keep(index).start())
+            pl.when(index >= self.each)(
+                lambda: self.send(index, self.group, self.peer(index)).start()
+            )
 
     def finish(self):
-        for index in range(max(self.count - 2, 0), self.count):
-            self.store(index).wait()
+        for index in range(self.each):
+            self.keep(index).wait()
+        for index in range(self.each, self.count):
+            source = self.peer(index)
+            self.send(index, source, source).wait_recv()
+            self.send(index, self.group, source).wait_send()
 
 
 def grad_gather_kernel(
     chips, partial_ref, whole_in_ref, residual_ref, grad_ref, gain_ref, pre_ref,
-    whole_ref, up_ref, residual_grad_ref, sums_ref, branch_ref, *rest
+    whole_ref, up_parts_ref, residual_grad_ref, sums_ref, branch_ref, *rest
 ):
     line = Line(chips, grad_ref.shape[0])
     reduce = Reduce(line, partial_ref, rest[:4], rest[4:9])
     gather = Gather(line, branch_ref, whole_ref, rest[9:14])
-    beside = Beside(whole_in_ref, pre_ref, up_ref, rest[14:])
+    beside = Beside(whole_in_ref, pre_ref, up_parts_ref, rest[14:])
     sums_ref[...] = jnp.zeros_like(sums_ref)
 
     def rows_done(at):
@@ -683,62 +716,14 @@
         sums_ref[3] += fold(out_grad)
 
     beside.start()
-    run_line(line, reduce, gather, rows_done, beside.slot)
+    line.enter(True)
+    run_line(line, reduce, gather, rows_done, beside.slot, True)
     beside.finish()
 
 
-class Exchange:
-    def __init__(self, partial, parts, scratch):
-        self.partial, self.parts = partial, parts
-        self.stage, self.in_sem, self.out_sem, self.send_sem, self.recv_sem = scratch
-        self.groups = lax.axis_size("dp")
-        self.group = lax.axis_index("dp")
-
-    @staticmethod
-    def scratch(groups, block):
-        dma = pltpu.SemaphoreType.DMA
-        return [pltpu.VMEM(block, jnp.bfloat16), dma, dma, dma((groups,)), dma((groups,))]
-
-    def peer(self, step):
-        return lax.rem(self.group + step, self.groups)
-
-    def copy(self, peer, slot, step):
-        return pltpu.make_async_remote_copy(
-            src_ref=self.partial.at[peer],
-            dst_ref=self.parts.at[slot],
-            send_sem=self.send_sem.at[step],
-            recv_sem=self.recv_sem.at[slot],
-            device_id={"dp": peer},
-            device_id_type=MESH,
-        )
-
-    def own_in(self):
-        return pltpu.make_async_copy(self.partial.at[self.group], self.stage, self.in_sem)
-
-    def own_out(self):
-        return pltpu.make_async_copy(self.stage, self.parts.at[self.group], self.out_sem)
-
-    def start(self):
-        for step in range(1, self.groups):
-            self.copy(self.peer(step), self.group, step).start()
-        self.own_in().start()
-
-    def slot(self, slot):
-        @pl.when(slot == 2)
-        def _():
-            self.own_in().wait()
-            self.own_out().start()
-
-    def finish(self):
-        for step in range(1, self.groups):
-            self.copy(self.peer(step), self.peer(step), step).wait_recv()
-            self.copy(self.peer(step), self.group, step).wait_send()
-        self.own_out().wait()
-
-
 def grad_kernel(
-    chips, up_ref, grad_cat_ref, weight_ref, input_ref, residual_grad_ref, gain_ref, early_ref, own_ref,
-    up_parts_ref, out_ref, early_out_ref, own_out_ref, late_ref, mirror, *rest
+    chips, grad_cat_ref, weight_ref, input_ref, residual_grad_ref, gain_ref, first_ref, second_ref, own_ref,
+    out_ref, sums_ref, own_out_ref, mirror, *rest
 ):
     line = Line(chips, input_ref.shape[0])
     rows = input_ref.shape[0]
@@ -759,41 +744,28 @@
             target[slot, :, index * part : (index + 1) * part] = total.astype(jnp.bfloat16)
 
     reduce = Reduce(line, mirror, rest[:4], rest[4:9], product)
-    sums = Sums(2 * chips, early_ref, own_ref, early_out_ref, own_out_ref, late_ref, rest[9:28])
-    exchange = Exchange(up_ref, up_parts_ref, rest[28:])
-    sums.late_sum[...] = jnp.zeros_like(sums.late_sum)
+    sums = Sums(2 * chips, first_ref, second_ref, own_ref, sums_ref, own_out_ref, rest[9:])
 
     def rows_done(at):
         unit, inv_std = unit_of(input_ref[at, :].astype(jnp.float32))
         grad = reduce.total(at)
         out_ref[at, :] = residual_grad_ref[at, :] + norm_back(grad, unit, inv_std, gain_ref[...])
-        sums.late_sum[0] += fold(grad * unit)
-        sums.late_sum[1] += fold(grad)
-
-    def beside(slot):
-        sums.beside(slot)
-        exchange.slot(slot)
 
     sums.greet()
-    exchange.start()
-    run_line(line, reduce, None, rows_done, beside, True)
+    run_line(line, reduce, None, rows_done, sums.beside, True)
     sums.close()
-    exchange.finish()
 
 
 class Sums:
-    def __init__(self, ranks, early_ref, own_ref, early_out, own_out, late_out, scratch):
+    def __init__(self, ranks, first_ref, second_ref, own_ref, out_ref, own_out_ref, scratch):
         self.ranks = ranks
         self.groups = lax.axis_size("dp")
         self.me = lax.axis_index("tensor")
         self.group = lax.axis_index("dp")
-        self.early, self.own = early_ref, own_ref
-        self.early_out, self.own_out, self.late_out = early_out, own_out, late_out
-        (
-            self.late_sum, self.mine, self.first, self.stage, self.second,
-            self.late_mine, self.late_group, self.late_stage, self.late_all,
-        ) = scratch[:9]
-        self.sems = scratch[9:]
+        self.early, self.late, self.own = first_ref, second_ref, own_ref
+        self.early_out, self.own_out = out_ref, own_out_ref
+        self.mine, self.first, self.stage, self.second = scratch[:4]
+        self.sems = scratch[4:]
         self.part = self.mine.shape[1] // ranks
 
     @staticmethod
@@ -802,17 +774,11 @@
         f32 = jnp.float32
         dma = pltpu.SemaphoreType.DMA
         return [
-            pltpu.VMEM((2, 8, width), f32),
             pltpu.VMEM((8, width), f32),
             pltpu.VMEM((ranks, 8, part), f32),
             pltpu.VMEM((16, part), f32),
             pltpu.VMEM((groups, 16, part), f32),
-            pltpu.VMEM((2, width), f32),
-            pltpu.VMEM((groups, 2, width), f32),
-            pltpu.VMEM((2, width), f32),
-            pltpu.VMEM((ranks, 2, width), f32),
-        ] + [dma((ranks,)), dma((ranks,)), dma((groups,)), dma((groups,)), dma((ranks,)), dma((ranks,)),
-             dma((groups,)), dma((groups,)), dma((ranks,)), dma((ranks,))]
+        ] + [dma((ranks,)), dma((ranks,)), dma((groups,)), dma((groups,)), dma((ranks,)), dma((ranks,))]
 
     def rank(self, step):
         return lax.rem(self.me + step, self.ranks)
@@ -857,18 +823,12 @@
             sem, rank, "tensor", peer,
         )
 
-    def late_exchange(self, peer, slot, sem):
-        return self.copy(3, self.late_mine, self.late_group.at[slot], sem, slot, "dp", peer)
-
-    def late_spread(self, peer, slot, sem):
-        return self.copy(4, self.late_stage, self.late_all.at[slot], sem, slot, "tensor", peer)
-
     def beside(self, slot):
         @pl.when(slot == 1)
         def _():
-            self.mine[...] = jnp.zeros_like(self.mine)
-            for row in range(self.early.shape[0]):
-                self.mine[row : row + 1, :] = jnp.sum(self.early[row], axis=0, keepdims=True)
+            self.mine[...] = self.early[...]
+            for row in range(self.late.shape[0]):
+                self.mine[row + 2 : row + 3, :] = jnp.sum(self.late[row], axis=0, keepdims=True)
             for step in range(1, self.ranks):
                 self.scatter(self.rank(step), self.me, step).start()
             self.first[self.me] = self.mine[:, self.columns(self.me)]
@@ -899,35 +859,12 @@
                 self.spread(self.rank(step), self.me, step).start()
 
     def close(self):
-        for row in range(2):
-            self.late_mine[row : row + 1, :] = jnp.sum(self.late_sum[row], axis=0, keepdims=True)
-        for step in range(1, self.groups):
-            self.late_exchange(self.peer(step), self.group, step).start()
-        self.late_group[self.group] = self.late_mine[...]
-        for step in range(1, self.groups):
-            self.late_exchange(self.peer(step), self.peer(step), step).wait_recv()
-        total = self.late_group[0]
-        for index in range(1, self.groups):
-            total = total + self.late_group[index]
-        self.late_stage[...] = total
-        for step in range(1, self.ranks):
-            self.late_spread(self.rank(step), self.me, step).start()
-        self.late_all[self.me] = total
         for step in range(1, self.ranks):
             self.spread(self.rank(step), self.rank(step), step).wait_recv()
-        for step in range(1, self.ranks):
-            self.late_spread(self.rank(step), self.rank(step), step).wait_recv()
-        total = self.late_all[0]
-        for rank in range(1, self.ranks):
-            total = total + self.late_all[rank]
-        self.late_out[...] = total
-        for step in range(1, self.ranks):
             self.scatter(self.rank(step), self.me, step).wait_send()
             self.spread(self.rank(step), self.me, step).wait_send()
-            self.late_spread(self.rank(step), self.me, step).wait_send()
         for step in range(1, self.groups):
             self.exchange(self.peer(step), self.group, step).wait_send()
-            self.late_exchange(self.peer(step), self.group, step).wait_send()
 
 
 def line_call(kernel, collective_id, operands, outs, rows, width, gathers=True, reduces=True, product=False, sums=False, placed=(), more=()):
@@ -964,49 +901,75 @@
     )(*operands)
 
 
-def qkv_grad_kernel(rows_ref, grad_ref, out_ref, sums_ref):
+def columns_of(row, count):
+    return jnp.broadcast_to(row, (128, row.shape[1])).T[:, :count]
+
+
+def qkv_grad_kernel(rows_ref, grad_ref, weight_ref, norm_ref, out_ref, sums_ref, first_ref, total):
     head_width = out_ref.shape[2]
 
     @pl.when(pl.program_id(0) == 0)
     def _():
         for kind in range(3):
             cols = slice(kind * head_width, (kind + 1) * head_width)
-            sums_ref[kind] = jnp.sum(
+            parts = jnp.sum(
                 grad_ref[:, cols].astype(jnp.float32).reshape(-1, 8, head_width), axis=0
             )
+            sums_ref[kind] = parts
+            total[kind] = jnp.broadcast_to(jnp.sum(parts, axis=0, keepdims=True), parts.shape)
 
     product = lax.dot_general(
         rows_ref[...], grad_ref[...], (((0,), (0,)), ((), ())), preferred_element_type=jnp.float32
     )
+    gain = columns_of(norm_ref[0:1, :], 1)
+    shift = columns_of(norm_ref[1:2, :], 1)
+    gain_sum = shift_sum = None
     for kind in range(3):
-        out_ref[kind] = product[:, kind * head_width : (kind + 1) * head_width].astype(jnp.bfloat16)
-
-
-def qkv_weight_grad(whole, grad_cat):
+        part = product[:, kind * head_width : (kind + 1) * head_width]
+        out_ref[kind] = part.astype(jnp.bfloat16)
+        weight = weight_ref[0, kind].astype(jnp.float32)
+        sums = total[kind, 0:1, :]
+        shift_term = jnp.sum(weight * sums, axis=1, keepdims=True)
+        gain_term = jnp.sum(weight * (part - shift * sums), axis=1, keepdims=True)
+        gain_sum = gain_term if kind == 0 else gain_sum + gain_term
+        shift_sum = shift_term if kind == 0 else shift_sum + shift_term
+    lane = lax.broadcasted_iota(jnp.int32, (product.shape[0], 128), 1)
+    both = jnp.where(lane == 0, gain_sum / gain, jnp.where(lane == 1, shift_sum, 0.0))
+    first_ref[...] = both.T[:8]
+
+
+def qkv_weight_grad(whole, grad_cat, qkv_all, gain, shift):
     tokens, width = whole.shape
-    head_width = grad_cat.shape[1] // 3
-    block = 256
+    part, head_width = qkv_all.shape[2:]
+    block = min(256, part)
+    each = part // block
+    norm = jnp.stack([gain, shift])
     return pl.pallas_call(
         qkv_grad_kernel,
         grid=(width // block,),
         in_specs=[
             pl.BlockSpec((tokens, block), lambda i: (0, i)),
             pl.BlockSpec(grad_cat.shape, lambda i: (0, 0)),
+            pl.BlockSpec((1, 3, block, head_width), lambda i: (i // each, 0, i % each, 0)),
+            pl.BlockSpec((2, block), lambda i: (0, i)),
         ],
         out_specs=[
             pl.BlockSpec((3, block, head_width), lambda i: (0, i, 0)),
             pl.BlockSpec((3, 8, head_width), lambda i: (0, 0, 0)),
+            pl.BlockSpec((8, block), lambda i: (0, i)),
         ],
         out_shape=[
             jax.ShapeDtypeStruct((3, width, head_width), jnp.bfloat16),
             jax.ShapeDtypeStruct((3, 8, head_width), jnp.float32),
-        ],
+            jax.ShapeDtypeStruct((8, width), jnp.float32),
+        ],
+        scratch_shapes=[pltpu.VMEM((3, 8, head_width), jnp.float32)],
         compiler_params=pltpu.CompilerParams(vmem_limit_bytes=VMEM_BYTES),
         cost_estimate=pl.CostEstimate(
             flops=6 * tokens * width * head_width, bytes_accessed=4 * tokens * width, transcendentals=0
         ),
         name="qkv_weight_grad",
-    )(whole, grad_cat)
+    )(whole, grad_cat, qkv_all, norm)
 
 
 def finish_kernel(down_ref, up_ref, dense_ref, qkv_ref, one_ref, two_ref, residual_ref, bias_ref, grad_ref,
@@ -1286,6 +1249,7 @@
 ):
     rows, width = layer_input.shape
     ranks = lax.axis_size("tensor")
+    groups = lax.axis_size("dp")
     tokens = ranks * rows
     f32_rows = jax.ShapeDtypeStruct((rows, width), jnp.float32)
 
@@ -1329,21 +1293,23 @@
     mlp_rows_one = lax.psum_scatter(mlp_one, "tensor", scatter_dimension=0, tiled=True)
     mlp_rows_two = lax.psum_scatter(mlp_two, "tensor", scatter_dimension=0, tiled=True)
 
-    branch_whole, up_grad, residual_grad, second_sums = line_call(
+    branch_whole, up_parts, residual_grad, second_sums = line_call(
         grad_gather_kernel, 3,
         (normed2_part.reshape(ranks, rows, width), whole2, residual, out_grad, second_gain[None], pre_grad),
         (
-            jax.ShapeDtypeStruct((width, up_width), jnp.bfloat16),
+            jax.ShapeDtypeStruct((groups, width // groups, up_width), jnp.bfloat16),
             f32_rows,
             jax.ShapeDtypeStruct((4, 8, width), jnp.float32),
         ),
-        rows, width, placed=(2, 1), more=Beside.scratch(tokens, width, up_width),
+        rows, width, placed=(2, 1), more=Beside.scratch(tokens, width, up_width, groups),
     )
     branch_whole = branch_whole.reshape(tokens, width)
     attended_grad, dense_grad = dense_backward(branch_whole, attended, dense_all)
     qkv_grad_cat = attention_backward(projected, attended_grad, segment_ids, slopes, log_sums)
     dense_wgrad = over_dp(dense_grad, 1)
-    qkv_grad, qkv_sums = qkv_weight_grad(whole1, qkv_grad_cat)
+    qkv_grad, qkv_sums, first_sums = qkv_weight_grad(
+        whole1, qkv_grad_cat, qkv_all, first_gain, first_shift
+    )
     qkv_grad, qkv_grad_cat = lax.optimization_barrier((qkv_grad, qkv_grad_cat))
     qkv_wgrad = over_dp(qkv_grad, 1)
     qkv_sums = jnp.sum(qkv_sums, axis=1)
@@ -1353,20 +1319,11 @@
     own = jnp.concatenate([qkv_sums[0], qkv_sums[2], up_bias_part]).reshape(-1, part)
     own = jnp.pad(own, ((0, 8 - own.shape[0]), (0, 0)))
     f32_sums = jax.ShapeDtypeStruct((8, width), jnp.float32)
-    groups = lax.axis_size("dp")
-    up_block = (width // groups, up_width)
-    up_parts, input_grad, early, own, late = line_call(
+    input_grad, sums, own = line_call(
         grad_kernel, 4,
-        (up_grad.reshape((groups,) + up_block), qkv_grad_cat, qkv_all, layer_input, residual_grad, first_gain[None], second_sums, own),
-        (
-            jax.ShapeDtypeStruct((groups,) + up_block, jnp.bfloat16),
-            f32_rows,
-            f32_sums,
-            jax.ShapeDtypeStruct((8, part), jnp.float32),
-            jax.ShapeDtypeStruct((2, width), jnp.float32),
-        ),
-        rows, width, gathers=False, product=True, sums=True, placed=(1, 1),
-        more=Exchange.scratch(groups, up_block),
+        (qkv_grad_cat, qkv_all, layer_input, residual_grad, first_gain[None], first_sums, second_sums, own),
+        (f32_rows, f32_sums, jax.ShapeDtypeStruct((8, part), jnp.float32)),
+        rows, width, gathers=False, product=True, sums=True,
     )
     down_wgrad, up_wgrad, dense_wgrad, qkv_wgrad, layer_out, input_grad = finish(
         down_wgrad, up_parts, dense_wgrad, qkv_wgrad,
@@ -1375,18 +1332,18 @@
     return (
         layer_out,
         input_grad,
-        late[0],
-        late[1],
+        sums[0],
+        sums[1],
         qkv_wgrad,
         own[:bias_rows].reshape(2, head_width),
         dense_wgrad,
-        early[2],
-        early[0],
-        early[1],
+        sums[4],
+        sums[2],
+        sums[3],
         up_wgrad,
         own[bias_rows : bias_rows + up_rows].reshape(up_width),
         down_wgrad,
-        early[3],
+        sums[5],
     )
 
 

time: 819 us -> 804 us (0.982)
  waiting for transfers between devices: 120 us -> 110 us
  transfers between devices with their start and end apart: 11 -> 11, of which waited for: 3 -> 2; matrix products, arithmetic and copies ran while one was open for 1% -> 1% of each run, Pallas kernels for 61% -> 60%
where the time goes in v4:
time: 804 us; the launch traced here: 802 us
  Pallas kernels  652 us (81%)
  waiting for transfers between devices  110 us (14%)
  matrix products  14.1 us (2%)
  between operations  14.1 us (2%)
  local copies, waits for them, and re-layouts  9.15 us (1%)
    pallas_call x4, Pallas kernels, line_call(): pl.pallas_call(functools.partial(kernel, chips), in_specs=[in_place] * in...  505 us
    reduce_scatter x3, waiting for transfers between devices, over_dp(): return lax.psum_scatter(grad, 'dp', scatter_dimension=dimension, tiled=True)  57.6 us
    reduce_scatter x1, waiting for transfers between devices, layer(): lax.psum_scatter(mlp_two, 'tensor', scatter_dimension=0, tiled=True)  47.6 us
    pallas_call x1, Pallas kernels, attention_backward(): pl.pallas_call(backward_kernel, grid=(seq_len // Q_BLOCK,), in_specs=[pl....  29.3 us
    pallas_call x1, Pallas kernels, mlp_forward(): pl.pallas_call(mlp_forward_kernel, grid=(tokens // block,), in_specs=[pl....  26.9 us
    pallas_call x1, Pallas kernels, mlp_backward(): pl.pallas_call(mlp_backward_kernel, grid=(ranks,), in_specs=[pl.BlockSpec...  25.2 us
    pallas_call x1, Pallas kernels, attention_forward(): pl.pallas_call(forward_kernel, grid=(seq_len // Q_BLOCK,), in_specs=[pl.B...  23.3 us
  transfers between devices with their start and end apart: 11, of which 2 were waited for; matrix products, arithmetic and copies ran while one was open for 1% of the time, Pallas kernels for 60%

profile of v4, /device:TPU:8, one launch (start us, length us, event | category | flops | bytes accessed | tf_op | source)
XLA Modules:
  0.0 801.6 jit_solution(14189413797898096168)
XLA Ops:
  7.2 0.0 all-gather.19.cloned.1.call-start
  7.2 0.7 all-gather.19.cloned.1.call-update
  7.9 0.0 all-gather.21.cloned.1.call-start
  8.0 0.7 all-gather.21.cloned.1.call-update
  8.7 0.0 all-gather.11.cloned.1.call-start
  8.7 0.7 all-gather.11.cloned.1.call-update
  9.4 0.0 all-gather.13.cloned.1.call-start
  9.5 0.5 all-gather.13.cloned.1.call-update
  10.0 0.0 all-gather.15.cloned.1.call-start
  10.0 2.3 fusion
  12.3 0.0 all-gather.17.cloned.1.call-start
  12.4 0.5 all-gather.17.cloned.1.call-update
  12.9 0.0 reduce-scatter.8.cloned.1.call-start
  13.0 0.6 broadcast_in_dim.40.bias_ref
  13.6 1.3 copy.31.seg_col_ref
  15.0 71.7 %shard_map.254 = bf16[8,256,2048]{2,1,0:T(8,128)(2,1)} custom-call(bf16[256,2048]{1,0:T(8,128)(2,1)} %input_ref.5, f32[1,2048]{1,0:T(1,128)} %bitcast.42, f32[1,2048]{1,0:T(1,128)} %bitcast.47), custom_call_target="tpu_custom_call" | custom-call | flops 419430400 | bytes 52428800 | tf_op jit(solution)/shard_map/pallas_call | solution.py:889
  86.6 0.5 multiply_power_fusion.slope_ref
  87.2 11.0 %project.1.proj_ref = bf16[2048,768]{1,0:T(8,128)(2,1)} custom-call(bf16[2048,2048]{1,0:T(8,128)(2,1)} %bitcast.32, bf16[4,3,512,256]{3,2,1,0:T(8,128)(2,1)} %bitcast.37, f32[1,768]{1,0:T(1,128)} %broadcast_in_dim.40.bias_ref), custom_call_target="tpu_custom_call" | custom-call | flops 6442450944 | bytes 8388608 | tf_op jit(solution)/shard_map/project/pallas_call | solution.py:1094
  98.1 23.3 %attention_forward.1 = (bf16[2048,256]{1,0:T(8,128)(2,1)}, f32[4,2048]{1,0:T(4,128)}) custom-call(f32[4]{0:T(128)} %multiply_power_fusion.slope_ref, bf16[2048,768]{1,0:T(8,128)(2,1)} %project.1.proj_ref, s32[1,2048]{1,0:T(1,128)} %bitcast.51, s32[2048,1]{1,0:T(8,128)} %copy.31.seg_col_ref), custom_call_target="tpu_custom_call" | custom-call | flops 1610612736 | bytes 3145728 | tf_op jit(solution)/shard_map/attention_forward/pallas_call | solution.py:91
  121.4 186.1 %shard_map.255 = (bf16[8,256,2048]{2,1,0:T(8,128)(2,1)}, f32[256,2048]{1,0:T(8,128)}) custom-call(bf16[2048,256]{1,0:T(8,128)(2,1)} %get-tuple-element.48.attended_ref, bf16[4,256,512]{2,1,0:T(8,128)(2,1)} %bitcast.40, bf16[256,2048]{1,0:T(8,128)(2,1)} %input_ref.5, f32[1,2048]{1,0:T(1,128)} %bitcast.49, f32[1,2048]{1,0:T(1,128)} %bitcast.45, f32[1,2048]{1,0:T(1,128)} %bitcast.50), custom_call_target="tpu_custom_call" | custom-call | flops 419430400 | bytes 52428800 | tf_op jit(solution)/shard_map/pallas_call | solution.py:889
  307.5 0.0 all-gather.11.cloned.1.call-done.up_ref
  307.6 0.0 all-gather.13.cloned.1.call-done.down_ref
  307.6 26.9 %mlp_forward.1 = (bf16[2048,1024]{1,0:T(8,128)(2,1)}, f32[2048,1024]{1,0:T(8,128)}, bf16[1024,2048]{1,0:T(8,128)(2,1)}, bf16[1024,2048]{1,0:T(8,128)(2,1)}) custom-call(bf16[2048,2048]{1,0:T(8,128)(2,1)} %bitcast.34, bf16[2048,1024]{1,0:T(8,128)(2,1)} %all-gather.11.cloned.1.call-done.up_ref, f32[1,1024]{1,0:T(1,128)} %bitcast.69, ...), custom_call_target="tpu_custom_call" | custom-call | flops 17179869184 | bytes 33554432 | tf_op jit(solution)/shard_map/mlp_forward/pallas_call | solution.py:1140
  334.5 25.2 %mlp_backward.1 = (bf16[2048,2048]{1,0:T(8,128)(2,1)}, bf16[2048,1024]{1,0:T(8,128)(2,1)}, bf16[2048,2048]{1,0:T(8,128)(2,1)}, f32[8,1024]{1,0:T(8,128)}) custom-call(bf16[8,128,2048]{2,1,0:T(8,128)(2,1)} %bitcast.67, bf16[8,128,2048]{2,1,0:T(8,128)(2,1)} %bitcast.68, f32[2048,1024]{1,0:T(8,128)} %get-tuple-element.50.slope_ref, ...), custom_call_target="tpu_custom_call" | custom-call | flops 17179869184 | bytes 41943040 | tf_op jit(solution)/shard_map/mlp_backward/pallas_call | solution.py:1199
  359.8 14.1 %convolution_convert_fusion = bf16[1024,2048]{1,0:T(8,128)(2,1)} fusion(bf16[2048,1024]{1,0:T(8,128)(2,1)} %get-tuple-element.52, bf16[2048,2048]{1,0:T(8,128)(2,1)} %get-tuple-element.53), kind=kOutput, calls=%fused_computation | convolution fusion | flops 8592031744 | bytes 16777216 | tf_op jit(solution)/shard_map/dot_general | solution.py:1288
  373.8 125.8 %shard_map.256 = (bf16[8,256,2048]{2,1,0:T(8,128)(2,1)}, bf16[4,512,1024]{2,1,0:T(8,128)(2,1)}, f32[256,2048]{1,0:T(8,128)}, f32[4,8,2048]{2,1,0:T(8,128)}) custom-call(bf16[8,256,2048]{2,1,0:T(8,128)(2,1)} %bitcast.36, bf16[2048,2048]{1,0:T(8,128)(2,1)} %bitcast.35, f32[256,2048]{1,0:T(8,128)} %get-tuple-element.56.residual_ref, ...), custom_call_target="tpu_custom_call" | custom-call | flops 419430400 | bytes 52428800 | tf_op jit(solution)/shard_map/pallas_call | solution.py:889
  499.7 8.9 %dense_backward.1 = (bf16[2048,256]{1,0:T(8,128)(2,1)}, bf16[256,2048]{1,0:T(8,128)(2,1)}) custom-call(bf16[2048,2048]{1,0:T(8,128)(2,1)} %bitcast.66, bf16[2048,256]{1,0:T(8,128)(2,1)} %get-tuple-element.48.attended_ref, bf16[4,256,512]{2,1,0:T(8,128)(2,1)} %bitcast.41), custom_call_target="tpu_custom_call" | custom-call | flops 4294967296 | bytes 8388608 | tf_op jit(solution)/shard_map/dense_backward/pallas_call | solution.py:1047
  508.7 0.0 reduce-scatter.10.cloned.1.call-start
  508.7 1.3 pad_maximum_fusion.norm_ref
  510.0 29.3 %attention_backward.1.grad_ref.grad_cat_ref = bf16[2048,768]{1,0:T(8,128)(2,1)} custom-call(f32[4]{0:T(128)} %multiply_power_fusion.slope_ref, bf16[2048,768]{1,0:T(8,128)(2,1)} %project.1.proj_ref, bf16[2048,256]{1,0:T(8,128)(2,1)} %get-tuple-element.61.grad_ref, f32[4,2048]{1,0:T(4,128)} %get-tuple-element.62.lse_ref, s32[1,2048]{1,0:T(1,128)} %bitcast.52, ...), custom_call_target="tpu_custom_call" | custom-call | flops 4026531840 | bytes 7340032 | tf_op jit(solution)/shard_map/attention_backward/pallas_call | solution.py:183
  539.4 14.6 %qkv_weight_grad.1 = (bf16[3,2048,256]{2,1,0:T(8,128)(2,1)}, f32[3,8,256]{2,1,0:T(8,128)}, f32[8,2048]{1,0:T(8,128)}) custom-call(bf16[2048,2048]{1,0:T(8,128)(2,1)} %bitcast.33, bf16[2048,768]{1,0:T(8,128)(2,1)} %attention_backward.1.grad_ref.grad_cat_ref, bf16[4,3,512,256]{3,2,1,0:T(8,128)(2,1)} %bitcast.38, f32[2,2048]{1,0:T(2,128)} %pad_maximum_fusion.norm_ref), custom_call_target="tpu_custom_call" | custom-call | flops 6442450944 | bytes 16777216 | tf_op jit(solution)/shard_map/qkv_weight_grad/pallas_call | solution.py:947
  554.0 0.0 reduce-scatter.12.cloned.1.call-start
  554.1 0.7 reduce-scatter.12.cloned.1.call-update
  554.8 0.0 reduce-scatter.14.cloned.1.call-start
  554.8 0.5 reduce-scatter.14.cloned.1.call-update
  555.4 0.0 reduce-scatter.6.cloned.1.call-start
  555.4 0.7 reduce-scatter.6.cloned.1.call-update
  556.2 0.6 pad.4.own_ref
  556.8 120.9 %shard_map.257 = (f32[256,2048]{1,0:T(8,128)}, f32[8,2048]{1,0:T(8,128)}, f32[8,256]{1,0:T(8,128)}) custom-call(bf16[2048,768]{1,0:T(8,128)(2,1)} %attention_backward.1.grad_ref.grad_cat_ref, bf16[4,3,512,256]{3,2,1,0:T(8,128)(2,1)} %bitcast.39, bf16[256,2048]{1,0:T(8,128)(2,1)} %input_ref.5, f32[256,2048]{1,0:T(8,128)} %get-tuple-element.68.residual_grad_ref, ...), custom_call_target="tpu_custom_call" | custom-call | flops 419430400 | bytes 52428800 | tf_op jit(solution)/shard_map/pallas_call | solution.py:889
  677.7 1.3 slice.50
  679.0 0.7 slice_bitcast_fusion
  679.7 0.6 copy.33
  680.3 1.7 fusion.1
  682.0 0.0 reduce-scatter.10.cloned.1.call-done.qkv_ref
  682.0 0.0 reduce-scatter.12.cloned.1.call-done.one_ref
  682.1 47.6 %reduce-scatter.14.cloned.1.call-done.two_ref = bf16[128,2048]{1,0:T(8,128)(2,1)} async-done(((bf16[1024,2048]{1,0:T(8,128)(2,1)}), bf16[128,2048]{1,0:T(8,128)(2,1)}) %reduce-scatter.14.cloned.1.call-update) | async-done | bytes 524304 | tf_op jit(solution)/shard_map/reduce_scatter | solution.py:1294
  729.7 57.6 %reduce-scatter.6.cloned.1.call-done.down_ref = bf16[1024,512]{1,0:T(8,128)(2,1)} async-done(((bf16[1024,2048]{1,0:T(8,128)(2,1)}), bf16[1024,512]{1,0:T(8,128)(2,1)}) %reduce-scatter.6.cloned.1.call-update) | async-done | bytes 1048592 | tf_op jit(solution)/shard_map/reduce_scatter | solution.py:1230
  787.3 7.8 finish.1
  (24 shorter events, 0.2 us)
Async XLA Ops:
  7.2 5.8 copy-start.3
  7.2 6.4 copy-start.2
  7.2 80.0 %all-gather.19.cloned.1.call-start = ((), (), s32[]{:S(2)}) async-start(), calls=%async_computation.14 | async-start | bytes 3932160 | tf_op jit(solution)/shard_map/all_gather | solution.py:1256
  7.9 113.5 %all-gather.21.cloned.1.call-start = ((), (), s32[]{:S(2)}) async-start(), calls=%async_computation.15 | async-start | bytes 1310720 | tf_op jit(solution)/shard_map/all_gather | solution.py:1257
  8.7 298.9 %all-gather.11.cloned.1.call-start = ((), (), s32[]{:S(2)}) async-start(), calls=%async_computation.5 | async-start | bytes 5242880 | tf_op jit(solution)/shard_map/all_gather | solution.py:1258
  9.4 298.2 %all-gather.13.cloned.1.call-start = ((), (), s32[]{:S(2)}) async-start(), calls=%async_computation.6 | async-start | bytes 5242880 | tf_op jit(solution)/shard_map/all_gather | solution.py:1259
  10.0 324.5 %all-gather.15.cloned.1.call-start = ((), (), s32[]{:S(2)}) async-start(), calls=%async_computation.12 | async-start | bytes 4718592 | tf_op jit(solution)/shard_map/all_gather | solution.py:1261
  12.3 322.2 %all-gather.17.cloned.1.call-start = ((), (), s32[]{:S(2)}) async-start(), calls=%async_computation.13 | async-start | bytes 4718592 | tf_op jit(solution)/shard_map/all_gather | solution.py:1262
  12.9 669.1 %reduce-scatter.8.cloned.1.call-start = ((), (), s32[]{:S(2)}) async-start(), calls=%async_computation.8 | async-start | bytes 1310720 | tf_op jit(solution)/shard_map/reduce_scatter | solution.py:1230
  508.7 173.4 %reduce-scatter.10.cloned.1.call-start = ((), (), s32[]{:S(2)}) async-start(), calls=%async_computation.9 | async-start | bytes 3932160 | tf_op jit(solution)/shard_map/reduce_scatter | solution.py:1230
  554.0 128.0 %reduce-scatter.12.cloned.1.call-start = ((), (), s32[]{:S(2)}) async-start(), calls=%async_computation.10 | async-start | bytes 4718592 | tf_op jit(solution)/shard_map/reduce_scatter | solution.py:1293
  554.8 174.9 %reduce-scatter.14.cloned.1.call-start = ((), (), s32[]{:S(2)}) async-start(), calls=%async_computation.11 | async-start | bytes 4718592 | tf_op jit(solution)/shard_map/reduce_scatter | solution.py:1294
  554.8 1.3 copy-start.1
  554.8 1.3 copy-start
  555.4 232.0 %reduce-scatter.6.cloned.1.call-start = ((), (), s32[]{:S(2)}) async-start(), calls=%async_computation.7 | async-start | bytes 5242880 | tf_op jit(solution)/shard_map/reduce_scatter | solution.py:1230
Sparse Core Ops, SparseCore 0:
  9.8 44.9 all-gather.18
  56.7 26.4 all-gather.20
  85.1 52.5 all-gather.10
  139.4 52.3 all-gather.12
  193.9 60.6 all-gather.14
  256.6 52.5 all-gather.16
  508.8 28.0 reduce-scatter.7
  554.2 44.7 reduce-scatter.9
  601.2 79.5 reduce-scatter.11
  683.0 46.6 reduce-scatter.13
  732.7 54.6 reduce-scatter.5
